TPU v7x, 32 devices: a whole 2x2x4 slice. The times are simulated.
32 devices in a mesh: path: 8 (over y, x, core), tm: 4 (over z).
Axes of the slice: x: 2, y: 2, z: 4, core: 2. Of those that a mesh axis runs over, the one named last changes fastest.
Arguments:
- increments: bfloat16 [8192, 32, 1000], P(('path', 'tm')), may hold values from -6 to 6
- level_table: int32 [4096], replicated, may hold values from 0 to 4, as said below
- time_table: int32 [4096], replicated, may hold values from 0 to 31, as said below
Outputs:
- value_est: float32 [32], P('tm')
- grad_est: float32 [32, 1000], P('tm')
Inputs may be any that keep to these rules, and one draw needn't show every extreme that they name: `level_table`: never falls from one block to the next. `time_table`: split the 32 time points into as many runs of consecutive points as the tm axis has devices; the 128 consecutive entries of each device fall equally into every run.
All inputs are finite; a program needn't handle non-finite values.
Results may differ from a plain program's by a relative error of at most 0.0003.
The roundings to bfloat16 on the way count: a program that leaves them out, or rounds other values in their place, can miss the bound.
Values may be sent and summed in bfloat16 or wider, within the bound.
No kernel may reach another device: no remote copies, remote signals or barrier semaphores. Data moves between devices by JAX's collectives and lax.ppermute only.
A program may use at most 128 MiB of HBM per device.

v0:
```python
import jax
import jax.numpy as jnp
from jax import lax
from jax.sharding import PartitionSpec as P

LEVELS = 5
BLOCK = 2


horizon = 0.3


def stride_weights(levels, starts, steps_k, step_len):
    steps = jnp.arange(steps_k)
    fine_stride = jnp.power(2, LEVELS - 1 - levels).astype(jnp.int32)
    coarse = fine_stride * 2
    live_steps = steps[None, :] >= starts[:, None]
    on_fine = steps[None, :] % fine_stride[:, None] == 0
    on_coarse = (steps[None, :] % coarse[:, None] == 0) & (levels[:, None] > 0)
    term = fine_stride[:, None] * on_fine.astype(jnp.int32) - coarse[:, None] * on_coarse.astype(
        jnp.int32
    )
    return step_len * (live_steps.astype(jnp.float32) * term.astype(jnp.float32))


def terminal(incr, starts):
    steps_k = incr.shape[1]
    width = incr.shape[2]
    step_len = horizon / steps_k
    steps = jnp.arange(steps_k)
    live_steps = (steps[None, :] >= starts[:, None]).astype(jnp.bfloat16)
    end_point = jnp.sqrt(step_len) * jnp.einsum(
        "pi,pid->pd", live_steps, incr, preferred_element_type=jnp.float32
    )
    remaining = horizon - starts.astype(jnp.float32) * step_len
    scaled = end_point / remaining[:, None]
    end_value = 1.0 / (2.0 + 0.4 * jnp.sum(end_point * end_point, axis=1) / width)
    return (scaled, end_value)


def partial_sums(path_total, scaled, row_index, path_share, row_count):
    select = (row_index[:, None] == jnp.arange(row_count)[None, :]).astype(jnp.float32)
    select = select * (path_share * path_total)[:, None]
    return (jnp.sum(select, axis=0), jnp.dot(select.T, scaled, precision=lax.Precision.HIGHEST))


def first_terms(incr, levels, starts, path_share, row_count, offset):
    scaled, end_value = terminal(incr, starts)
    path_total = end_value * (levels == 0).astype(jnp.float32)
    return partial_sums(path_total, scaled, starts - offset, path_share, row_count)


def second_terms(incr, levels, starts, path_share, value_one, grad_low, row_count, offset):
    paths, steps_k, width = incr.shape
    step_len = horizon / steps_k
    scaled, end_value = terminal(incr, starts)
    inner_dots = jnp.dot(
        incr.reshape(paths * steps_k, width), grad_low.T, preferred_element_type=jnp.float32
    ).reshape(paths, steps_k, steps_k)
    steps = jnp.arange(steps_k)
    window = (steps[None, :, None] >= starts[:, None, None]) & (
        steps[None, :, None] < steps[None, None, :]
    )
    estimate = value_one[None, :] + jnp.sqrt(step_len) * jnp.sum(
        inner_dots * window.astype(jnp.float32), axis=1
    )
    drift_term = estimate - estimate * estimate * estimate
    weights = stride_weights(levels, starts, steps_k, step_len)
    path_total = end_value * (levels == 0).astype(jnp.float32) + jnp.sum(
        weights * drift_term, axis=1
    )
    return partial_sums(path_total, scaled, starts - offset, path_share, row_count)


def shards(increments, level_table, time_table):
    groups = lax.axis_size("tm")
    devices = lax.axis_size("path") * groups
    my_index = lax.axis_index("path") * groups + lax.axis_index("tm")
    blk_dev = level_table.shape[0] // devices
    steps_k = increments.shape[1]
    lvl_hot = (level_table[:, None] == jnp.arange(LEVELS)[None, :]).astype(jnp.float32)
    time_hot = (time_table[:, None] == jnp.arange(steps_k)[None, :]).astype(jnp.float32)
    counts = jnp.dot(lvl_hot.T, time_hot, precision=lax.Precision.HIGHEST)
    own_levels = lax.dynamic_slice_in_dim(level_table, my_index * blk_dev, blk_dev)
    own_times = lax.dynamic_slice_in_dim(time_table, my_index * blk_dev, blk_dev)
    lvl_path = jnp.repeat(own_levels, BLOCK)
    time_path = jnp.repeat(own_times, BLOCK)
    path_share = 1.0 / (BLOCK * counts[lvl_path, time_path])
    value_one, grad_one = lax.psum(
        first_terms(increments, lvl_path, time_path, path_share, steps_k, 0), ("path", "tm")
    )
    grad_low = grad_one.astype(jnp.bfloat16)
    value_part, grad_part = lax.psum_scatter(
        second_terms(increments, lvl_path, time_path, path_share, value_one, grad_low, steps_k, 0),
        "tm",
        scatter_dimension=0,
        tiled=True,
    )
    value_est, grad_est = lax.psum((value_part, grad_part), "path")
    return (value_est, grad_est)


def solution(mesh):
    placed = (P(("path", "tm"), None, None), P(), P())
    return jax.shard_map(
        shards, mesh=mesh, in_specs=placed, out_specs=(P("tm"), P("tm", None)), check_vma=False
    )
```

profile of v0, /device:TPU:0, one launch (start us, length us, event | category | flops | bytes accessed | tf_op | source)
XLA Modules:
  0.0 158.6 jit_solution(13497619476478879534)
XLA Ops:
  7.2 0.0 reduce-scatter.2.cloned.1.call-start
  7.2 0.8 broadcast_compare_fusion
  8.0 0.8 dynamic_slice.6
  8.7 0.9 fusion
  9.7 0.1 broadcast_in_dim.22
  9.8 0.2 reshape.283
  9.9 0.1 eq.74
  10.1 0.1 broadcast_in_dim.23
  10.2 0.1 reshape.282
  10.4 23.5 %copy.11 = bf16[256,32,1000]{2,1,0:T(8,128)(2,1)} copy(bf16[256,32,1000]{0,2,1:T(8,128)(2,1)} %param.5) | data formatting | bytes 32768000 | tf_op args[0]
  33.9 7.1 %multiply_reduce_fusion = f32[256,1000]{0,1:T(8,128)S(1)} fusion(bf16[256,32,1000]{0,2,1:T(8,128)(2,1)} %param.5, f32[256,32]{0,1:T(8,128)S(1)} %get-tuple-element.18), kind=kLoop, calls=%fused_computation.1 | loop fusion | flops 24320000 | bytes 17440768 | tf_op jit(solution)/shard_map/pi,pid->pd/dot_general | solution.py:32
  41.0 0.2 multiply_reduce_fusion.1
  41.1 0.1 broadcast_in_dim.24
  41.2 0.1 eq.85
  41.4 1.4 gather_fusion
  42.8 0.1 select_reduce_fusion.2
  42.9 1.0 fusion.2
  43.9 0.0 copy-start
  43.9 44.4 %all-reduce.1 = (bf16[32,1000]{1,0:T(8,128)(2,1)S(1)}, f32[32]{0:T(128)S(1)}) all-reduce(f32[32,1000]{1,0:T(8,128)S(1)} %fusion.2, f32[32]{0:T(128)S(1)} %select_reduce_fusion.2), channel_id=1, replica_groups=mesh['path'=8,'tm'=4] {'path','tm'}, use_global_device_ids=true, to_apply=%region_3.5 | all-reduce | flops 32032 | bytes 192256 | tf_op jit(solution)/shard_map/psum | solution.py:89
  88.3 10.7 %convolution_bitcast_fusion = f32[8192,32]{0,1:T(8,128)S(1)} fusion(bf16[8192,1000]{1,0:T(8,128)(2,1)} %bitcast.11, bf16[32,1000]{1,0:T(8,128)(2,1)S(1)} %get-tuple-element.3), kind=kOutput, calls=%fused_computation.2 | convolution fusion | flops 524288000 | bytes 17496576 | tf_op jit(solution)/shard_map/dot_general | solution.py:57
  99.0 2.7 %reshape.285 = f32[256,32,32]{1,0,2:T(8,128)} reshape(f32[8192,32]{0,1:T(8,128)S(1)} %convolution_bitcast_fusion) | data formatting | bytes 2097152 | tf_op jit(solution)/shard_map/reshape | solution.py:59
  101.7 0.1 copy.10
  101.9 0.1 broadcast.622
  102.0 0.1 reshape.301
  102.1 0.1 broadcast.629
  102.2 0.1 reshape.303
  102.4 0.1 broadcast_in_dim.28
  102.5 0.1 ne.146
  102.6 0.1 broadcast.601
  102.7 0.1 reshape.291
  102.8 0.1 broadcast.611
  102.9 0.1 reshape.297
  103.1 0.1 broadcast_in_dim.29
  103.2 0.2 select_n.157
  103.3 0.1 broadcast_in_dim.30
  103.4 0.1 gt.14
  103.6 3.3 %select_reduce_fusion = f32[256,32]{0,1:T(8,128)S(1)} fusion(f32[256,32,32]{1,0,2:T(8,128)} %reshape.285, pred[32,32]{0,1:T(8,128)(4,1)S(1)} %iota_compare_fusion.8, pred[256,32]{1,0:T(8,128)(4,1)S(1)} %copy.10), kind=kLoop, calls=%fused_computation.3 | loop fusion | flops 778240 | bytes 1090560 | tf_op jit(solution)/shard_map/reduce_sum | solution.py:64
  106.9 0.7 fusion.9
  107.6 1.6 %fusion.1 = f32[32,1000]{1,0:T(8,128)} fusion(f32[256,1000]{0,1:T(8,128)S(1)} %multiply_reduce_fusion, f32[256]{0:T(256)S(1)} %get-tuple-element.26, f32[256]{0:T(256)S(1)} %add_multiply_fusion, s32[256]{0:T(256)S(1)} %eq.74), kind=kOutput, calls=%fused_computation.8 | convolution fusion | flops 98832384 | bytes 1155072 | tf_op jit(solution)/shard_map/dot_general | solution.py:44
  109.3 0.0 reduce-scatter.2.cloned.1.call-update
  109.3 0.0 copy-done
  109.3 0.6 dynamic-slice
  110.5 0.1 select_reduce_fusion.1
  110.7 10.6 %all-reduce = f32[32]{0:T(128)S(1)} all-reduce(f32[32]{0:T(128)S(1)} %select_reduce_fusion.1), channel_id=2, replica_groups=mesh['path'=8,'tm'=4] {'tm'}, use_global_device_ids=true, to_apply=%region_7.9.clone | all-reduce | flops 32 | bytes 256
  121.2 0.1 dynamic-slice.1
  121.3 6.6 %reduce-scatter.2.cloned.1.call-done = f32[8,1000]{1,0:T(8,128)} async-done(((f32[32,1000]{1,0:T(8,128)}), f32[8,1000]{1,0:T(8,128)}) %reduce-scatter.2.cloned.1.call-update) | async-done | bytes 32016 | tf_op jit(solution)/shard_map/reduce_scatter | solution.py:93
  127.9 23.9 %all-reduce.2 = (f32[8]{0:T(128)}, f32[8,1000]{1,0:T(8,128)}) all-reduce(f32[8]{0:T(128)S(1)} %dynamic-slice.1, f32[8,1000]{1,0:T(8,128)} %reduce-scatter.2.cloned.1.call-done), channel_id=1, replica_groups=mesh['path'=8,'tm'=4] {'path'}, use_global_device_ids=true, to_apply=%region_8.10 | all-reduce | flops 8008 | bytes 64064 | tf_op jit(solution)/shard_map/psum | solution.py:99
  (12 shorter events, 0.2 us)
Async XLA Ops:
  7.2 120.7 %reduce-scatter.2.cloned.1.call-start = ((), (), s32[]{:S(2)}) async-start(), calls=%async_computation.1 | async-start | bytes 163840 | tf_op jit(solution)/shard_map/reduce_scatter | solution.py:93
  43.9 65.4 %copy-start = (u32[32]{0:T(128)S(1)}, u32[32]{0:T(128)}, u32[]{:S(2)}) copy-start(u32[32]{0:T(128)} %constant.92) | copy-start | bytes 388
Sparse Core Ops, SparseCore 0:
  109.4 18.4 reduce-scatter.1
where the time goes:
time: 160 us; the launch traced here: 159 us
  blocking collectives  78.9 us (49%)
  local copies, waits for them, and re-layouts  31.6 us (20%)
  between operations  14.9 us (9%)
  matrix products  14.2 us (9%)
  other arithmetic  12.4 us (8%)
  waiting for transfers between devices  6.62 us (4%)
    psum x1, blocking collectives, shards(): lax.psum(first_terms(increments, lvl_path, time_path, path_share, steps_k...  44.4 us
    unnamed x5, local copies, waits for them, and re-layouts  24.1 us
    psum x1, blocking collectives, shards(): value_est, grad_est = lax.psum((value_part, grad_part), 'path')  23.9 us
    dot_general x1, matrix products, second_terms(): jnp.dot(incr.reshape(paths * steps_k, width), grad_low.T, preferred_eleme...  10.7 us
    unnamed x1, blocking collectives  10.6 us
    dot_general x1, other arithmetic, terminal(): jnp.einsum('pi,pid->pd', live_steps, incr, preferred_element_type=jnp.flo...  7.07 us
    reduce_scatter x1, waiting for transfers between devices, shards(): lax.psum_scatter(second_terms(increments, lvl_path, time_path, path_share...  6.6 us
    reduce_sum x1, other arithmetic, second_terms(): jnp.sum(inner_dots * window.astype(jnp.float32), axis=1)  3.35 us
  transfers between devices with their start and end apart: 1, of which 1 were waited for; matrix products, arithmetic and copies ran while one was open for 0% of the time, Pallas kernels for 0%

commit v1 on v0

v1 whole, which is shorter than its diff:
```python
import functools

import jax
import jax.numpy as jnp
from jax import lax
from jax.experimental import pallas as pl
from jax.experimental.pallas import tpu as pltpu
from jax.sharding import PartitionSpec as P

LEVELS = 5
BLOCK = 2
LANES = 128

horizon = 0.3
f32, bf16, i32 = jnp.float32, jnp.bfloat16, jnp.int32


def round_up(value, unit):
    return -(-value // unit) * unit


def chunk_rows(width):
    return next(r for r in (40, 32, 48, 24, 16, 8) if width % r == 0)


def split3(x):
    hi = x.astype(bf16)
    rest = x - hi.astype(f32)
    mid = rest.astype(bf16)
    low = (rest - mid.astype(f32)).astype(bf16)
    return hi, mid, low


def split2(x):
    hi = x.astype(bf16)
    return hi, (x - hi.astype(f32)).astype(bf16)


def contract_last(a, b):
    return lax.dot_general(a, b, (((1,), (1,)), ((), ())), preferred_element_type=f32)


def dot(a, b):
    return jnp.dot(a, b, preferred_element_type=f32)


def path_rows(lvl_ref, time_ref, steps_k, blk_dev, my_block):
    paths = BLOCK * blk_dev
    blocks = lvl_ref.shape[1]
    start = pl.multiple_of(my_block, LANES)
    own = jnp.concatenate(
        [lvl_ref[:, pl.ds(start, blk_dev)], time_ref[:, pl.ds(start, blk_dev)]], axis=0
    ).astype(f32)
    own = jnp.concatenate([own, jnp.zeros((6, blk_dev), f32)], axis=0).astype(bf16)
    block_of = lax.broadcasted_iota(i32, (blk_dev, paths), 1) // BLOCK
    repeat = (block_of == lax.broadcasted_iota(i32, (blk_dev, paths), 0)).astype(f32).astype(bf16)
    both = dot(own, repeat)
    level, start_t = both[0:1], both[1:2]
    lvl_hot = (lax.broadcasted_iota(i32, (8, blocks), 0) == lvl_ref[...]).astype(f32).astype(bf16)
    time_hot = (
        (lax.broadcasted_iota(i32, (steps_k, blocks), 0) == time_ref[...]).astype(f32).astype(bf16)
    )
    counts = contract_last(lvl_hot, time_hot)
    high = jnp.floor(counts * (1.0 / 256.0))
    low = counts - 256.0 * high
    own_time = start_hot(start_t, steps_k)
    at_time = 256.0 * dot(high.astype(bf16), own_time) + dot(low.astype(bf16), own_time)
    own_lvl = lax.broadcasted_iota(i32, (8, paths), 0).astype(f32) == level
    count = jnp.sum(jnp.where(own_lvl, at_time, 0.0), axis=0, keepdims=True)
    return level, start_t, 1.0 / (BLOCK * count)


def start_hot(start_t, steps_k):
    rows = lax.broadcasted_iota(i32, (steps_k, start_t.shape[1]), 0).astype(f32)
    return (rows == start_t).astype(f32).astype(bf16)


def weighted_sums(end_ref, store, hot, coef, value_row, width, split):
    full = end_ref.shape[0]
    for c in range(full // LANES):
        y = end_ref[c * LANES : (c + 1) * LANES, :] * coef
        if c * LANES <= width < (c + 1) * LANES:
            row = lax.broadcasted_iota(i32, y.shape, 0)
            y = jnp.where(row == width - c * LANES, value_row, y)
        store(c, sum(contract_last(hot, part) for part in split(y)))


def first_kernel(
    n_path, n_tm, inc_ref, lvl_ref, time_ref, out_ref, end_ref, rows_ref, buf, sems
):
    steps_k, width, paths = inc_ref.shape
    blk_dev = paths // BLOCK
    step_len = horizon / steps_k
    rows = chunk_rows(width)
    chunks = width // rows

    def copy(c):
        part = pl.ds(pl.multiple_of(c * rows, 8), rows)
        return pltpu.make_async_copy(inc_ref.at[:, part, :], buf.at[:, part, :], sems.at[c])

    @pl.loop(0, chunks)
    def _(c):
        copy(c).start()

    me = lax.axis_index("path") * n_tm + lax.axis_index("tm")
    level, start_t, share = path_rows(lvl_ref, time_ref, steps_k, blk_dev, me * blk_dev)
    tile_start = jnp.broadcast_to(start_t, (8, paths))

    def chunk(c, norm):
        copy(c).wait()
        base = pl.multiple_of(c * rows, 8)
        acc = [jnp.zeros((8, paths), f32) for _ in range(rows // 8)]
        for i in range(steps_k):
            live = tile_start <= float(i)
            x = buf[i, pl.ds(base, rows), :].astype(f32)
            for r in range(rows // 8):
                acc[r] = acc[r] + jnp.where(live, x[8 * r : 8 * r + 8], 0.0)
        root = jnp.sqrt(jnp.float32(step_len))
        for r in range(rows // 8):
            end = root * acc[r]
            end_ref[pl.ds(pl.multiple_of(base + 8 * r, 8), 8), :] = end
            norm = norm + end * end
        return norm

    norm = lax.fori_loop(0, chunks, chunk, jnp.zeros((8, paths), f32))
    full = end_ref.shape[0]
    end_ref[width:full, :] = jnp.zeros((full - width, paths), f32)
    value = 1.0 / (2.0 + 0.4 * jnp.sum(norm, axis=0, keepdims=True) / width)
    first = jnp.where(level == 0.0, value, 0.0)
    remaining = horizon - start_t * step_len
    coef = share / remaining
    hot = start_hot(start_t, steps_k)
    rows_ref[...] = jnp.concatenate(
        [level, start_t, first, share, coef, jnp.zeros((3, paths), f32)], axis=0
    )
    group, cols = out_ref.shape[2], out_ref.shape[3]

    def store(c, tile):
        for part in range(LANES // cols):
            a = c * (LANES // cols) + part
            for b in range(n_tm):
                out_ref[a, b] = tile[group * b : group * (b + 1), cols * part : cols * (part + 1)]

    weighted_sums(end_ref, store, hot, coef * first, share * first, width, split3)


def second_kernel(n_path, n_tm, inc_ref, z_ref, end_ref, rows_ref, out_ref, buf, z_all, sems):
    steps_k, width, paths = inc_ref.shape
    step_len = horizon / steps_k

    def copy(i):
        return pltpu.make_async_copy(inc_ref.at[i], buf.at[i], sems.at[i])

    @pl.loop(0, steps_k)
    def _(i):
        copy(i).start()

    group, cols = z_ref.shape[2], z_ref.shape[3]
    for a in range(n_path):
        for b in range(n_tm):
            z_all[group * b : group * (b + 1), cols * a : cols * (a + 1)] = z_ref[a, b]
    value_one = z_all[:, width : width + 1]
    z_low = z_all[:, 0:width].astype(bf16)
    level, start_t, first, share, coef = (rows_ref[r : r + 1, :] for r in range(5))
    at = lax.broadcasted_iota(i32, (steps_k, paths), 0)

    total = jnp.zeros((steps_k, paths), f32)
    for i in range(steps_k - 1):
        copy(i).wait()
        dots = dot(z_low, buf[i])
        seen = (at > i) & (start_t <= float(i))
        total = total + jnp.where(seen, dots, 0.0)
    copy(steps_k - 1).wait()
    estimate = value_one + jnp.sqrt(jnp.float32(step_len)) * total
    drift = estimate - estimate * estimate * estimate
    lvl = level.astype(i32)
    fine = lax.shift_left(jnp.ones_like(lvl), LEVELS - 1 - lvl)
    on_fine = (at & (fine - 1)) == 0
    on_coarse = ((at & (2 * fine - 1)) == 0) & (lvl > 0)
    weight = jnp.where(on_fine, fine, 0) - jnp.where(on_coarse, 2 * fine, 0)
    weight = jnp.where(at.astype(f32) >= start_t, weight.astype(f32), 0.0) * step_len
    second = first + jnp.sum(weight * drift, axis=0, keepdims=True)
    hot = start_hot(start_t, steps_k)

    def store(c, tile):
        for b in range(n_tm):
            out_ref[b, :, c * LANES : (c + 1) * LANES] = tile[group * b : group * (b + 1)]

    weighted_sums(end_ref, store, hot, coef * second, share * second, width, split2)


def params():
    return pltpu.CompilerParams(vmem_limit_bytes=48 * 1024 * 1024)


def shards(n_path, n_tm, increments, level_table, time_table):
    paths, steps_k, width = increments.shape
    group = steps_k // n_tm
    full = round_up(width + 1, LANES * max(1, n_path // LANES))
    cols = full // n_path
    inc = jnp.transpose(increments, (1, 2, 0))
    vmem = pl.BlockSpec(memory_space=pltpu.VMEM)
    hbm = pl.BlockSpec(memory_space=pl.ANY)
    chunks = width // chunk_rows(width)

    pieces, end, rows = pl.pallas_call(
        functools.partial(first_kernel, n_path, n_tm),
        out_shape=(
            jax.ShapeDtypeStruct((n_path, n_tm, group, cols), f32),
            jax.ShapeDtypeStruct((full, paths), f32),
            jax.ShapeDtypeStruct((8, paths), f32),
        ),
        in_specs=[hbm, vmem, vmem],
        out_specs=(vmem, vmem, vmem),
        scratch_shapes=[
            pltpu.VMEM((steps_k, width, paths), bf16),
            pltpu.SemaphoreType.DMA((chunks,)),
        ],
        compiler_params=params(),
        name="first_iterate",
    )(inc, level_table.reshape(1, -1), time_table.reshape(1, -1))

    def exchange(x):
        return lax.all_to_all(x, ("path", "tm"), 0, 0, tiled=True)

    received = exchange(pieces.reshape(n_path * n_tm, group, cols))
    own = jnp.sum(received, axis=0)
    spread = exchange(jnp.broadcast_to(own[None], received.shape))

    parts = pl.pallas_call(
        functools.partial(second_kernel, n_path, n_tm),
        out_shape=jax.ShapeDtypeStruct((n_tm, group, full), f32),
        in_specs=[hbm, vmem, vmem, vmem],
        out_specs=vmem,
        scratch_shapes=[
            pltpu.VMEM((steps_k, width, paths), bf16),
            pltpu.VMEM((steps_k, full), f32),
            pltpu.SemaphoreType.DMA((steps_k,)),
        ],
        compiler_params=params(),
        name="second_iterate",
    )(inc, spread.reshape(n_path, n_tm, group, cols), end, rows)

    over_tm = jnp.sum(lax.all_to_all(parts, "tm", 0, 0, tiled=True), axis=0)
    total = jnp.sum(lax.all_gather(over_tm, "path"), axis=0)
    return total[:, width], total[:, :width]


def solution(mesh):
    placed = (P(("path", "tm"), None, None), P(), P())
    return jax.shard_map(
        functools.partial(shards, mesh.shape["path"], mesh.shape["tm"]),
        mesh=mesh,
        in_specs=placed,
        out_specs=(P("tm"), P("tm", None)),
        check_vma=False,
    )
```

time: 160 us -> 62.4 us (0.39)
  blocking collectives: 78.9 us -> 42.6 us
  local copies, waits for them, and re-layouts: 31.6 us -> 2.14 us
  Pallas kernels: 0 us -> 16.5 us
  between operations: 14.9 us -> 0.67 us
  matrix products: 14.2 us -> 0 us
  other arithmetic: 12.4 us -> 0.06 us
  waiting for transfers between devices: 6.62 us -> 0 us
    psum x2 -> x0, blocking collectives: 68.3 us -> none  [the longest x1 44.4 us: shards(): lax.psum(first_terms(increments, lvl_path, time_path, path_share, steps_k...]
    all_to_all x0 -> x3, blocking collectives: none -> 33.9 us  [the longest x2 25.6 us: exchange(): return lax.all_to_all(x, ('path', 'tm'), 0, 0, tiled=True)]
    unnamed x5 -> x6, local copies, waits for them, and re-layouts: 24.1 us -> 1.43 us
    pallas_call x0 -> x2, Pallas kernels: none -> 16.5 us  [the longest x1 9.82 us: shards(): pl.pallas_call(functools.partial(second_kernel, n_path, n_tm), out_shape=...]
    dot_general x4 -> x0, matrix products: 14.2 us -> none  [the longest x1 10.7 us: second_terms(): jnp.dot(incr.reshape(paths * steps_k, width), grad_low.T, preferred_eleme...]
    unnamed x1 -> x0, blocking collectives: 10.6 us -> none
    all_gather x0 -> x1, blocking collectives: none -> 8.7 us  [shards(): total = jnp.sum(lax.all_gather(over_tm, 'path'), axis=0)]
    dot_general x1 -> x0, other arithmetic: 7.07 us -> none  [terminal(): jnp.einsum('pi,pid->pd', live_steps, incr, preferred_element_type=jnp.flo...]
  transfers between devices with their start and end apart: 1 -> 0, of which waited for: 1 -> 0; matrix products, arithmetic and copies ran while one was open for 0% -> 0% of each run, Pallas kernels for 0% -> 0%
where the time goes in v1:
time: 62.4 us; the launch traced here: 62 us
  blocking collectives  42.6 us (68%)
  Pallas kernels  16.5 us (26%)
  local copies, waits for them, and re-layouts  2.14 us (3%)
  between operations  0.67 us (1%)
    all_to_all x2, blocking collectives, exchange(): return lax.all_to_all(x, ('path', 'tm'), 0, 0, tiled=True)  25.6 us
    pallas_call x1, Pallas kernels, shards(): pl.pallas_call(functools.partial(second_kernel, n_path, n_tm), out_shape=...  9.82 us
    all_gather x1, blocking collectives, shards(): total = jnp.sum(lax.all_gather(over_tm, 'path'), axis=0)  8.7 us
    all_to_all x1, blocking collectives, shards(): over_tm = jnp.sum(lax.all_to_all(parts, 'tm', 0, 0, tiled=True), axis=0)  8.34 us
    pallas_call x1, Pallas kernels, shards(): pl.pallas_call(functools.partial(first_kernel, n_path, n_tm), out_shape=(...  6.72 us
    unnamed x6, local copies, waits for them, and re-layouts  1.43 us

profile of v1, /device:TPU:0, one launch (start us, length us, event | category | flops | bytes accessed | tf_op | source)
XLA Modules:
  0.0 62.0 jit_solution(8912471574040195097)
XLA Ops:
  0.6 0.0 copy-start
  0.6 0.7 %copy-done = s32[4096]{0:T(1024)S(1)} copy-done((s32[4096]{0:T(1024)S(1)}, s32[4096]{0:T(1024)}, u32[]{:S(2)}) %copy-start) | copy-done | bytes 16408
  1.3 0.0 copy-start.1
  1.4 0.7 %copy-done.1 = s32[4096]{0:T(1024)S(1)} copy-done((s32[4096]{0:T(1024)S(1)}, s32[4096]{0:T(1024)}, u32[]{:S(2)}) %copy-start.1) | copy-done | bytes 16408
  2.1 6.7 %first_iterate.1 = (f32[8,4,8,128]{3,2,1,0:T(8,128)S(1)}, f32[1024,256]{1,0:T(8,128)S(1)}, f32[8,256]{1,0:T(8,128)S(1)}) custom-call(bf16[32,1000,256]{2,1,0:T(8,128)(2,1)} %bitcast.12, s32[1,4096]{1,0:T(1,128)S(1)} %bitcast.10, s32[1,4096]{1,0:T(1,128)S(1)} %bitcast.11), custom_call_target="tpu_custom_call" | custom-call | tf_op jit(solution)/shard_map/first_iterate/pallas_call | solution.py:206
  8.8 15.5 %all_to_all.15 = f32[32,8,128]{2,1,0:T(8,128)S(1)} all-to-all(f32[32,8,128]{2,1,0:T(8,128)S(1)} %bitcast.9), channel_id=1, replica_groups=mesh['path'=8,'tm'=4] {'path','tm'}, dimensions={0} | all-to-all | bytes 262144 | tf_op jit(solution)/shard_map/all_to_all | solution.py:224
  24.4 10.1 %all_to_all.16 = f32[32,8,128]{2,1,0:T(8,128)S(1)} all-to-all(f32[32,8,128]{2,1,0:T(8,128)S(1)} %broadcast_in_dim.2), channel_id=1, replica_groups=mesh['path'=8,'tm'=4] {'path','tm'}, dimensions={0} | all-to-all | bytes 262144 | tf_op jit(solution)/shard_map/all_to_all | solution.py:224
  34.4 9.8 %second_iterate.1 = f32[4,8,1024]{2,1,0:T(8,128)S(1)} custom-call(bf16[32,1000,256]{2,1,0:T(8,128)(2,1)} %bitcast.13, f32[8,4,8,128]{3,2,1,0:T(8,128)S(1)} %bitcast.8, f32[1024,256]{1,0:T(8,128)S(1)} %get-tuple-element.6.end_ref, f32[8,256]{1,0:T(8,128)S(1)} %get-tuple-element.7.rows_ref), custom_call_target="tpu_custom_call" | custom-call | tf_op jit(solution)/shard_map/second_iterate/pallas_call | solution.py:230
  44.3 8.3 %all_to_all.17 = f32[4,8,1024]{2,1,0:T(8,128)S(1)} all-to-all(f32[4,8,1024]{2,1,0:T(8,128)S(1)} %second_iterate.1), channel_id=1, replica_groups=mesh['path'=8,'tm'=4] {'tm'}, dimensions={0} | all-to-all | bytes 262144 | tf_op jit(solution)/shard_map/all_to_all | solution.py:244
  52.6 8.7 %all-gather = f32[64,1024]{1,0:T(8,128)S(1)} all-gather(f32[8,1024]{1,0:T(8,128)S(1)} %reduce_sum.28), channel_id=2, replica_groups=mesh['path'=8,'tm'=4] {'path'}, dimensions={0}, use_global_device_ids=true | all-gather | bytes 294912 | tf_op jit(solution)/shard_map/all_gather | solution.py:245
  61.3 0.0 copy-start.2
  61.3 0.7 %slice_reduce_fusion = f32[8]{0:T(128)} fusion(f32[8,1024]{1,0:T(8,128)S(1)} %bitcast_reduce_fusion), kind=kLoop, calls=%fused_computation.1 | loop fusion | bytes 64 | tf_op jit(solution)/shard_map/slice | solution.py:246
  62.0 0.0 copy-done.2
  (4 shorter events, 0.1 us)
Async XLA Ops:
  0.6 0.7 %copy-start = (s32[4096]{0:T(1024)S(1)}, s32[4096]{0:T(1024)}, u32[]{:S(2)}) copy-start(s32[4096]{0:T(1024)} %param.4) | copy-start | bytes 49156
  1.3 0.7 %copy-start.1 = (s32[4096]{0:T(1024)S(1)}, s32[4096]{0:T(1024)}, u32[]{:S(2)}) copy-start(s32[4096]{0:T(1024)} %param.5) | copy-start | bytes 49156
  61.3 0.7 %copy-start.2 = (f32[8,1024]{1,0:T(8,128)}, f32[8,1024]{1,0:T(8,128)S(1)}, u32[]{:S(2)}) copy-start(f32[8,1024]{1,0:T(8,128)S(1)} %bitcast_reduce_fusion) | copy-start | bytes 98308

commit v2 on v1

--- a/solution.py
+++ b/solution.py
@@ -10,6 +10,8 @@
 LEVELS = 5
 BLOCK = 2
 LANES = 128
+VALUE_COPIES = 3
+VMEM_LIMIT = 24 * 1024 * 1024
 
 horizon = 0.3
 f32, bf16, i32 = jnp.float32, jnp.bfloat16, jnp.int32
@@ -79,14 +81,15 @@
     full = end_ref.shape[0]
     for c in range(full // LANES):
         y = end_ref[c * LANES : (c + 1) * LANES, :] * coef
-        if c * LANES <= width < (c + 1) * LANES:
-            row = lax.broadcasted_iota(i32, y.shape, 0)
-            y = jnp.where(row == width - c * LANES, value_row, y)
+        if (c + 1) * LANES > width:
+            row = lax.broadcasted_iota(i32, y.shape, 0) + (c * LANES - width)
+            y = jnp.where((row >= 0) & (row < VALUE_COPIES), value_row, y)
         store(c, sum(contract_last(hot, part) for part in split(y)))
 
 
 def first_kernel(
-    n_path, n_tm, inc_ref, lvl_ref, time_ref, out_ref, end_ref, rows_ref, buf, sems
+    n_path, n_tm, inc_ref, lvl_hbm, time_hbm, mine_ref, other_ref, end_ref, rows_ref, buf,
+    lvl_ref, time_ref, part_ref, sems, table_sems,
 ):
     steps_k, width, paths = inc_ref.shape
     blk_dev = paths // BLOCK
@@ -98,10 +101,19 @@
         part = pl.ds(pl.multiple_of(c * rows, 8), rows)
         return pltpu.make_async_copy(inc_ref.at[:, part, :], buf.at[:, part, :], sems.at[c])
 
+    tables = [
+        pltpu.make_async_copy(lvl_hbm, lvl_ref, table_sems.at[0]),
+        pltpu.make_async_copy(time_hbm, time_ref, table_sems.at[1]),
+    ]
+    for table in tables:
+        table.start()
+
     @pl.loop(0, chunks)
     def _(c):
         copy(c).start()
 
+    for table in tables:
+        table.wait()
     me = lax.axis_index("path") * n_tm + lax.axis_index("tm")
     level, start_t, share = path_rows(lvl_ref, time_ref, steps_k, blk_dev, me * blk_dev)
     tile_start = jnp.broadcast_to(start_t, (8, paths))
@@ -133,44 +145,40 @@
     rows_ref[...] = jnp.concatenate(
         [level, start_t, first, share, coef, jnp.zeros((3, paths), f32)], axis=0
     )
-    group, cols = out_ref.shape[2], out_ref.shape[3]
+    half = mine_ref.shape[1]
 
     def store(c, tile):
-        for part in range(LANES // cols):
-            a = c * (LANES // cols) + part
-            for b in range(n_tm):
-                out_ref[a, b] = tile[group * b : group * (b + 1), cols * part : cols * (part + 1)]
+        side, at = divmod(c * LANES, half)
+        part_ref[side, :, at : at + LANES] = tile
 
     weighted_sums(end_ref, store, hot, coef * first, share * first, width, split3)
-
-
-def second_kernel(n_path, n_tm, inc_ref, z_ref, end_ref, rows_ref, out_ref, buf, z_all, sems):
-    steps_k, width, paths = inc_ref.shape
+    side = lax.axis_index("path") % 2
+    mine_ref[...] = part_ref[side]
+    other_ref[...] = part_ref[1 - side]
+
+
+def second_kernel(
+    n_path, n_tm, buf, mine_ref, other_ref, end_ref, rows_ref, out_mine, out_other, z_ref, part_ref
+):
+    steps_k, width, paths = buf.shape
     step_len = horizon / steps_k
-
-    def copy(i):
-        return pltpu.make_async_copy(inc_ref.at[i], buf.at[i], sems.at[i])
-
-    @pl.loop(0, steps_k)
-    def _(i):
-        copy(i).start()
-
-    group, cols = z_ref.shape[2], z_ref.shape[3]
-    for a in range(n_path):
-        for b in range(n_tm):
-            z_all[group * b : group * (b + 1), cols * a : cols * (a + 1)] = z_ref[a, b]
-    value_one = z_all[:, width : width + 1]
-    z_low = z_all[:, 0:width].astype(bf16)
+    half = mine_ref.shape[1]
+    group = steps_k // n_tm
+    side = lax.axis_index("path") % 2
+    z_ref[side] = mine_ref[...].astype(f32)
+    z_ref[1 - side] = other_ref[...].astype(f32)
+    value_one = sum(
+        z_ref[1, :, width + r - half : width + r - half + 1] for r in range(VALUE_COPIES)
+    )
+    z_low = jnp.concatenate([z_ref[0], z_ref[1]], axis=1)[:, :width].astype(bf16)
     level, start_t, first, share, coef = (rows_ref[r : r + 1, :] for r in range(5))
     at = lax.broadcasted_iota(i32, (steps_k, paths), 0)
 
     total = jnp.zeros((steps_k, paths), f32)
     for i in range(steps_k - 1):
-        copy(i).wait()
         dots = dot(z_low, buf[i])
         seen = (at > i) & (start_t <= float(i))
         total = total + jnp.where(seen, dots, 0.0)
-    copy(steps_k - 1).wait()
     estimate = value_one + jnp.sqrt(jnp.float32(step_len)) * total
     drift = estimate - estimate * estimate * estimate
     lvl = level.astype(i32)
@@ -183,66 +191,129 @@
     hot = start_hot(start_t, steps_k)
 
     def store(c, tile):
-        for b in range(n_tm):
-            out_ref[b, :, c * LANES : (c + 1) * LANES] = tile[group * b : group * (b + 1)]
+        part, at = divmod(c * LANES, half)
+        part_ref[part, :, at : at + LANES] = tile
 
     weighted_sums(end_ref, store, hot, coef * second, share * second, width, split2)
+    me = lax.axis_index("tm")
+    for away in range(n_tm):
+        rows = pl.ds(pl.multiple_of((me ^ away) * group, group), group)
+        out_mine[away] = part_ref[side, rows, :]
+        out_other[away] = part_ref[1 - side, rows, :]
 
 
 def params():
-    return pltpu.CompilerParams(vmem_limit_bytes=48 * 1024 * 1024)
+    return pltpu.CompilerParams(vmem_limit_bytes=VMEM_LIMIT)
+
+
+def in_hbm(x):
+    return pltpu.with_memory_space_constraint(x, pltpu.HBM)
+
+
+def swap(x, axis, offset):
+    return lax.ppermute(x, axis, [(i, i ^ offset) for i in range(lax.axis_size(axis))])
+
+
+def add_kernel(*refs):
+    *parts, out_ref = refs
+    out_ref[...] = pairwise([part[...] for part in parts])
+
+
+def round_kernel(width, *refs):
+    *parts, out_ref = refs
+    total = pairwise([part[...] for part in parts])
+    first = lax.axis_index("path") % 2 * total.shape[1] - width
+    column = lax.broadcasted_iota(i32, total.shape, 1) + first
+    high, middle, low = (part.astype(f32) for part in split3(total))
+    out_ref[...] = jnp.where(column == 1, middle, jnp.where(column == 2, low, high)).astype(bf16)
+
+
+def pairwise(parts):
+    while len(parts) > 1:
+        parts = [a + b for a, b in zip(parts[::2], parts[1::2])]
+    return parts[0]
+
+
+def local(kernel, dtype, parts):
+    vmem = pl.BlockSpec(memory_space=pltpu.VMEM)
+    return pl.pallas_call(
+        kernel,
+        out_shape=jax.ShapeDtypeStruct(parts[0].shape, dtype),
+        in_specs=[vmem] * len(parts),
+        out_specs=vmem,
+        compiler_params=pltpu.CompilerParams(vmem_limit_bytes=4 * 1024 * 1024),
+    )(*parts)
+
+
+def terms(x, axis, first_bit):
+    ways = 4 if 2 * first_bit < lax.axis_size(axis) else 2
+    return [x] + [swap(x, axis, first_bit * away) for away in range(1, ways)]
+
+
+def steps_over(axis, first_bit):
+    bits = []
+    while first_bit < lax.axis_size(axis):
+        bits.append((axis, first_bit))
+        first_bit *= 4
+    return bits
 
 
 def shards(n_path, n_tm, increments, level_table, time_table):
     paths, steps_k, width = increments.shape
     group = steps_k // n_tm
-    full = round_up(width + 1, LANES * max(1, n_path // LANES))
-    cols = full // n_path
+    full = round_up(width + VALUE_COPIES, 2 * LANES)
+    half = full // 2
     inc = jnp.transpose(increments, (1, 2, 0))
     vmem = pl.BlockSpec(memory_space=pltpu.VMEM)
-    hbm = pl.BlockSpec(memory_space=pl.ANY)
+    hbm = pl.BlockSpec(memory_space=pltpu.HBM)
     chunks = width // chunk_rows(width)
-
-    pieces, end, rows = pl.pallas_call(
+    side = lax.axis_index("path") % 2
+
+    mine, other, end, rows, held = pl.pallas_call(
         functools.partial(first_kernel, n_path, n_tm),
         out_shape=(
-            jax.ShapeDtypeStruct((n_path, n_tm, group, cols), f32),
+            jax.ShapeDtypeStruct((steps_k, half), f32),
+            jax.ShapeDtypeStruct((steps_k, half), f32),
             jax.ShapeDtypeStruct((full, paths), f32),
             jax.ShapeDtypeStruct((8, paths), f32),
+            pltpu.VMEM(inc.shape, bf16),
         ),
-        in_specs=[hbm, vmem, vmem],
-        out_specs=(vmem, vmem, vmem),
+        in_specs=[hbm, hbm, hbm],
+        out_specs=(vmem,) * 5,
         scratch_shapes=[
-            pltpu.VMEM((steps_k, width, paths), bf16),
+            pltpu.VMEM((1, level_table.shape[0]), i32),
+            pltpu.VMEM((1, time_table.shape[0]), i32),
+            pltpu.VMEM((2, steps_k, half), f32),
             pltpu.SemaphoreType.DMA((chunks,)),
+            pltpu.SemaphoreType.DMA((2,)),
         ],
         compiler_params=params(),
         name="first_iterate",
-    )(inc, level_table.reshape(1, -1), time_table.reshape(1, -1))
-
-    def exchange(x):
-        return lax.all_to_all(x, ("path", "tm"), 0, 0, tiled=True)
-
-    received = exchange(pieces.reshape(n_path * n_tm, group, cols))
-    own = jnp.sum(received, axis=0)
-    spread = exchange(jnp.broadcast_to(own[None], received.shape))
-
-    parts = pl.pallas_call(
+    )(inc, *(in_hbm(table.reshape(1, -1)) for table in (level_table, time_table)))
+
+    parts = [mine, swap(other, "path", 1)]
+    for step in steps_over("path", 2) + steps_over("tm", 1):
+        parts = terms(local(add_kernel, f32, parts), *step)
+    own = local(functools.partial(round_kernel, width), bf16, parts)
+
+    mine, other = pl.pallas_call(
         functools.partial(second_kernel, n_path, n_tm),
-        out_shape=jax.ShapeDtypeStruct((n_tm, group, full), f32),
-        in_specs=[hbm, vmem, vmem, vmem],
-        out_specs=vmem,
-        scratch_shapes=[
-            pltpu.VMEM((steps_k, width, paths), bf16),
-            pltpu.VMEM((steps_k, full), f32),
-            pltpu.SemaphoreType.DMA((steps_k,)),
-        ],
+        out_shape=(jax.ShapeDtypeStruct((n_tm, group, half), f32),) * 2,
+        in_specs=[vmem] * 5,
+        out_specs=(vmem, vmem),
+        scratch_shapes=[pltpu.VMEM((2, steps_k, half), f32)] * 2,
         compiler_params=params(),
         name="second_iterate",
-    )(inc, spread.reshape(n_path, n_tm, group, cols), end, rows)
-
-    over_tm = jnp.sum(lax.all_to_all(parts, "tm", 0, 0, tiled=True), axis=0)
-    total = jnp.sum(lax.all_gather(over_tm, "path"), axis=0)
+    )(pltpu.with_memory_space_constraint(held, pltpu.VMEM), own, swap(own, "path", 1), end, rows)
+
+    part = mine + swap(other, "path", 1)
+    own = pairwise([part[0]] + [swap(part[away], "tm", away) for away in range(1, n_tm)])
+    for step in steps_over("path", 2):
+        own = pairwise(terms(own, *step))
+    other = swap(own, "path", 1)
+    total = jnp.concatenate(
+        [jnp.where(side == 0, own, other), jnp.where(side == 0, other, own)], axis=1
+    )
     return total[:, width], total[:, :width]
 
 

time: 62.4 us -> 49.9 us (0.80)
  blocking collectives: 42.6 us -> 0 us
  waiting for transfers between devices: 0 us -> 20.3 us
  starting transfers between devices: 0 us -> 16.9 us
  Pallas kernels: 16.5 us -> 10.4 us
  local copies, waits for them, and re-layouts: 2.14 us -> 0.7 us
    all_to_all x3 -> x0, blocking collectives: 33.9 us -> none  [the longest x2 25.6 us: exchange(): return lax.all_to_all(x, ('path', 'tm'), 0, 0, tiled=True)]
    ppermute x0 -> x16, waiting for transfers between devices: none -> 20.3 us  [swap(): lax.ppermute(x, axis, [(i, i ^ offset) for i in range(lax.axis_size(axis))])]
    ppermute x0 -> x16, starting transfers between devices: none -> 16.9 us  [swap(): lax.ppermute(x, axis, [(i, i ^ offset) for i in range(lax.axis_size(axis))])]
    all_gather x1 -> x0, blocking collectives: 8.7 us -> none  [shards(): total = jnp.sum(lax.all_gather(over_tm, 'path'), axis=0)]
    pallas_call x1, Pallas kernels: 9.82 us -> 3.46 us  [shards(): pl.pallas_call(functools.partial(second_kernel, n_path, n_tm), out_shape=...]
    unnamed x6 -> x0, local copies, waits for them, and re-layouts: 1.43 us -> none
  transfers between devices with their start and end apart: 0 -> 16, of which waited for: 0 -> 15; matrix products, arithmetic and copies ran while one was open for 0% -> 0% of each run, Pallas kernels for 0% -> 0%
where the time goes in v2:
time: 49.9 us; the launch traced here: 49.6 us
  waiting for transfers between devices  20.3 us (41%)
  starting transfers between devices  16.9 us (34%)
  Pallas kernels  10.4 us (21%)
  between operations  0.71 us (1%)
  local copies, waits for them, and re-layouts  0.7 us (1%)
  other arithmetic  0.65 us (1%)
    ppermute x16, waiting for transfers between devices, swap(): lax.ppermute(x, axis, [(i, i ^ offset) for i in range(lax.axis_size(axis))])  20.3 us
    ppermute x16, starting transfers between devices, swap(): lax.ppermute(x, axis, [(i, i ^ offset) for i in range(lax.axis_size(axis))])  16.9 us
    pallas_call x1, Pallas kernels, shards(): pl.pallas_call(functools.partial(first_kernel, n_path, n_tm), out_shape=(...  6.87 us
    pallas_call x1, Pallas kernels, shards(): pl.pallas_call(functools.partial(second_kernel, n_path, n_tm), out_shape=...  3.46 us
  transfers between devices with their start and end apart: 16, of which 15 were waited for; matrix products, arithmetic and copies ran while one was open for 0% of the time, Pallas kernels for 0%

profile of v2, /device:TPU:0, one launch (start us, length us, event | category | flops | bytes accessed | tf_op | source)
XLA Modules:
  0.0 49.6 jit_solution(10835760227292229345)
XLA Ops:
  0.6 6.9 %first_iterate.1 = (f32[32,512]{1,0:T(8,128)S(1)}, f32[32,512]{1,0:T(8,128)S(1)}, f32[1024,256]{1,0:T(8,128)S(1)}, f32[8,256]{1,0:T(8,128)S(1)}, bf16[32,1000,256]{2,1,0:T(8,128)(2,1)S(1)}) custom-call(bf16[32,1000,256]{2,1,0:T(8,128)(2,1)} %bitcast.15, s32[1,4096]{1,0:T(1,128)} %bitcast.16, s32[1,4096]{1,0:T(1,128)} %bitcast.17), custom_call_target="tpu_custom_call" | custom-call | tf_op jit(solution)/shard_map/first_iterate/pallas_call | solution.py:272
  7.5 0.6 %collective-permute-start = (f32[32,512]{1,0:T(8,128)S(1)}, f32[32,512]{1,0:T(8,128)S(1)}, u32[]{:S(2)}, u32[]{:S(2)}) collective-permute-start(f32[32,512]{1,0:T(8,128)S(1)} %get-tuple-element.11), channel_id=1, source_target_pairs={{0,4},{4,0},{8,12},{12,8},{16,20},{20,16},{24,28},{28,24},{1,5},{5... | collective-permute-start | bytes 196616 | tf_op jit(solution)/shard_map/ppermute | solution.py:214
  8.1 0.9 %collective-permute-done.refs_1_ = f32[32,512]{1,0:T(8,128)S(1)} collective-permute-done((f32[32,512]{1,0:T(8,128)S(1)}, f32[32,512]{1,0:T(8,128)S(1)}, u32[]{:S(2)}, u32[]{:S(2)}) %collective-permute-start) | collective-permute-done | bytes 65568 | tf_op jit(solution)/shard_map/ppermute | solution.py:214
  9.0 2.9 %collective-permute-start.1 = (f32[32,512]{1,0:T(8,128)S(1)}, f32[32,512]{1,0:T(8,128)S(1)}, u32[]{:S(2)}, u32[]{:S(2)}) collective-permute-start(f32[32,512]{1,0:T(8,128)S(1)} %shard_map.50.refs_0_), channel_id=1, source_target_pairs={{0,8},{4,12},{8,0},{12,4},{16,24},{20,28},{24,16},{28,20},{1,9},{5... | collective-permute-start | bytes 196616 | tf_op jit(solution)/shard_map/ppermute | solution.py:214
  11.9 1.5 %collective-permute-start.2 = (f32[32,512]{1,0:T(8,128)S(1)}, f32[32,512]{1,0:T(8,128)S(1)}, u32[]{:S(2)}, u32[]{:S(2)}) collective-permute-start(f32[32,512]{1,0:T(8,128)S(1)} %shard_map.50.refs_0_), channel_id=1, source_target_pairs={{0,16},{4,20},{8,24},{12,28},{16,0},{20,4},{24,8},{28,12},{1,17},{... | collective-permute-start | bytes 196616 | tf_op jit(solution)/shard_map/ppermute | solution.py:214
  13.4 0.0 collective-permute-start.3
  13.4 0.9 %collective-permute-done.1.refs_1_ = f32[32,512]{1,0:T(8,128)S(1)} collective-permute-done((f32[32,512]{1,0:T(8,128)S(1)}, f32[32,512]{1,0:T(8,128)S(1)}, u32[]{:S(2)}, u32[]{:S(2)}) %collective-permute-start.1) | collective-permute-done | bytes 65568 | tf_op jit(solution)/shard_map/ppermute | solution.py:214
  14.3 1.9 %collective-permute-done.2.refs_2_ = f32[32,512]{1,0:T(8,128)S(1)} collective-permute-done((f32[32,512]{1,0:T(8,128)S(1)}, f32[32,512]{1,0:T(8,128)S(1)}, u32[]{:S(2)}, u32[]{:S(2)}) %collective-permute-start.2) | collective-permute-done | bytes 65568 | tf_op jit(solution)/shard_map/ppermute | solution.py:214
  16.1 2.4 %collective-permute-done.3.refs_3_ = f32[32,512]{1,0:T(8,128)S(1)} collective-permute-done((f32[32,512]{1,0:T(8,128)S(1)}, f32[32,512]{1,0:T(8,128)S(1)}, u32[]{:S(2)}, u32[]{:S(2)}) %collective-permute-start.3) | collective-permute-done | bytes 65568 | tf_op jit(solution)/shard_map/ppermute | solution.py:214
  18.6 1.6 %collective-permute-start.4 = (f32[32,512]{1,0:T(8,128)S(1)}, f32[32,512]{1,0:T(8,128)S(1)}, u32[]{:S(2)}, u32[]{:S(2)}) collective-permute-start(f32[32,512]{1,0:T(8,128)S(1)} %shard_map.51.refs_0_), channel_id=1, source_target_pairs={{0,1},{1,0},{2,3},{3,2},{4,5},{5,4},{6,7},{7,6},{8,9},{9,8},{10,11... | collective-permute-start | bytes 196616 | tf_op jit(solution)/shard_map/ppermute | solution.py:214
  20.2 2.6 %collective-permute-start.5 = (f32[32,512]{1,0:T(8,128)S(1)}, f32[32,512]{1,0:T(8,128)S(1)}, u32[]{:S(2)}, u32[]{:S(2)}) collective-permute-start(f32[32,512]{1,0:T(8,128)S(1)} %shard_map.51.refs_0_), channel_id=1, source_target_pairs={{0,2},{1,3},{2,0},{3,1},{4,6},{5,7},{6,4},{7,5},{8,10},{9,11},{10,... | collective-permute-start | bytes 196616 | tf_op jit(solution)/shard_map/ppermute | solution.py:214
  22.8 0.2 collective-permute-start.6
  23.0 0.2 collective-permute-done.4.refs_1_
  23.2 3.6 %collective-permute-done.5.refs_2_ = f32[32,512]{1,0:T(8,128)S(1)} collective-permute-done((f32[32,512]{1,0:T(8,128)S(1)}, f32[32,512]{1,0:T(8,128)S(1)}, u32[]{:S(2)}, u32[]{:S(2)}) %collective-permute-start.5) | collective-permute-done | bytes 65568 | tf_op jit(solution)/shard_map/ppermute | solution.py:214
  26.8 2.1 %collective-permute-done.6.refs_3_ = f32[32,512]{1,0:T(8,128)S(1)} collective-permute-done((f32[32,512]{1,0:T(8,128)S(1)}, f32[32,512]{1,0:T(8,128)S(1)}, u32[]{:S(2)}, u32[]{:S(2)}) %collective-permute-start.6) | collective-permute-done | bytes 65568 | tf_op jit(solution)/shard_map/ppermute | solution.py:214
  28.9 0.1 collective-permute-start.7
  29.0 1.2 %collective-permute-done.7.other_ref = bf16[32,512]{1,0:T(8,128)(2,1)S(1)} collective-permute-done((bf16[32,512]{1,0:T(8,128)(2,1)S(1)}, bf16[32,512]{1,0:T(8,128)(2,1)S(1)}, u32[]{:S(2)}, u32[]{:S(2)}) %collective-permute-start.7) | collective-permute-done | bytes 32800 | tf_op jit(solution)/shard_map/ppermute | solution.py:214
  30.2 3.5 %second_iterate.1 = (f32[4,8,512]{2,1,0:T(8,128)S(1)}, f32[4,8,512]{2,1,0:T(8,128)S(1)}) custom-call(bf16[32,1000,256]{2,1,0:T(8,128)(2,1)S(1)} %get-tuple-element.9.buf, bf16[32,512]{1,0:T(8,128)(2,1)S(1)} %shard_map.52.mine_ref, bf16[32,512]{1,0:T(8,128)(2,1)S(1)} %collective-permute-done.7.other_ref, f32[1024,256]{1,0:T(8,128)S(1)} %get-tuple-element.12.end_ref, ...), custom_call_target="tpu_custom_call" | custom-call | tf_op jit(solution)/shard_map/second_iterate/pallas_call | solution.py:299
  33.7 0.2 collective-permute-start.8
  33.9 1.1 %collective-permute-done.8 = f32[4,8,512]{2,1,0:T(8,128)S(1)} collective-permute-done((f32[4,8,512]{2,1,0:T(8,128)S(1)}, f32[4,8,512]{2,1,0:T(8,128)S(1)}, u32[]{:S(2)}, u32[]{:S(2)}) %collective-permute-start.8) | collective-permute-done | bytes 65568 | tf_op jit(solution)/shard_map/ppermute | solution.py:214
  35.0 0.6 %collective-permute-start.10 = (f32[8,512]{1,0:T(8,128)S(1)}, f32[8,512]{1,0:T(8,128)S(1)}, u32[]{:S(2)}, u32[]{:S(2)}) collective-permute-start(f32[8,512]{1,0:T(8,128)S(1)} %get-tuple-element.17), channel_id=1, source_target_pairs={{0,2},{1,3},{2,0},{3,1},{4,6},{5,7},{6,4},{7,5},{8,10},{9,11},{10,... | collective-permute-start | bytes 49160 | tf_op jit(solution)/shard_map/ppermute | solution.py:214
  35.6 1.0 %collective-permute-start.11 = (f32[8,512]{1,0:T(8,128)S(1)}, f32[8,512]{1,0:T(8,128)S(1)}, u32[]{:S(2)}, u32[]{:S(2)}) collective-permute-start(f32[8,512]{1,0:T(8,128)S(1)} %get-tuple-element.16), channel_id=1, source_target_pairs={{0,3},{1,2},{2,1},{3,0},{4,7},{5,6},{6,5},{7,4},{8,11},{9,10},{10,... | collective-permute-start | bytes 49160 | tf_op jit(solution)/shard_map/ppermute | solution.py:214
  36.6 1.9 %collective-permute-start.9 = (f32[8,512]{1,0:T(8,128)S(1)}, f32[8,512]{1,0:T(8,128)S(1)}, u32[]{:S(2)}, u32[]{:S(2)}) collective-permute-start(f32[8,512]{1,0:T(8,128)S(1)} %get-tuple-element.18), channel_id=1, source_target_pairs={{0,1},{1,0},{2,3},{3,2},{4,5},{5,4},{6,7},{7,6},{8,9},{9,8},{10,11... | collective-permute-start | bytes 49160 | tf_op jit(solution)/shard_map/ppermute | solution.py:214
  38.6 1.1 %collective-permute-done.10 = f32[8,512]{1,0:T(8,128)S(1)} collective-permute-done((f32[8,512]{1,0:T(8,128)S(1)}, f32[8,512]{1,0:T(8,128)S(1)}, u32[]{:S(2)}, u32[]{:S(2)}) %collective-permute-start.10) | collective-permute-done | bytes 16416 | tf_op jit(solution)/shard_map/ppermute | solution.py:214
  39.7 1.4 %collective-permute-done.11 = f32[8,512]{1,0:T(8,128)S(1)} collective-permute-done((f32[8,512]{1,0:T(8,128)S(1)}, f32[8,512]{1,0:T(8,128)S(1)}, u32[]{:S(2)}, u32[]{:S(2)}) %collective-permute-start.11) | collective-permute-done | bytes 16416 | tf_op jit(solution)/shard_map/ppermute | solution.py:214
  41.1 0.0 collective-permute-done.9
  41.1 0.7 %collective-permute-start.12 = (f32[8,512]{1,0:T(8,128)S(1)}, f32[8,512]{1,0:T(8,128)S(1)}, u32[]{:S(2)}, u32[]{:S(2)}) collective-permute-start(f32[8,512]{1,0:T(8,128)S(1)} %fusion.1), channel_id=1, source_target_pairs={{0,8},{4,12},{8,0},{12,4},{16,24},{20,28},{24,16},{28,20},{1,9},{5... | collective-permute-start | bytes 49160 | tf_op jit(solution)/shard_map/ppermute | solution.py:214
  41.8 0.6 %collective-permute-start.13 = (f32[8,512]{1,0:T(8,128)S(1)}, f32[8,512]{1,0:T(8,128)S(1)}, u32[]{:S(2)}, u32[]{:S(2)}) collective-permute-start(f32[8,512]{1,0:T(8,128)S(1)} %fusion.1), channel_id=1, source_target_pairs={{0,16},{4,20},{8,24},{12,28},{16,0},{20,4},{24,8},{28,12},{1,17},{... | collective-permute-start | bytes 49160 | tf_op jit(solution)/shard_map/ppermute | solution.py:214
  42.4 2.3 %collective-permute-start.14 = (f32[8,512]{1,0:T(8,128)S(1)}, f32[8,512]{1,0:T(8,128)S(1)}, u32[]{:S(2)}, u32[]{:S(2)}) collective-permute-start(f32[8,512]{1,0:T(8,128)S(1)} %fusion.1), channel_id=1, source_target_pairs={{0,24},{4,28},{8,16},{12,20},{16,8},{20,12},{24,0},{28,4},{1,25},{... | collective-permute-start | bytes 49160 | tf_op jit(solution)/shard_map/ppermute | solution.py:214
  44.7 0.2 collective-permute-done.12
  44.9 0.6 %collective-permute-done.13 = f32[8,512]{1,0:T(8,128)S(1)} collective-permute-done((f32[8,512]{1,0:T(8,128)S(1)}, f32[8,512]{1,0:T(8,128)S(1)}, u32[]{:S(2)}, u32[]{:S(2)}) %collective-permute-start.13) | collective-permute-done | bytes 16416 | tf_op jit(solution)/shard_map/ppermute | solution.py:214
  45.5 1.5 %collective-permute-done.14 = f32[8,512]{1,0:T(8,128)S(1)} collective-permute-done((f32[8,512]{1,0:T(8,128)S(1)}, f32[8,512]{1,0:T(8,128)S(1)}, u32[]{:S(2)}, u32[]{:S(2)}) %collective-permute-start.14) | collective-permute-done | bytes 16416 | tf_op jit(solution)/shard_map/ppermute | solution.py:214
  47.1 0.1 collective-permute-start.15
  47.1 1.2 %collective-permute-done.15 = f32[8,512]{1,0:T(8,128)S(1)} collective-permute-done((f32[8,512]{1,0:T(8,128)S(1)}, f32[8,512]{1,0:T(8,128)S(1)}, u32[]{:S(2)}, u32[]{:S(2)}) %collective-permute-start.15) | collective-permute-done | bytes 16416 | tf_op jit(solution)/shard_map/ppermute | solution.py:214
  48.3 0.7 %slice_reduce_fusion = f32[8]{0:T(128)} fusion(f32[8,512]{1,0:T(8,128)S(1)} %get-tuple-element.20), kind=kLoop, calls=%fused_computation.10 | loop fusion | bytes 64 | tf_op jit(solution)/shard_map/slice | solution.py:317
  49.0 0.6 %pad_maximum_fusion = f32[8,1000]{1,0:T(8,128)} fusion(f32[8,512]{1,0:T(8,128)S(1)} %get-tuple-element.20, f32[8,512]{1,0:T(8,128)S(1)} %get-tuple-element.19), kind=kLoop, calls=%fused_computation | loop fusion | flops 8000 | bytes 64768 | tf_op jit(solution)/shard_map/concatenate | solution.py:314
  (8 shorter events, 0.1 us)
Async XLA Ops:
  7.5 1.5 %collective-permute-start = (f32[32,512]{1,0:T(8,128)S(1)}, f32[32,512]{1,0:T(8,128)S(1)}, u32[]{:S(2)}, u32[]{:S(2)}) collective-permute-start(f32[32,512]{1,0:T(8,128)S(1)} %get-tuple-element.11), channel_id=1, source_target_pairs={{0,4},{4,0},{8,12},{12,8},{16,20},{20,16},{24,28},{28,24},{1,5},{5... | collective-permute-start | bytes 196616 | tf_op jit(solution)/shard_map/ppermute | solution.py:214
  9.0 5.3 %collective-permute-start.1 = (f32[32,512]{1,0:T(8,128)S(1)}, f32[32,512]{1,0:T(8,128)S(1)}, u32[]{:S(2)}, u32[]{:S(2)}) collective-permute-start(f32[32,512]{1,0:T(8,128)S(1)} %shard_map.50.refs_0_), channel_id=1, source_target_pairs={{0,8},{4,12},{8,0},{12,4},{16,24},{20,28},{24,16},{28,20},{1,9},{5... | collective-permute-start | bytes 196616 | tf_op jit(solution)/shard_map/ppermute | solution.py:214
  11.9 4.3 %collective-permute-start.2 = (f32[32,512]{1,0:T(8,128)S(1)}, f32[32,512]{1,0:T(8,128)S(1)}, u32[]{:S(2)}, u32[]{:S(2)}) collective-permute-start(f32[32,512]{1,0:T(8,128)S(1)} %shard_map.50.refs_0_), channel_id=1, source_target_pairs={{0,16},{4,20},{8,24},{12,28},{16,0},{20,4},{24,8},{28,12},{1,17},{... | collective-permute-start | bytes 196616 | tf_op jit(solution)/shard_map/ppermute | solution.py:214
  13.4 5.2 %collective-permute-start.3 = (f32[32,512]{1,0:T(8,128)S(1)}, f32[32,512]{1,0:T(8,128)S(1)}, u32[]{:S(2)}, u32[]{:S(2)}) collective-permute-start(f32[32,512]{1,0:T(8,128)S(1)} %shard_map.50.refs_0_), channel_id=1, source_target_pairs={{0,24},{4,28},{8,16},{12,20},{16,8},{20,12},{24,0},{28,4},{1,25},{... | collective-permute-start | bytes 196616 | tf_op jit(solution)/shard_map/ppermute | solution.py:214
  18.6 4.6 %collective-permute-start.4 = (f32[32,512]{1,0:T(8,128)S(1)}, f32[32,512]{1,0:T(8,128)S(1)}, u32[]{:S(2)}, u32[]{:S(2)}) collective-permute-start(f32[32,512]{1,0:T(8,128)S(1)} %shard_map.51.refs_0_), channel_id=1, source_target_pairs={{0,1},{1,0},{2,3},{3,2},{4,5},{5,4},{6,7},{7,6},{8,9},{9,8},{10,11... | collective-permute-start | bytes 196616 | tf_op jit(solution)/shard_map/ppermute | solution.py:214
  20.2 6.6 %collective-permute-start.5 = (f32[32,512]{1,0:T(8,128)S(1)}, f32[32,512]{1,0:T(8,128)S(1)}, u32[]{:S(2)}, u32[]{:S(2)}) collective-permute-start(f32[32,512]{1,0:T(8,128)S(1)} %shard_map.51.refs_0_), channel_id=1, source_target_pairs={{0,2},{1,3},{2,0},{3,1},{4,6},{5,7},{6,4},{7,5},{8,10},{9,11},{10,... | collective-permute-start | bytes 196616 | tf_op jit(solution)/shard_map/ppermute | solution.py:214
  22.8 6.1 %collective-permute-start.6 = (f32[32,512]{1,0:T(8,128)S(1)}, f32[32,512]{1,0:T(8,128)S(1)}, u32[]{:S(2)}, u32[]{:S(2)}) collective-permute-start(f32[32,512]{1,0:T(8,128)S(1)} %shard_map.51.refs_0_), channel_id=1, source_target_pairs={{0,3},{1,2},{2,1},{3,0},{4,7},{5,6},{6,5},{7,4},{8,11},{9,10},{10,... | collective-permute-start | bytes 196616 | tf_op jit(solution)/shard_map/ppermute | solution.py:214
  28.9 1.3 %collective-permute-start.7 = (bf16[32,512]{1,0:T(8,128)(2,1)S(1)}, bf16[32,512]{1,0:T(8,128)(2,1)S(1)}, u32[]{:S(2)}, u32[]{:S(2)}) collective-permute-start(bf16[32,512]{1,0:T(8,128)(2,1)S(1)} %shard_map.52.mine_ref), channel_id=1, source_target_pairs={{0,4},{4,0},{8,12},{12,8},{16,20},{20,16},{24,28},{28,24},{1,5},{5... | collective-permute-start | bytes 98312 | tf_op jit(solution)/shard_map/ppermute | solution.py:214
  33.7 1.3 %collective-permute-start.8 = (f32[4,8,512]{2,1,0:T(8,128)S(1)}, f32[4,8,512]{2,1,0:T(8,128)S(1)}, u32[]{:S(2)}, u32[]{:S(2)}) collective-permute-start(f32[4,8,512]{2,1,0:T(8,128)S(1)} %get-tuple-element.15), channel_id=1, source_target_pairs={{0,4},{4,0},{8,12},{12,8},{16,20},{20,16},{24,28},{28,24},{1,5},{5... | collective-permute-start | bytes 196616 | tf_op jit(solution)/shard_map/ppermute | solution.py:214
  35.0 4.7 %collective-permute-start.10 = (f32[8,512]{1,0:T(8,128)S(1)}, f32[8,512]{1,0:T(8,128)S(1)}, u32[]{:S(2)}, u32[]{:S(2)}) collective-permute-start(f32[8,512]{1,0:T(8,128)S(1)} %get-tuple-element.17), channel_id=1, source_target_pairs={{0,2},{1,3},{2,0},{3,1},{4,6},{5,7},{6,4},{7,5},{8,10},{9,11},{10,... | collective-permute-start | bytes 49160 | tf_op jit(solution)/shard_map/ppermute | solution.py:214
  35.6 5.5 %collective-permute-start.11 = (f32[8,512]{1,0:T(8,128)S(1)}, f32[8,512]{1,0:T(8,128)S(1)}, u32[]{:S(2)}, u32[]{:S(2)}) collective-permute-start(f32[8,512]{1,0:T(8,128)S(1)} %get-tuple-element.16), channel_id=1, source_target_pairs={{0,3},{1,2},{2,1},{3,0},{4,7},{5,6},{6,5},{7,4},{8,11},{9,10},{10,... | collective-permute-start | bytes 49160 | tf_op jit(solution)/shard_map/ppermute | solution.py:214
  36.6 4.5 %collective-permute-start.9 = (f32[8,512]{1,0:T(8,128)S(1)}, f32[8,512]{1,0:T(8,128)S(1)}, u32[]{:S(2)}, u32[]{:S(2)}) collective-permute-start(f32[8,512]{1,0:T(8,128)S(1)} %get-tuple-element.18), channel_id=1, source_target_pairs={{0,1},{1,0},{2,3},{3,2},{4,5},{5,4},{6,7},{7,6},{8,9},{9,8},{10,11... | collective-permute-start | bytes 49160 | tf_op jit(solution)/shard_map/ppermute | solution.py:214
  41.1 3.8 %collective-permute-start.12 = (f32[8,512]{1,0:T(8,128)S(1)}, f32[8,512]{1,0:T(8,128)S(1)}, u32[]{:S(2)}, u32[]{:S(2)}) collective-permute-start(f32[8,512]{1,0:T(8,128)S(1)} %fusion.1), channel_id=1, source_target_pairs={{0,8},{4,12},{8,0},{12,4},{16,24},{20,28},{24,16},{28,20},{1,9},{5... | collective-permute-start | bytes 49160 | tf_op jit(solution)/shard_map/ppermute | solution.py:214
  41.8 3.7 %collective-permute-start.13 = (f32[8,512]{1,0:T(8,128)S(1)}, f32[8,512]{1,0:T(8,128)S(1)}, u32[]{:S(2)}, u32[]{:S(2)}) collective-permute-start(f32[8,512]{1,0:T(8,128)S(1)} %fusion.1), channel_id=1, source_target_pairs={{0,16},{4,20},{8,24},{12,28},{16,0},{20,4},{24,8},{28,12},{1,17},{... | collective-permute-start | bytes 49160 | tf_op jit(solution)/shard_map/ppermute | solution.py:214
  42.4 4.6 %collective-permute-start.14 = (f32[8,512]{1,0:T(8,128)S(1)}, f32[8,512]{1,0:T(8,128)S(1)}, u32[]{:S(2)}, u32[]{:S(2)}) collective-permute-start(f32[8,512]{1,0:T(8,128)S(1)} %fusion.1), channel_id=1, source_target_pairs={{0,24},{4,28},{8,16},{12,20},{16,8},{20,12},{24,0},{28,4},{1,25},{... | collective-permute-start | bytes 49160 | tf_op jit(solution)/shard_map/ppermute | solution.py:214
  47.1 1.2 %collective-permute-start.15 = (f32[8,512]{1,0:T(8,128)S(1)}, f32[8,512]{1,0:T(8,128)S(1)}, u32[]{:S(2)}, u32[]{:S(2)}) collective-permute-start(f32[8,512]{1,0:T(8,128)S(1)} %add_add_fusion), channel_id=1, source_target_pairs={{0,4},{4,0},{8,12},{12,8},{16,20},{20,16},{24,28},{28,24},{1,5},{5... | collective-permute-start | bytes 49160 | tf_op jit(solution)/shard_map/ppermute | solution.py:214

commit v3 on v2

--- a/solution.py
+++ b/solution.py
@@ -11,7 +11,9 @@
 BLOCK = 2
 LANES = 128
 VALUE_COPIES = 3
+PACKED = 16
 VMEM_LIMIT = 24 * 1024 * 1024
+SMALL_LIMIT = 4 * 1024 * 1024
 
 horizon = 0.3
 f32, bf16, i32 = jnp.float32, jnp.bfloat16, jnp.int32
@@ -89,7 +91,7 @@
 
 def first_kernel(
     n_path, n_tm, inc_ref, lvl_hbm, time_hbm, mine_ref, other_ref, end_ref, rows_ref, buf,
-    lvl_ref, time_ref, part_ref, sems, table_sems,
+    lvl_ref, time_ref, part_ref, mask_ref, sems, table_sems,
 ):
     steps_k, width, paths = inc_ref.shape
     blk_dev = paths // BLOCK
@@ -116,17 +118,25 @@
         table.wait()
     me = lax.axis_index("path") * n_tm + lax.axis_index("tm")
     level, start_t, share = path_rows(lvl_ref, time_ref, steps_k, blk_dev, me * blk_dev)
-    tile_start = jnp.broadcast_to(start_t, (8, paths))
+    tile_start = jnp.broadcast_to(start_t, (PACKED, paths))
+    for i in range(steps_k):
+        mask_ref[i] = (tile_start <= float(i)).astype(f32).astype(bf16)
 
     def chunk(c, norm):
         copy(c).wait()
         base = pl.multiple_of(c * rows, 8)
         acc = [jnp.zeros((8, paths), f32) for _ in range(rows // 8)]
         for i in range(steps_k):
-            live = tile_start <= float(i)
-            x = buf[i, pl.ds(base, rows), :].astype(f32)
+            live = mask_ref[i]
+            x = buf[i, pl.ds(base, rows), :]
+            x = jnp.concatenate(
+                [x[r : r + PACKED] * live[: min(PACKED, rows - r)] for r in range(0, rows, PACKED)],
+                axis=0,
+            )
+            buf[i, pl.ds(base, rows), :] = x
+            x = x.astype(f32)
             for r in range(rows // 8):
-                acc[r] = acc[r] + jnp.where(live, x[8 * r : 8 * r + 8], 0.0)
+                acc[r] = acc[r] + x[8 * r : 8 * r + 8]
         root = jnp.sqrt(jnp.float32(step_len))
         for r in range(rows // 8):
             end = root * acc[r]
@@ -152,33 +162,36 @@
         part_ref[side, :, at : at + LANES] = tile
 
     weighted_sums(end_ref, store, hot, coef * first, share * first, width, split3)
-    side = lax.axis_index("path") % 2
+    side = my_side()
     mine_ref[...] = part_ref[side]
     other_ref[...] = part_ref[1 - side]
 
 
 def second_kernel(
-    n_path, n_tm, buf, mine_ref, other_ref, end_ref, rows_ref, out_mine, out_other, z_ref, part_ref
+    n_tm, buf, mine_ref, other_ref, end_ref, rows_ref, *refs
 ):
+    *out_refs, z_ref, part_ref = refs
     steps_k, width, paths = buf.shape
     step_len = horizon / steps_k
     half = mine_ref.shape[1]
     group = steps_k // n_tm
-    side = lax.axis_index("path") % 2
+    side = my_side()
     z_ref[side] = mine_ref[...].astype(f32)
     z_ref[1 - side] = other_ref[...].astype(f32)
     value_one = sum(
         z_ref[1, :, width + r - half : width + r - half + 1] for r in range(VALUE_COPIES)
     )
-    z_low = jnp.concatenate([z_ref[0], z_ref[1]], axis=1)[:, :width].astype(bf16)
+    z_low = jnp.concatenate([z_ref[0], z_ref[1]], axis=1).astype(bf16)
+    z_cols = [z_low[:, c : c + LANES] for c in range(0, round_up(width, LANES), LANES)]
     level, start_t, first, share, coef = (rows_ref[r : r + 1, :] for r in range(5))
     at = lax.broadcasted_iota(i32, (steps_k, paths), 0)
 
+    later = lax.broadcasted_iota(i32, (steps_k, LANES), 0)
     total = jnp.zeros((steps_k, paths), f32)
     for i in range(steps_k - 1):
-        dots = dot(z_low, buf[i])
-        seen = (at > i) & (start_t <= float(i))
-        total = total + jnp.where(seen, dots, 0.0)
+        open_rows = (later > i).astype(f32).astype(bf16)
+        z_open = jnp.concatenate([z * open_rows for z in z_cols], axis=1)[:, :width]
+        total = total + dot(z_open, buf[i])
     estimate = value_one + jnp.sqrt(jnp.float32(step_len)) * total
     drift = estimate - estimate * estimate * estimate
     lvl = level.astype(i32)
@@ -191,15 +204,31 @@
     hot = start_hot(start_t, steps_k)
 
     def store(c, tile):
-        part, at = divmod(c * LANES, half)
-        part_ref[part, :, at : at + LANES] = tile
+        part_ref[:, c * LANES : (c + 1) * LANES] = tile
 
     weighted_sums(end_ref, store, hot, coef * second, share * second, width, split2)
     me = lax.axis_index("tm")
-    for away in range(n_tm):
-        rows = pl.ds(pl.multiple_of((me ^ away) * group, group), group)
-        out_mine[away] = part_ref[side, rows, :]
-        out_other[away] = part_ref[1 - side, rows, :]
+    for away, out_ref in enumerate(out_refs):
+        out_ref[...] = part_ref[pl.ds(pl.multiple_of((me ^ away) * group, group), group), :]
+
+
+def last_kernel(width, *refs):
+    *parts, value_ref, grad_ref, value_buf, grad_buf, sems = refs
+    total = pairwise([part[...] for part in parts])
+    group = total.shape[0]
+    grad_buf[...] = total[:, :width]
+    square = (group, group)
+    eye = lax.broadcasted_iota(i32, square, 0) == lax.broadcasted_iota(i32, square, 1)
+    column = jnp.broadcast_to(total[:, width : width + 1], square)
+    value_buf[...] = jnp.sum(jnp.where(eye, column, 0.0), axis=0, keepdims=True)
+    copies = [
+        pltpu.make_async_copy(grad_buf, grad_ref, sems.at[0]),
+        pltpu.make_async_copy(value_buf, value_ref, sems.at[1]),
+    ]
+    for copy in copies:
+        copy.start()
+    for copy in copies:
+        copy.wait()
 
 
 def params():
@@ -210,8 +239,14 @@
     return pltpu.with_memory_space_constraint(x, pltpu.HBM)
 
 
-def swap(x, axis, offset):
-    return lax.ppermute(x, axis, [(i, i ^ offset) for i in range(lax.axis_size(axis))])
+def swap(x, path_xor, tm_xor):
+    flip = path_xor * lax.axis_size("tm") + tm_xor
+    devices = lax.axis_size(("path", "tm"))
+    return lax.ppermute(x, ("path", "tm"), [(i, i ^ flip) for i in range(devices)])
+
+
+def my_side():
+    return lax.axis_index("path") & 1
 
 
 def add_kernel(*refs):
@@ -222,7 +257,7 @@
 def round_kernel(width, *refs):
     *parts, out_ref = refs
     total = pairwise([part[...] for part in parts])
-    first = lax.axis_index("path") % 2 * total.shape[1] - width
+    first = my_side() * total.shape[1] - width
     column = lax.broadcasted_iota(i32, total.shape, 1) + first
     high, middle, low = (part.astype(f32) for part in split3(total))
     out_ref[...] = jnp.where(column == 1, middle, jnp.where(column == 2, low, high)).astype(bf16)
@@ -241,21 +276,20 @@
         out_shape=jax.ShapeDtypeStruct(parts[0].shape, dtype),
         in_specs=[vmem] * len(parts),
         out_specs=vmem,
-        compiler_params=pltpu.CompilerParams(vmem_limit_bytes=4 * 1024 * 1024),
+        compiler_params=pltpu.CompilerParams(vmem_limit_bytes=SMALL_LIMIT),
     )(*parts)
 
 
-def terms(x, axis, first_bit):
-    ways = 4 if 2 * first_bit < lax.axis_size(axis) else 2
-    return [x] + [swap(x, axis, first_bit * away) for away in range(1, ways)]
-
-
-def steps_over(axis, first_bit):
-    bits = []
-    while first_bit < lax.axis_size(axis):
-        bits.append((axis, first_bit))
-        first_bit *= 4
-    return bits
+def path_steps(n_path):
+    steps, bit = [], 2
+    while bit < n_path:
+        steps.append((bit, 2 * bit, 3 * bit) if 2 * bit < n_path else (bit,))
+        bit *= 4
+    return steps
+
+
+def tm_steps(n_tm):
+    return [tuple(step // 2 for step in steps) for steps in path_steps(2 * n_tm)]
 
 
 def shards(n_path, n_tm, increments, level_table, time_table):
@@ -267,7 +301,6 @@
     vmem = pl.BlockSpec(memory_space=pltpu.VMEM)
     hbm = pl.BlockSpec(memory_space=pltpu.HBM)
     chunks = width // chunk_rows(width)
-    side = lax.axis_index("path") % 2
 
     mine, other, end, rows, held = pl.pallas_call(
         functools.partial(first_kernel, n_path, n_tm),
@@ -276,7 +309,7 @@
             jax.ShapeDtypeStruct((steps_k, half), f32),
             jax.ShapeDtypeStruct((full, paths), f32),
             jax.ShapeDtypeStruct((8, paths), f32),
-            pltpu.VMEM(inc.shape, bf16),
+            jax.ShapeDtypeStruct(inc.shape, bf16),
         ),
         in_specs=[hbm, hbm, hbm],
         out_specs=(vmem,) * 5,
@@ -284,6 +317,7 @@
             pltpu.VMEM((1, level_table.shape[0]), i32),
             pltpu.VMEM((1, time_table.shape[0]), i32),
             pltpu.VMEM((2, steps_k, half), f32),
+            pltpu.VMEM((steps_k, PACKED, paths), bf16),
             pltpu.SemaphoreType.DMA((chunks,)),
             pltpu.SemaphoreType.DMA((2,)),
         ],
@@ -291,30 +325,46 @@
         name="first_iterate",
     )(inc, *(in_hbm(table.reshape(1, -1)) for table in (level_table, time_table)))
 
-    parts = [mine, swap(other, "path", 1)]
-    for step in steps_over("path", 2) + steps_over("tm", 1):
-        parts = terms(local(add_kernel, f32, parts), *step)
+    parts = [mine, swap(other, 1, 0)]
+    hops = [[(flip, 0) for flip in step] for step in path_steps(n_path)]
+    hops += [[(0, flip) for flip in step] for step in tm_steps(n_tm)]
+    for step in hops:
+        total = local(add_kernel, f32, parts)
+        parts = [total] + [swap(total, *flips) for flips in step]
     own = local(functools.partial(round_kernel, width), bf16, parts)
 
-    mine, other = pl.pallas_call(
-        functools.partial(second_kernel, n_path, n_tm),
-        out_shape=(jax.ShapeDtypeStruct((n_tm, group, half), f32),) * 2,
+    parts = pl.pallas_call(
+        functools.partial(second_kernel, n_tm),
+        out_shape=(jax.ShapeDtypeStruct((group, full), f32),) * n_tm,
         in_specs=[vmem] * 5,
-        out_specs=(vmem, vmem),
-        scratch_shapes=[pltpu.VMEM((2, steps_k, half), f32)] * 2,
+        out_specs=(vmem,) * n_tm,
+        scratch_shapes=[pltpu.VMEM((2, steps_k, half), f32), pltpu.VMEM((steps_k, full), f32)],
         compiler_params=params(),
         name="second_iterate",
-    )(pltpu.with_memory_space_constraint(held, pltpu.VMEM), own, swap(own, "path", 1), end, rows)
-
-    part = mine + swap(other, "path", 1)
-    own = pairwise([part[0]] + [swap(part[away], "tm", away) for away in range(1, n_tm)])
-    for step in steps_over("path", 2):
-        own = pairwise(terms(own, *step))
-    other = swap(own, "path", 1)
-    total = jnp.concatenate(
-        [jnp.where(side == 0, own, other), jnp.where(side == 0, other, own)], axis=1
-    )
-    return total[:, width], total[:, :width]
+    )(held, own, swap(own, 1, 0), end, rows)
+
+    own = pairwise([parts[0]] + [swap(parts[away], 1, away) for away in range(1, n_tm)])
+    parts = [own, swap(own, 1, 0)]
+    for step in path_steps(n_path):
+        total = pairwise(parts)
+        parts = [total] + [swap(total, flip + 1, 0) for flip in step]
+    value, grad = pl.pallas_call(
+        functools.partial(last_kernel, width),
+        out_shape=(
+            jax.ShapeDtypeStruct((1, group), f32),
+            jax.ShapeDtypeStruct((group, width), f32),
+        ),
+        in_specs=[vmem] * len(parts),
+        out_specs=(hbm, hbm),
+        scratch_shapes=[
+            pltpu.VMEM((1, group), f32),
+            pltpu.VMEM((group, width), f32),
+            pltpu.SemaphoreType.DMA((2,)),
+        ],
+        compiler_params=pltpu.CompilerParams(vmem_limit_bytes=SMALL_LIMIT),
+        name="last_sum",
+    )(*parts)
+    return value.reshape(group), grad
 
 
 def solution(mesh):

time: 49.9 us -> 47.3 us (0.948)
  waiting for transfers between devices: 20.3 us -> 18.4 us
  local copies, waits for them, and re-layouts: 0.7 us -> 0 us
  other arithmetic: 0.65 us -> 0.01 us
  Pallas kernels: 10.4 us -> 10.9 us
    ppermute x16 -> x15, waiting for transfers between devices: 20.3 us -> 18.4 us  [swap(): lax.ppermute(x, ('path', 'tm'), [(i, i ^ flip) for i in range(devices)])]
    slice x1 -> x0, local copies, waits for them, and re-layouts: 0.7 us -> none  [shards(): return (total[:, width], total[:, :width])]
    concatenate x1 -> x0, other arithmetic: 0.62 us -> none  [shards(): jnp.concatenate([jnp.where(side == 0, own, other), jnp.where(side == 0, o...]
    pallas_call x1 -> x2, Pallas kernels: 3.46 us -> 3.98 us  [the longest x1 3.34 us: shards(): pl.pallas_call(functools.partial(second_kernel, n_tm), out_shape=(jax.Sha...]
    ppermute x16 -> x15, starting transfers between devices: 16.9 us -> 17.1 us  [swap(): lax.ppermute(x, ('path', 'tm'), [(i, i ^ flip) for i in range(devices)])]
  transfers between devices with their start and end apart: 16 -> 15, of which waited for: 15 -> 13; matrix products, arithmetic and copies ran while one was open for 0% -> 0% of each run, Pallas kernels for 0% -> 0%
where the time goes in v3:
time: 47.3 us; the launch traced here: 47.1 us
  waiting for transfers between devices  18.4 us (39%)
  starting transfers between devices  17.1 us (36%)
  Pallas kernels  10.9 us (23%)
  between operations  0.68 us (1%)
    ppermute x15, waiting for transfers between devices, swap(): lax.ppermute(x, ('path', 'tm'), [(i, i ^ flip) for i in range(devices)])  18.4 us
    ppermute x15, starting transfers between devices, swap(): lax.ppermute(x, ('path', 'tm'), [(i, i ^ flip) for i in range(devices)])  17.1 us
    pallas_call x1, Pallas kernels, shards(): pl.pallas_call(functools.partial(first_kernel, n_path, n_tm), out_shape=(...  6.88 us
    pallas_call x1, Pallas kernels, shards(): pl.pallas_call(functools.partial(second_kernel, n_tm), out_shape=(jax.Sha...  3.34 us
  transfers between devices with their start and end apart: 15, of which 13 were waited for; matrix products, arithmetic and copies ran while one was open for 0% of the time, Pallas kernels for 0%

profile of v3, /device:TPU:0, one launch (start us, length us, event | category | flops | bytes accessed | tf_op | source)
XLA Modules:
  0.0 47.1 jit_solution(8063733680780170940)
XLA Ops:
  0.6 6.9 %first_iterate.1 = (f32[32,512]{1,0:T(8,128)S(1)}, f32[32,512]{1,0:T(8,128)S(1)}, f32[1024,256]{1,0:T(8,128)S(1)}, f32[8,256]{1,0:T(8,128)S(1)}, bf16[32,1000,256]{2,1,0:T(8,128)(2,1)S(1)}) custom-call(bf16[32,1000,256]{2,1,0:T(8,128)(2,1)} %bitcast.4, s32[1,4096]{1,0:T(1,128)} %bitcast.5, s32[1,4096]{1,0:T(1,128)} %bitcast.6), custom_call_target="tpu_custom_call" | custom-call | tf_op jit(solution)/shard_map/first_iterate/pallas_call | solution.py:305
  7.5 0.6 %collective-permute-start = (f32[32,512]{1,0:T(8,128)S(1)}, f32[32,512]{1,0:T(8,128)S(1)}, u32[]{:S(2)}, u32[]{:S(2)}) collective-permute-start(f32[32,512]{1,0:T(8,128)S(1)} %get-tuple-element.15), channel_id=1, source_target_pairs={{0,4},{1,5},{2,6},{3,7},{4,0},{5,1},{6,2},{7,3},{8,12},{9,13},{10,... | collective-permute-start | bytes 196616 | tf_op jit(solution)/shard_map/ppermute | solution.py:245
  8.1 0.9 %collective-permute-done.refs_1_ = f32[32,512]{1,0:T(8,128)S(1)} collective-permute-done((f32[32,512]{1,0:T(8,128)S(1)}, f32[32,512]{1,0:T(8,128)S(1)}, u32[]{:S(2)}, u32[]{:S(2)}) %collective-permute-start) | collective-permute-done | bytes 65568 | tf_op jit(solution)/shard_map/ppermute | solution.py:245
  9.0 3.8 %collective-permute-start.3 = (f32[32,512]{1,0:T(8,128)S(1)}, f32[32,512]{1,0:T(8,128)S(1)}, u32[]{:S(2)}, u32[]{:S(2)}) collective-permute-start(f32[32,512]{1,0:T(8,128)S(1)} %shard_map.50.refs_0_), channel_id=1, source_target_pairs={{0,24},{1,25},{2,26},{3,27},{4,28},{5,29},{6,30},{7,31},{8,16},{9,... | collective-permute-start | bytes 196616 | tf_op jit(solution)/shard_map/ppermute | solution.py:245
  12.8 0.5 %collective-permute-start.2 = (f32[32,512]{1,0:T(8,128)S(1)}, f32[32,512]{1,0:T(8,128)S(1)}, u32[]{:S(2)}, u32[]{:S(2)}) collective-permute-start(f32[32,512]{1,0:T(8,128)S(1)} %shard_map.50.refs_0_), channel_id=1, source_target_pairs={{0,16},{1,17},{2,18},{3,19},{4,20},{5,21},{6,22},{7,23},{8,24},{9,... | collective-permute-start | bytes 196616 | tf_op jit(solution)/shard_map/ppermute | solution.py:245
  13.3 0.1 collective-permute-start.1
  13.5 1.8 %collective-permute-done.3.refs_3_ = f32[32,512]{1,0:T(8,128)S(1)} collective-permute-done((f32[32,512]{1,0:T(8,128)S(1)}, f32[32,512]{1,0:T(8,128)S(1)}, u32[]{:S(2)}, u32[]{:S(2)}) %collective-permute-start.3) | collective-permute-done | bytes 65568 | tf_op jit(solution)/shard_map/ppermute | solution.py:245
  15.3 1.9 %collective-permute-done.2.refs_2_ = f32[32,512]{1,0:T(8,128)S(1)} collective-permute-done((f32[32,512]{1,0:T(8,128)S(1)}, f32[32,512]{1,0:T(8,128)S(1)}, u32[]{:S(2)}, u32[]{:S(2)}) %collective-permute-start.2) | collective-permute-done | bytes 65568 | tf_op jit(solution)/shard_map/ppermute | solution.py:245
  17.1 0.5 %collective-permute-done.1.refs_1_ = f32[32,512]{1,0:T(8,128)S(1)} collective-permute-done((f32[32,512]{1,0:T(8,128)S(1)}, f32[32,512]{1,0:T(8,128)S(1)}, u32[]{:S(2)}, u32[]{:S(2)}) %collective-permute-start.1) | collective-permute-done | bytes 65568 | tf_op jit(solution)/shard_map/ppermute | solution.py:245
  17.6 3.7 %collective-permute-start.6 = (f32[32,512]{1,0:T(8,128)S(1)}, f32[32,512]{1,0:T(8,128)S(1)}, u32[]{:S(2)}, u32[]{:S(2)}) collective-permute-start(f32[32,512]{1,0:T(8,128)S(1)} %shard_map.51.refs_0_), channel_id=1, source_target_pairs={{0,3},{1,2},{2,1},{3,0},{4,7},{5,6},{6,5},{7,4},{8,11},{9,10},{10,... | collective-permute-start | bytes 196616 | tf_op jit(solution)/shard_map/ppermute | solution.py:245
  21.3 0.0 collective-permute-start.5
  21.3 0.8 %collective-permute-start.4 = (f32[32,512]{1,0:T(8,128)S(1)}, f32[32,512]{1,0:T(8,128)S(1)}, u32[]{:S(2)}, u32[]{:S(2)}) collective-permute-start(f32[32,512]{1,0:T(8,128)S(1)} %shard_map.51.refs_0_), channel_id=1, source_target_pairs={{0,1},{1,0},{2,3},{3,2},{4,5},{5,4},{6,7},{7,6},{8,9},{9,8},{10,11... | collective-permute-start | bytes 196616 | tf_op jit(solution)/shard_map/ppermute | solution.py:245
  22.1 1.7 %collective-permute-done.6.refs_3_ = f32[32,512]{1,0:T(8,128)S(1)} collective-permute-done((f32[32,512]{1,0:T(8,128)S(1)}, f32[32,512]{1,0:T(8,128)S(1)}, u32[]{:S(2)}, u32[]{:S(2)}) %collective-permute-start.6) | collective-permute-done | bytes 65568 | tf_op jit(solution)/shard_map/ppermute | solution.py:245
  23.8 2.7 %collective-permute-done.5.refs_2_ = f32[32,512]{1,0:T(8,128)S(1)} collective-permute-done((f32[32,512]{1,0:T(8,128)S(1)}, f32[32,512]{1,0:T(8,128)S(1)}, u32[]{:S(2)}, u32[]{:S(2)}) %collective-permute-start.5) | collective-permute-done | bytes 65568 | tf_op jit(solution)/shard_map/ppermute | solution.py:245
  26.5 0.0 collective-permute-done.4.refs_1_
  26.5 0.1 collective-permute-start.7
  26.6 1.2 %collective-permute-done.7.other_ref = bf16[32,512]{1,0:T(8,128)(2,1)S(1)} collective-permute-done((bf16[32,512]{1,0:T(8,128)(2,1)S(1)}, bf16[32,512]{1,0:T(8,128)(2,1)S(1)}, u32[]{:S(2)}, u32[]{:S(2)}) %collective-permute-start.7) | collective-permute-done | bytes 32800 | tf_op jit(solution)/shard_map/ppermute | solution.py:245
  27.8 3.3 %second_iterate.1 = (f32[8,1024]{1,0:T(8,128)S(1)}, f32[8,1024]{1,0:T(8,128)S(1)}, f32[8,1024]{1,0:T(8,128)S(1)}, f32[8,1024]{1,0:T(8,128)S(1)}) custom-call(bf16[32,1000,256]{2,1,0:T(8,128)(2,1)S(1)} %get-tuple-element.13.buf, bf16[32,512]{1,0:T(8,128)(2,1)S(1)} %shard_map.52.mine_ref, bf16[32,512]{1,0:T(8,128)(2,1)S(1)} %collective-permute-done.7.other_ref, ...), custom_call_target="tpu_custom_call" | custom-call | tf_op jit(solution)/shard_map/second_iterate/pallas_call | solution.py:336
  31.1 0.4 collective-permute-start.8
  31.5 1.9 %collective-permute-start.9 = (f32[8,1024]{1,0:T(8,128)S(1)}, f32[8,1024]{1,0:T(8,128)S(1)}, u32[]{:S(2)}, u32[]{:S(2)}) collective-permute-start(f32[8,1024]{1,0:T(8,128)S(1)} %get-tuple-element.20), channel_id=1, source_target_pairs={{0,6},{1,7},{2,4},{3,5},{4,2},{5,3},{6,0},{7,1},{8,14},{9,15},{10,... | collective-permute-start | bytes 98312 | tf_op jit(solution)/shard_map/ppermute | solution.py:245
  33.4 1.6 %collective-permute-start.10 = (f32[8,1024]{1,0:T(8,128)S(1)}, f32[8,1024]{1,0:T(8,128)S(1)}, u32[]{:S(2)}, u32[]{:S(2)}) collective-permute-start(f32[8,1024]{1,0:T(8,128)S(1)} %get-tuple-element.21), channel_id=1, source_target_pairs={{0,7},{1,6},{2,5},{3,4},{4,3},{5,2},{6,1},{7,0},{8,15},{9,14},{10,... | collective-permute-start | bytes 98312 | tf_op jit(solution)/shard_map/ppermute | solution.py:245
  35.1 0.0 collective-permute-done.8
  35.1 0.7 %collective-permute-done.9 = f32[8,1024]{1,0:T(8,128)S(1)} collective-permute-done((f32[8,1024]{1,0:T(8,128)S(1)}, f32[8,1024]{1,0:T(8,128)S(1)}, u32[]{:S(2)}, u32[]{:S(2)}) %collective-permute-start.9) | collective-permute-done | bytes 32800 | tf_op jit(solution)/shard_map/ppermute | solution.py:245
  35.7 2.8 %collective-permute-done.10 = f32[8,1024]{1,0:T(8,128)S(1)} collective-permute-done((f32[8,1024]{1,0:T(8,128)S(1)}, f32[8,1024]{1,0:T(8,128)S(1)}, u32[]{:S(2)}, u32[]{:S(2)}) %collective-permute-start.10) | collective-permute-done | bytes 32800 | tf_op jit(solution)/shard_map/ppermute | solution.py:245
  38.6 0.2 collective-permute-start.11
  38.8 1.0 %collective-permute-done.11 = f32[8,1024]{1,0:T(8,128)S(1)} collective-permute-done((f32[8,1024]{1,0:T(8,128)S(1)}, f32[8,1024]{1,0:T(8,128)S(1)}, u32[]{:S(2)}, u32[]{:S(2)}) %collective-permute-start.11) | collective-permute-done | bytes 32800 | tf_op jit(solution)/shard_map/ppermute | solution.py:245
  39.9 1.5 %collective-permute-start.14 = (f32[8,1024]{1,0:T(8,128)S(1)}, f32[8,1024]{1,0:T(8,128)S(1)}, u32[]{:S(2)}, u32[]{:S(2)}) collective-permute-start(f32[8,1024]{1,0:T(8,128)S(1)} %add.15.refs_0_), channel_id=1, source_target_pairs={{0,28},{1,29},{2,30},{3,31},{4,24},{5,25},{6,26},{7,27},{8,20},{9,... | collective-permute-start | bytes 98312 | tf_op jit(solution)/shard_map/ppermute | solution.py:245
  41.4 1.7 %collective-permute-start.13 = (f32[8,1024]{1,0:T(8,128)S(1)}, f32[8,1024]{1,0:T(8,128)S(1)}, u32[]{:S(2)}, u32[]{:S(2)}) collective-permute-start(f32[8,1024]{1,0:T(8,128)S(1)} %add.15.refs_0_), channel_id=1, source_target_pairs={{0,20},{1,21},{2,22},{3,23},{4,16},{5,17},{6,18},{7,19},{8,28},{9,... | collective-permute-start | bytes 98312 | tf_op jit(solution)/shard_map/ppermute | solution.py:245
  43.1 0.1 collective-permute-start.12
  43.2 0.9 %collective-permute-done.14.refs_3_ = f32[8,1024]{1,0:T(8,128)S(1)} collective-permute-done((f32[8,1024]{1,0:T(8,128)S(1)}, f32[8,1024]{1,0:T(8,128)S(1)}, u32[]{:S(2)}, u32[]{:S(2)}) %collective-permute-start.14) | collective-permute-done | bytes 32800 | tf_op jit(solution)/shard_map/ppermute | solution.py:245
  44.1 0.7 %collective-permute-done.13.refs_2_ = f32[8,1024]{1,0:T(8,128)S(1)} collective-permute-done((f32[8,1024]{1,0:T(8,128)S(1)}, f32[8,1024]{1,0:T(8,128)S(1)}, u32[]{:S(2)}, u32[]{:S(2)}) %collective-permute-start.13) | collective-permute-done | bytes 32800 | tf_op jit(solution)/shard_map/ppermute | solution.py:245
  44.8 1.6 %collective-permute-done.12.refs_1_ = f32[8,1024]{1,0:T(8,128)S(1)} collective-permute-done((f32[8,1024]{1,0:T(8,128)S(1)}, f32[8,1024]{1,0:T(8,128)S(1)}, u32[]{:S(2)}, u32[]{:S(2)}) %collective-permute-start.12) | collective-permute-done | bytes 32800 | tf_op jit(solution)/shard_map/ppermute | solution.py:245
  46.4 0.6 %last_sum.1 = (f32[1,8]{1,0:T(1,128)}, f32[8,1000]{1,0:T(8,128)}) custom-call(f32[8,1024]{1,0:T(8,128)S(1)} %add.15.refs_0_, f32[8,1024]{1,0:T(8,128)S(1)} %collective-permute-done.12.refs_1_, f32[8,1024]{1,0:T(8,128)S(1)} %collective-permute-done.13.refs_2_, f32[8,1024]{1,0:T(8,128)S(1)} %collective-permute-done.14.refs_3_), custom_call_target="tpu_custom_call" | custom-call | tf_op jit(solution)/shard_map/last_sum/pallas_call | solution.py:351
  (5 shorter events, 0.1 us)
Async XLA Ops:
  7.5 1.5 %collective-permute-start = (f32[32,512]{1,0:T(8,128)S(1)}, f32[32,512]{1,0:T(8,128)S(1)}, u32[]{:S(2)}, u32[]{:S(2)}) collective-permute-start(f32[32,512]{1,0:T(8,128)S(1)} %get-tuple-element.15), channel_id=1, source_target_pairs={{0,4},{1,5},{2,6},{3,7},{4,0},{5,1},{6,2},{7,3},{8,12},{9,13},{10,... | collective-permute-start | bytes 196616 | tf_op jit(solution)/shard_map/ppermute | solution.py:245
  9.0 6.3 %collective-permute-start.3 = (f32[32,512]{1,0:T(8,128)S(1)}, f32[32,512]{1,0:T(8,128)S(1)}, u32[]{:S(2)}, u32[]{:S(2)}) collective-permute-start(f32[32,512]{1,0:T(8,128)S(1)} %shard_map.50.refs_0_), channel_id=1, source_target_pairs={{0,24},{1,25},{2,26},{3,27},{4,28},{5,29},{6,30},{7,31},{8,16},{9,... | collective-permute-start | bytes 196616 | tf_op jit(solution)/shard_map/ppermute | solution.py:245
  12.8 4.3 %collective-permute-start.2 = (f32[32,512]{1,0:T(8,128)S(1)}, f32[32,512]{1,0:T(8,128)S(1)}, u32[]{:S(2)}, u32[]{:S(2)}) collective-permute-start(f32[32,512]{1,0:T(8,128)S(1)} %shard_map.50.refs_0_), channel_id=1, source_target_pairs={{0,16},{1,17},{2,18},{3,19},{4,20},{5,21},{6,22},{7,23},{8,24},{9,... | collective-permute-start | bytes 196616 | tf_op jit(solution)/shard_map/ppermute | solution.py:245
  13.3 4.3 %collective-permute-start.1 = (f32[32,512]{1,0:T(8,128)S(1)}, f32[32,512]{1,0:T(8,128)S(1)}, u32[]{:S(2)}, u32[]{:S(2)}) collective-permute-start(f32[32,512]{1,0:T(8,128)S(1)} %shard_map.50.refs_0_), channel_id=1, source_target_pairs={{0,8},{1,9},{2,10},{3,11},{4,12},{5,13},{6,14},{7,15},{8,0},{9,1},... | collective-permute-start | bytes 196616 | tf_op jit(solution)/shard_map/ppermute | solution.py:245
  17.6 6.1 %collective-permute-start.6 = (f32[32,512]{1,0:T(8,128)S(1)}, f32[32,512]{1,0:T(8,128)S(1)}, u32[]{:S(2)}, u32[]{:S(2)}) collective-permute-start(f32[32,512]{1,0:T(8,128)S(1)} %shard_map.51.refs_0_), channel_id=1, source_target_pairs={{0,3},{1,2},{2,1},{3,0},{4,7},{5,6},{6,5},{7,4},{8,11},{9,10},{10,... | collective-permute-start | bytes 196616 | tf_op jit(solution)/shard_map/ppermute | solution.py:245
  21.3 5.2 %collective-permute-start.5 = (f32[32,512]{1,0:T(8,128)S(1)}, f32[32,512]{1,0:T(8,128)S(1)}, u32[]{:S(2)}, u32[]{:S(2)}) collective-permute-start(f32[32,512]{1,0:T(8,128)S(1)} %shard_map.51.refs_0_), channel_id=1, source_target_pairs={{0,2},{1,3},{2,0},{3,1},{4,6},{5,7},{6,4},{7,5},{8,10},{9,11},{10,... | collective-permute-start | bytes 196616 | tf_op jit(solution)/shard_map/ppermute | solution.py:245
  21.3 5.2 %collective-permute-start.4 = (f32[32,512]{1,0:T(8,128)S(1)}, f32[32,512]{1,0:T(8,128)S(1)}, u32[]{:S(2)}, u32[]{:S(2)}) collective-permute-start(f32[32,512]{1,0:T(8,128)S(1)} %shard_map.51.refs_0_), channel_id=1, source_target_pairs={{0,1},{1,0},{2,3},{3,2},{4,5},{5,4},{6,7},{7,6},{8,9},{9,8},{10,11... | collective-permute-start | bytes 196616 | tf_op jit(solution)/shard_map/ppermute | solution.py:245
  26.5 1.3 %collective-permute-start.7 = (bf16[32,512]{1,0:T(8,128)(2,1)S(1)}, bf16[32,512]{1,0:T(8,128)(2,1)S(1)}, u32[]{:S(2)}, u32[]{:S(2)}) collective-permute-start(bf16[32,512]{1,0:T(8,128)(2,1)S(1)} %shard_map.52.mine_ref), channel_id=1, source_target_pairs={{0,4},{1,5},{2,6},{3,7},{4,0},{5,1},{6,2},{7,3},{8,12},{9,13},{10,... | collective-permute-start | bytes 98312 | tf_op jit(solution)/shard_map/ppermute | solution.py:245
  31.1 3.9 %collective-permute-start.8 = (f32[8,1024]{1,0:T(8,128)S(1)}, f32[8,1024]{1,0:T(8,128)S(1)}, u32[]{:S(2)}, u32[]{:S(2)}) collective-permute-start(f32[8,1024]{1,0:T(8,128)S(1)} %get-tuple-element.19), channel_id=1, source_target_pairs={{0,5},{1,4},{2,7},{3,6},{4,1},{5,0},{6,3},{7,2},{8,13},{9,12},{10,... | collective-permute-start | bytes 98312 | tf_op jit(solution)/shard_map/ppermute | solution.py:245
  31.5 4.2 %collective-permute-start.9 = (f32[8,1024]{1,0:T(8,128)S(1)}, f32[8,1024]{1,0:T(8,128)S(1)}, u32[]{:S(2)}, u32[]{:S(2)}) collective-permute-start(f32[8,1024]{1,0:T(8,128)S(1)} %get-tuple-element.20), channel_id=1, source_target_pairs={{0,6},{1,7},{2,4},{3,5},{4,2},{5,3},{6,0},{7,1},{8,14},{9,15},{10,... | collective-permute-start | bytes 98312 | tf_op jit(solution)/shard_map/ppermute | solution.py:245
  33.4 5.1 %collective-permute-start.10 = (f32[8,1024]{1,0:T(8,128)S(1)}, f32[8,1024]{1,0:T(8,128)S(1)}, u32[]{:S(2)}, u32[]{:S(2)}) collective-permute-start(f32[8,1024]{1,0:T(8,128)S(1)} %get-tuple-element.21), channel_id=1, source_target_pairs={{0,7},{1,6},{2,5},{3,4},{4,3},{5,2},{6,1},{7,0},{8,15},{9,14},{10,... | collective-permute-start | bytes 98312 | tf_op jit(solution)/shard_map/ppermute | solution.py:245
  38.6 1.3 %collective-permute-start.11 = (f32[8,1024]{1,0:T(8,128)S(1)}, f32[8,1024]{1,0:T(8,128)S(1)}, u32[]{:S(2)}, u32[]{:S(2)}) collective-permute-start(f32[8,1024]{1,0:T(8,128)S(1)} %add_add_fusion), channel_id=1, source_target_pairs={{0,4},{1,5},{2,6},{3,7},{4,0},{5,1},{6,2},{7,3},{8,12},{9,13},{10,... | collective-permute-start | bytes 98312 | tf_op jit(solution)/shard_map/ppermute | solution.py:245
  39.9 4.2 %collective-permute-start.14 = (f32[8,1024]{1,0:T(8,128)S(1)}, f32[8,1024]{1,0:T(8,128)S(1)}, u32[]{:S(2)}, u32[]{:S(2)}) collective-permute-start(f32[8,1024]{1,0:T(8,128)S(1)} %add.15.refs_0_), channel_id=1, source_target_pairs={{0,28},{1,29},{2,30},{3,31},{4,24},{5,25},{6,26},{7,27},{8,20},{9,... | collective-permute-start | bytes 98312 | tf_op jit(solution)/shard_map/ppermute | solution.py:245
  41.4 3.5 %collective-permute-start.13 = (f32[8,1024]{1,0:T(8,128)S(1)}, f32[8,1024]{1,0:T(8,128)S(1)}, u32[]{:S(2)}, u32[]{:S(2)}) collective-permute-start(f32[8,1024]{1,0:T(8,128)S(1)} %add.15.refs_0_), channel_id=1, source_target_pairs={{0,20},{1,21},{2,22},{3,23},{4,16},{5,17},{6,18},{7,19},{8,28},{9,... | collective-permute-start | bytes 98312 | tf_op jit(solution)/shard_map/ppermute | solution.py:245
  43.1 3.3 %collective-permute-start.12 = (f32[8,1024]{1,0:T(8,128)S(1)}, f32[8,1024]{1,0:T(8,128)S(1)}, u32[]{:S(2)}, u32[]{:S(2)}) collective-permute-start(f32[8,1024]{1,0:T(8,128)S(1)} %add.15.refs_0_), channel_id=1, source_target_pairs={{0,12},{1,13},{2,14},{3,15},{4,8},{5,9},{6,10},{7,11},{8,4},{9,5},... | collective-permute-start | bytes 98312 | tf_op jit(solution)/shard_map/ppermute | solution.py:245

commit v4 on v3

--- a/solution.py
+++ b/solution.py
@@ -167,31 +167,52 @@
     other_ref[...] = part_ref[1 - side]
 
 
+def dots_over(z_half, buf, begin, end):
+    steps_k, paths = buf.shape[0], buf.shape[2]
+    later = lax.broadcasted_iota(i32, (steps_k, LANES), 0)
+    total = jnp.zeros((steps_k, paths), f32)
+    for i in range(steps_k - 1):
+        open_rows = (later > i).astype(f32).astype(bf16)
+        z_open = [
+            z_half[:, c : c + LANES] * open_rows for c in range(0, z_half.shape[1], LANES)
+        ]
+        z_open = jnp.concatenate(z_open, axis=1)[:, : end - begin]
+        total = total + dot(z_open, buf[i, begin:end, :])
+    return total
+
+
+def half_dots(z_half, side, buf, total_ref):
+    width, half = buf.shape[1], z_half.shape[1]
+    for which, begin, end in ((0, 0, min(half, width)), (1, half, width)):
+
+        @pl.when(side == which)
+        def _(begin=begin, end=end):
+            total_ref[...] = dots_over(z_half, buf, begin, end)
+
+
+def own_half_kernel(buf, z_ref, total_ref):
+    half_dots(z_ref[...], my_side(), buf, total_ref)
+
+
 def second_kernel(
-    n_tm, buf, mine_ref, other_ref, end_ref, rows_ref, *refs
+    n_tm, buf, mine_ref, other_ref, total_ref, end_ref, rows_ref, *refs
 ):
-    *out_refs, z_ref, part_ref = refs
+    *out_refs, z_ref, part_ref, rest_ref = refs
     steps_k, width, paths = buf.shape
     step_len = horizon / steps_k
     half = mine_ref.shape[1]
     group = steps_k // n_tm
     side = my_side()
+    half_dots(other_ref[...], 1 - side, buf, rest_ref)
     z_ref[side] = mine_ref[...].astype(f32)
     z_ref[1 - side] = other_ref[...].astype(f32)
     value_one = sum(
         z_ref[1, :, width + r - half : width + r - half + 1] for r in range(VALUE_COPIES)
     )
-    z_low = jnp.concatenate([z_ref[0], z_ref[1]], axis=1).astype(bf16)
-    z_cols = [z_low[:, c : c + LANES] for c in range(0, round_up(width, LANES), LANES)]
     level, start_t, first, share, coef = (rows_ref[r : r + 1, :] for r in range(5))
     at = lax.broadcasted_iota(i32, (steps_k, paths), 0)
 
-    later = lax.broadcasted_iota(i32, (steps_k, LANES), 0)
-    total = jnp.zeros((steps_k, paths), f32)
-    for i in range(steps_k - 1):
-        open_rows = (later > i).astype(f32).astype(bf16)
-        z_open = jnp.concatenate([z * open_rows for z in z_cols], axis=1)[:, :width]
-        total = total + dot(z_open, buf[i])
+    total = total_ref[...] + rest_ref[...]
     estimate = value_one + jnp.sqrt(jnp.float32(step_len)) * total
     drift = estimate - estimate * estimate * estimate
     lvl = level.astype(i32)
@@ -239,10 +260,13 @@
     return pltpu.with_memory_space_constraint(x, pltpu.HBM)
 
 
-def swap(x, path_xor, tm_xor):
-    flip = path_xor * lax.axis_size("tm") + tm_xor
-    devices = lax.axis_size(("path", "tm"))
-    return lax.ppermute(x, ("path", "tm"), [(i, i ^ flip) for i in range(devices)])
+def swap(x, flips, odd_flips=None):
+    n_tm = lax.axis_size("tm")
+    even, odd = (path * n_tm + tm for path, tm in (flips, odd_flips or flips))
+    pairs = [
+        (i, i ^ (odd if i // n_tm % 2 else even)) for i in range(lax.axis_size(("path", "tm")))
+    ]
+    return lax.ppermute(x, ("path", "tm"), pairs)
 
 
 def my_side():
@@ -325,29 +349,48 @@
         name="first_iterate",
     )(inc, *(in_hbm(table.reshape(1, -1)) for table in (level_table, time_table)))
 
-    parts = [mine, swap(other, 1, 0)]
-    hops = [[(flip, 0) for flip in step] for step in path_steps(n_path)]
-    hops += [[(0, flip) for flip in step] for step in tm_steps(n_tm)]
-    for step in hops:
+    parts = [mine, swap(other, (1, 0))]
+    over_path = [[(flip, 0) for flip in step] for step in path_steps(n_path)]
+    over_tm = [[(0, flip) for flip in step] for step in tm_steps(n_tm)]
+    odd, even = over_tm + over_path, over_path + over_tm
+    if [len(step) for step in even] != [len(step) for step in odd]:
+        odd = even
+    for even_step, odd_step in zip(even, odd):
         total = local(add_kernel, f32, parts)
-        parts = [total] + [swap(total, *flips) for flips in step]
+        parts = [total] + [swap(total, *flips) for flips in zip(even_step, odd_step)]
     own = local(functools.partial(round_kernel, width), bf16, parts)
 
+    other = swap(own, (1, 0))
+    total = pl.pallas_call(
+        own_half_kernel,
+        out_shape=jax.ShapeDtypeStruct((steps_k, paths), f32),
+        in_specs=[vmem] * 2,
+        out_specs=vmem,
+        compiler_params=params(),
+        cost_estimate=pl.CostEstimate(
+            flops=paths * steps_k * steps_k * width, bytes_accessed=0, transcendentals=0
+        ),
+        name="own_half",
+    )(held, own)
     parts = pl.pallas_call(
         functools.partial(second_kernel, n_tm),
         out_shape=(jax.ShapeDtypeStruct((group, full), f32),) * n_tm,
-        in_specs=[vmem] * 5,
+        in_specs=[vmem] * 6,
         out_specs=(vmem,) * n_tm,
-        scratch_shapes=[pltpu.VMEM((2, steps_k, half), f32), pltpu.VMEM((steps_k, full), f32)],
+        scratch_shapes=[
+            pltpu.VMEM((2, steps_k, half), f32),
+            pltpu.VMEM((steps_k, full), f32),
+            pltpu.VMEM((steps_k, paths), f32),
+        ],
         compiler_params=params(),
         name="second_iterate",
-    )(held, own, swap(own, 1, 0), end, rows)
-
-    own = pairwise([parts[0]] + [swap(parts[away], 1, away) for away in range(1, n_tm)])
-    parts = [own, swap(own, 1, 0)]
+    )(held, own, other, total, end, rows)
+
+    own = pairwise([parts[0]] + [swap(parts[away], (1, away)) for away in range(1, n_tm)])
+    parts = [own, swap(own, (1, 0))]
     for step in path_steps(n_path):
         total = pairwise(parts)
-        parts = [total] + [swap(total, flip + 1, 0) for flip in step]
+        parts = [total] + [swap(total, (flip + 1, 0)) for flip in step]
     value, grad = pl.pallas_call(
         functools.partial(last_kernel, width),
         out_shape=(

time: 47.3 us -> 44.8 us (0.947)
  waiting for transfers between devices: 18.4 us -> 15.8 us
    ppermute x15, waiting for transfers between devices: 18.4 us -> 15.8 us  [swap(): return lax.ppermute(x, ('path', 'tm'), pairs)]
    pallas_call x0 -> x1, Pallas kernels: none -> 1.49 us  [shards(): pl.pallas_call(own_half_kernel, out_shape=jax.ShapeDtypeStruct((steps_k,...]
    pallas_call x1, Pallas kernels: 3.34 us -> 1.93 us  [shards(): pl.pallas_call(functools.partial(second_kernel, n_tm), out_shape=(jax.Sha...]
  transfers between devices with their start and end apart: 15 -> 15, of which waited for: 13 -> 11; matrix products, arithmetic and copies ran while one was open for 0% -> 0% of each run, Pallas kernels for 0% -> 3%
where the time goes in v4:
time: 44.8 us; the launch traced here: 44.6 us
  starting transfers between devices  17.1 us (38%)
  waiting for transfers between devices  15.8 us (35%)
  Pallas kernels  11 us (25%)
  between operations  0.69 us (2%)
    ppermute x15, starting transfers between devices, swap(): return lax.ppermute(x, ('path', 'tm'), pairs)  17.1 us
    ppermute x15, waiting for transfers between devices, swap(): return lax.ppermute(x, ('path', 'tm'), pairs)  15.8 us
    pallas_call x1, Pallas kernels, shards(): pl.pallas_call(functools.partial(first_kernel, n_path, n_tm), out_shape=(...  6.88 us
    pallas_call x1, Pallas kernels, shards(): pl.pallas_call(functools.partial(second_kernel, n_tm), out_shape=(jax.Sha...  1.93 us
    pallas_call x1, Pallas kernels, shards(): pl.pallas_call(own_half_kernel, out_shape=jax.ShapeDtypeStruct((steps_k,...  1.49 us
  transfers between devices with their start and end apart: 15, of which 11 were waited for; matrix products, arithmetic and copies ran while one was open for 0% of the time, Pallas kernels for 3%

profile of v4, /device:TPU:0, one launch (start us, length us, event | category | flops | bytes accessed | tf_op | source)
XLA Modules:
  0.0 44.6 jit_solution(4280373615247855905)
XLA Ops:
  0.6 6.9 %first_iterate.1 = (f32[32,512]{1,0:T(8,128)S(1)}, f32[32,512]{1,0:T(8,128)S(1)}, f32[1024,256]{1,0:T(8,128)S(1)}, f32[8,256]{1,0:T(8,128)S(1)}, bf16[32,1000,256]{2,1,0:T(8,128)(2,1)S(1)}) custom-call(bf16[32,1000,256]{2,1,0:T(8,128)(2,1)} %bitcast.4, s32[1,4096]{1,0:T(1,128)} %bitcast.5, s32[1,4096]{1,0:T(1,128)} %bitcast.6), custom_call_target="tpu_custom_call" | custom-call | tf_op jit(solution)/shard_map/first_iterate/pallas_call | solution.py:329
  7.5 0.6 %collective-permute-start = (f32[32,512]{1,0:T(8,128)S(1)}, f32[32,512]{1,0:T(8,128)S(1)}, u32[]{:S(2)}, u32[]{:S(2)}) collective-permute-start(f32[32,512]{1,0:T(8,128)S(1)} %get-tuple-element.15), channel_id=1, source_target_pairs={{0,4},{1,5},{2,6},{3,7},{4,0},{5,1},{6,2},{7,3},{8,12},{9,13},{10,... | collective-permute-start | bytes 196616 | tf_op jit(solution)/shard_map/ppermute | solution.py:269
  8.1 0.9 %collective-permute-done.refs_1_ = f32[32,512]{1,0:T(8,128)S(1)} collective-permute-done((f32[32,512]{1,0:T(8,128)S(1)}, f32[32,512]{1,0:T(8,128)S(1)}, u32[]{:S(2)}, u32[]{:S(2)}) %collective-permute-start) | collective-permute-done | bytes 65568 | tf_op jit(solution)/shard_map/ppermute | solution.py:269
  9.0 3.8 %collective-permute-start.3 = (f32[32,512]{1,0:T(8,128)S(1)}, f32[32,512]{1,0:T(8,128)S(1)}, u32[]{:S(2)}, u32[]{:S(2)}) collective-permute-start(f32[32,512]{1,0:T(8,128)S(1)} %shard_map.50.refs_0_), channel_id=1, source_target_pairs={{0,24},{1,25},{2,26},{3,27},{4,7},{5,6},{6,5},{7,4},{8,16},{9,17},... | collective-permute-start | bytes 196616 | tf_op jit(solution)/shard_map/ppermute | solution.py:269
  12.8 0.5 %collective-permute-start.2 = (f32[32,512]{1,0:T(8,128)S(1)}, f32[32,512]{1,0:T(8,128)S(1)}, u32[]{:S(2)}, u32[]{:S(2)}) collective-permute-start(f32[32,512]{1,0:T(8,128)S(1)} %shard_map.50.refs_0_), channel_id=1, source_target_pairs={{0,16},{1,17},{2,18},{3,19},{4,6},{5,7},{6,4},{7,5},{8,24},{9,25},... | collective-permute-start | bytes 196616 | tf_op jit(solution)/shard_map/ppermute | solution.py:269
  13.3 0.1 collective-permute-start.1
  13.5 1.6 %collective-permute-done.3.refs_3_ = f32[32,512]{1,0:T(8,128)S(1)} collective-permute-done((f32[32,512]{1,0:T(8,128)S(1)}, f32[32,512]{1,0:T(8,128)S(1)}, u32[]{:S(2)}, u32[]{:S(2)}) %collective-permute-start.3) | collective-permute-done | bytes 65568 | tf_op jit(solution)/shard_map/ppermute | solution.py:269
  15.1 2.0 %collective-permute-done.2.refs_2_ = f32[32,512]{1,0:T(8,128)S(1)} collective-permute-done((f32[32,512]{1,0:T(8,128)S(1)}, f32[32,512]{1,0:T(8,128)S(1)}, u32[]{:S(2)}, u32[]{:S(2)}) %collective-permute-start.2) | collective-permute-done | bytes 65568 | tf_op jit(solution)/shard_map/ppermute | solution.py:269
  17.1 0.5 %collective-permute-done.1.refs_1_ = f32[32,512]{1,0:T(8,128)S(1)} collective-permute-done((f32[32,512]{1,0:T(8,128)S(1)}, f32[32,512]{1,0:T(8,128)S(1)}, u32[]{:S(2)}, u32[]{:S(2)}) %collective-permute-start.1) | collective-permute-done | bytes 65568 | tf_op jit(solution)/shard_map/ppermute | solution.py:269
  17.6 3.7 %collective-permute-start.6 = (f32[32,512]{1,0:T(8,128)S(1)}, f32[32,512]{1,0:T(8,128)S(1)}, u32[]{:S(2)}, u32[]{:S(2)}) collective-permute-start(f32[32,512]{1,0:T(8,128)S(1)} %shard_map.51.refs_0_), channel_id=1, source_target_pairs={{0,3},{1,2},{2,1},{3,0},{4,28},{5,29},{6,30},{7,31},{8,11},{9,10},... | collective-permute-start | bytes 196616 | tf_op jit(solution)/shard_map/ppermute | solution.py:269
  21.3 0.0 collective-permute-start.5
  21.3 0.8 %collective-permute-start.4 = (f32[32,512]{1,0:T(8,128)S(1)}, f32[32,512]{1,0:T(8,128)S(1)}, u32[]{:S(2)}, u32[]{:S(2)}) collective-permute-start(f32[32,512]{1,0:T(8,128)S(1)} %shard_map.51.refs_0_), channel_id=1, source_target_pairs={{0,1},{1,0},{2,3},{3,2},{4,12},{5,13},{6,14},{7,15},{8,9},{9,8},{1... | collective-permute-start | bytes 196616 | tf_op jit(solution)/shard_map/ppermute | solution.py:269
  22.1 1.7 %collective-permute-done.6.refs_3_ = f32[32,512]{1,0:T(8,128)S(1)} collective-permute-done((f32[32,512]{1,0:T(8,128)S(1)}, f32[32,512]{1,0:T(8,128)S(1)}, u32[]{:S(2)}, u32[]{:S(2)}) %collective-permute-start.6) | collective-permute-done | bytes 65568 | tf_op jit(solution)/shard_map/ppermute | solution.py:269
  23.8 2.7 %collective-permute-done.5.refs_2_ = f32[32,512]{1,0:T(8,128)S(1)} collective-permute-done((f32[32,512]{1,0:T(8,128)S(1)}, f32[32,512]{1,0:T(8,128)S(1)}, u32[]{:S(2)}, u32[]{:S(2)}) %collective-permute-start.5) | collective-permute-done | bytes 65568 | tf_op jit(solution)/shard_map/ppermute | solution.py:269
  26.5 0.0 collective-permute-done.4.refs_1_
  26.5 0.1 collective-permute-start.7
  26.6 1.5 %own_half.1.total_ref = f32[32,256]{1,0:T(8,128)S(1)} custom-call(bf16[32,1000,256]{2,1,0:T(8,128)(2,1)S(1)} %get-tuple-element.13.buf, bf16[32,512]{1,0:T(8,128)(2,1)S(1)} %shard_map.52.z_ref.mine_ref), custom_call_target="tpu_custom_call" | custom-call | flops 262144000 | tf_op jit(solution)/shard_map/own_half/pallas_call | solution.py:364
  28.1 0.0 collective-permute-done.7.other_ref
  28.1 1.9 %second_iterate.1 = (f32[8,1024]{1,0:T(8,128)S(1)}, f32[8,1024]{1,0:T(8,128)S(1)}, f32[8,1024]{1,0:T(8,128)S(1)}, f32[8,1024]{1,0:T(8,128)S(1)}) custom-call(bf16[32,1000,256]{2,1,0:T(8,128)(2,1)S(1)} %get-tuple-element.13.buf, bf16[32,512]{1,0:T(8,128)(2,1)S(1)} %shard_map.52.z_ref.mine_ref, bf16[32,512]{1,0:T(8,128)(2,1)S(1)} %collective-permute-done.7.other_ref, ...), custom_call_target="tpu_custom_call" | custom-call | tf_op jit(solution)/shard_map/second_iterate/pallas_call | solution.py:375
  30.0 0.7 %collective-permute-start.8 = (f32[8,1024]{1,0:T(8,128)S(1)}, f32[8,1024]{1,0:T(8,128)S(1)}, u32[]{:S(2)}, u32[]{:S(2)}) collective-permute-start(f32[8,1024]{1,0:T(8,128)S(1)} %get-tuple-element.19), channel_id=1, source_target_pairs={{0,5},{1,4},{2,7},{3,6},{4,1},{5,0},{6,3},{7,2},{8,13},{9,12},{10,... | collective-permute-start | bytes 98312 | tf_op jit(solution)/shard_map/ppermute | solution.py:269
  30.7 1.6 %collective-permute-start.9 = (f32[8,1024]{1,0:T(8,128)S(1)}, f32[8,1024]{1,0:T(8,128)S(1)}, u32[]{:S(2)}, u32[]{:S(2)}) collective-permute-start(f32[8,1024]{1,0:T(8,128)S(1)} %get-tuple-element.20), channel_id=1, source_target_pairs={{0,6},{1,7},{2,4},{3,5},{4,2},{5,3},{6,0},{7,1},{8,14},{9,15},{10,... | collective-permute-start | bytes 98312 | tf_op jit(solution)/shard_map/ppermute | solution.py:269
  32.3 2.0 %collective-permute-start.10 = (f32[8,1024]{1,0:T(8,128)S(1)}, f32[8,1024]{1,0:T(8,128)S(1)}, u32[]{:S(2)}, u32[]{:S(2)}) collective-permute-start(f32[8,1024]{1,0:T(8,128)S(1)} %get-tuple-element.21), channel_id=1, source_target_pairs={{0,7},{1,6},{2,5},{3,4},{4,3},{5,2},{6,1},{7,0},{8,15},{9,14},{10,... | collective-permute-start | bytes 98312 | tf_op jit(solution)/shard_map/ppermute | solution.py:269
  34.3 0.0 collective-permute-done.8
  34.3 0.8 %collective-permute-done.9 = f32[8,1024]{1,0:T(8,128)S(1)} collective-permute-done((f32[8,1024]{1,0:T(8,128)S(1)}, f32[8,1024]{1,0:T(8,128)S(1)}, u32[]{:S(2)}, u32[]{:S(2)}) %collective-permute-start.9) | collective-permute-done | bytes 32800 | tf_op jit(solution)/shard_map/ppermute | solution.py:269
  35.1 2.4 %collective-permute-done.10 = f32[8,1024]{1,0:T(8,128)S(1)} collective-permute-done((f32[8,1024]{1,0:T(8,128)S(1)}, f32[8,1024]{1,0:T(8,128)S(1)}, u32[]{:S(2)}, u32[]{:S(2)}) %collective-permute-start.10) | collective-permute-done | bytes 32800 | tf_op jit(solution)/shard_map/ppermute | solution.py:269
  37.5 0.2 collective-permute-start.11
  37.8 1.0 %collective-permute-done.11 = f32[8,1024]{1,0:T(8,128)S(1)} collective-permute-done((f32[8,1024]{1,0:T(8,128)S(1)}, f32[8,1024]{1,0:T(8,128)S(1)}, u32[]{:S(2)}, u32[]{:S(2)}) %collective-permute-start.11) | collective-permute-done | bytes 32800 | tf_op jit(solution)/shard_map/ppermute | solution.py:269
  38.8 1.3 %collective-permute-start.14 = (f32[8,1024]{1,0:T(8,128)S(1)}, f32[8,1024]{1,0:T(8,128)S(1)}, u32[]{:S(2)}, u32[]{:S(2)}) collective-permute-start(f32[8,1024]{1,0:T(8,128)S(1)} %add.15.refs_0_), channel_id=1, source_target_pairs={{0,28},{1,29},{2,30},{3,31},{4,24},{5,25},{6,26},{7,27},{8,20},{9,... | collective-permute-start | bytes 98312 | tf_op jit(solution)/shard_map/ppermute | solution.py:269
  40.1 0.4 %collective-permute-start.13 = (f32[8,1024]{1,0:T(8,128)S(1)}, f32[8,1024]{1,0:T(8,128)S(1)}, u32[]{:S(2)}, u32[]{:S(2)}) collective-permute-start(f32[8,1024]{1,0:T(8,128)S(1)} %add.15.refs_0_), channel_id=1, source_target_pairs={{0,20},{1,21},{2,22},{3,23},{4,16},{5,17},{6,18},{7,19},{8,28},{9,... | collective-permute-start | bytes 98312 | tf_op jit(solution)/shard_map/ppermute | solution.py:269
  40.5 1.3 %collective-permute-start.12 = (f32[8,1024]{1,0:T(8,128)S(1)}, f32[8,1024]{1,0:T(8,128)S(1)}, u32[]{:S(2)}, u32[]{:S(2)}) collective-permute-start(f32[8,1024]{1,0:T(8,128)S(1)} %add.15.refs_0_), channel_id=1, source_target_pairs={{0,12},{1,13},{2,14},{3,15},{4,8},{5,9},{6,10},{7,11},{8,4},{9,5},... | collective-permute-start | bytes 98312 | tf_op jit(solution)/shard_map/ppermute | solution.py:269
  41.8 1.3 %collective-permute-done.14.refs_3_ = f32[8,1024]{1,0:T(8,128)S(1)} collective-permute-done((f32[8,1024]{1,0:T(8,128)S(1)}, f32[8,1024]{1,0:T(8,128)S(1)}, u32[]{:S(2)}, u32[]{:S(2)}) %collective-permute-start.14) | collective-permute-done | bytes 32800 | tf_op jit(solution)/shard_map/ppermute | solution.py:269
  43.1 0.9 %collective-permute-done.13.refs_2_ = f32[8,1024]{1,0:T(8,128)S(1)} collective-permute-done((f32[8,1024]{1,0:T(8,128)S(1)}, f32[8,1024]{1,0:T(8,128)S(1)}, u32[]{:S(2)}, u32[]{:S(2)}) %collective-permute-start.13) | collective-permute-done | bytes 32800 | tf_op jit(solution)/shard_map/ppermute | solution.py:269
  43.9 0.0 collective-permute-done.12.refs_1_
  43.9 0.6 %last_sum.1 = (f32[1,8]{1,0:T(1,128)}, f32[8,1000]{1,0:T(8,128)}) custom-call(f32[8,1024]{1,0:T(8,128)S(1)} %add.15.refs_0_, f32[8,1024]{1,0:T(8,128)S(1)} %collective-permute-done.12.refs_1_, f32[8,1024]{1,0:T(8,128)S(1)} %collective-permute-done.13.refs_2_, f32[8,1024]{1,0:T(8,128)S(1)} %collective-permute-done.14.refs_3_), custom_call_target="tpu_custom_call" | custom-call | tf_op jit(solution)/shard_map/last_sum/pallas_call | solution.py:394
  (5 shorter events, 0.1 us)
Async XLA Ops:
  7.5 1.5 %collective-permute-start = (f32[32,512]{1,0:T(8,128)S(1)}, f32[32,512]{1,0:T(8,128)S(1)}, u32[]{:S(2)}, u32[]{:S(2)}) collective-permute-start(f32[32,512]{1,0:T(8,128)S(1)} %get-tuple-element.15), channel_id=1, source_target_pairs={{0,4},{1,5},{2,6},{3,7},{4,0},{5,1},{6,2},{7,3},{8,12},{9,13},{10,... | collective-permute-start | bytes 196616 | tf_op jit(solution)/shard_map/ppermute | solution.py:269
  9.0 6.1 %collective-permute-start.3 = (f32[32,512]{1,0:T(8,128)S(1)}, f32[32,512]{1,0:T(8,128)S(1)}, u32[]{:S(2)}, u32[]{:S(2)}) collective-permute-start(f32[32,512]{1,0:T(8,128)S(1)} %shard_map.50.refs_0_), channel_id=1, source_target_pairs={{0,24},{1,25},{2,26},{3,27},{4,7},{5,6},{6,5},{7,4},{8,16},{9,17},... | collective-permute-start | bytes 196616 | tf_op jit(solution)/shard_map/ppermute | solution.py:269
  12.8 4.3 %collective-permute-start.2 = (f32[32,512]{1,0:T(8,128)S(1)}, f32[32,512]{1,0:T(8,128)S(1)}, u32[]{:S(2)}, u32[]{:S(2)}) collective-permute-start(f32[32,512]{1,0:T(8,128)S(1)} %shard_map.50.refs_0_), channel_id=1, source_target_pairs={{0,16},{1,17},{2,18},{3,19},{4,6},{5,7},{6,4},{7,5},{8,24},{9,25},... | collective-permute-start | bytes 196616 | tf_op jit(solution)/shard_map/ppermute | solution.py:269
  13.3 4.3 %collective-permute-start.1 = (f32[32,512]{1,0:T(8,128)S(1)}, f32[32,512]{1,0:T(8,128)S(1)}, u32[]{:S(2)}, u32[]{:S(2)}) collective-permute-start(f32[32,512]{1,0:T(8,128)S(1)} %shard_map.50.refs_0_), channel_id=1, source_target_pairs={{0,8},{1,9},{2,10},{3,11},{4,5},{5,4},{6,7},{7,6},{8,0},{9,1},{10,... | collective-permute-start | bytes 196616 | tf_op jit(solution)/shard_map/ppermute | solution.py:269
  17.6 6.1 %collective-permute-start.6 = (f32[32,512]{1,0:T(8,128)S(1)}, f32[32,512]{1,0:T(8,128)S(1)}, u32[]{:S(2)}, u32[]{:S(2)}) collective-permute-start(f32[32,512]{1,0:T(8,128)S(1)} %shard_map.51.refs_0_), channel_id=1, source_target_pairs={{0,3},{1,2},{2,1},{3,0},{4,28},{5,29},{6,30},{7,31},{8,11},{9,10},... | collective-permute-start | bytes 196616 | tf_op jit(solution)/shard_map/ppermute | solution.py:269
  21.3 5.2 %collective-permute-start.5 = (f32[32,512]{1,0:T(8,128)S(1)}, f32[32,512]{1,0:T(8,128)S(1)}, u32[]{:S(2)}, u32[]{:S(2)}) collective-permute-start(f32[32,512]{1,0:T(8,128)S(1)} %shard_map.51.refs_0_), channel_id=1, source_target_pairs={{0,2},{1,3},{2,0},{3,1},{4,20},{5,21},{6,22},{7,23},{8,10},{9,11},... | collective-permute-start | bytes 196616 | tf_op jit(solution)/shard_map/ppermute | solution.py:269
  21.3 5.2 %collective-permute-start.4 = (f32[32,512]{1,0:T(8,128)S(1)}, f32[32,512]{1,0:T(8,128)S(1)}, u32[]{:S(2)}, u32[]{:S(2)}) collective-permute-start(f32[32,512]{1,0:T(8,128)S(1)} %shard_map.51.refs_0_), channel_id=1, source_target_pairs={{0,1},{1,0},{2,3},{3,2},{4,12},{5,13},{6,14},{7,15},{8,9},{9,8},{1... | collective-permute-start | bytes 196616 | tf_op jit(solution)/shard_map/ppermute | solution.py:269
  26.5 1.6 %collective-permute-start.7 = (bf16[32,512]{1,0:T(8,128)(2,1)S(1)}, bf16[32,512]{1,0:T(8,128)(2,1)S(1)}, u32[]{:S(2)}, u32[]{:S(2)}) collective-permute-start(bf16[32,512]{1,0:T(8,128)(2,1)S(1)} %shard_map.52.z_ref.mine_ref), channel_id=1, source_target_pairs={{0,4},{1,5},{2,6},{3,7},{4,0},{5,1},{6,2},{7,3},{8,12},{9,13},{10,... | collective-permute-start | bytes 98312 | tf_op jit(solution)/shard_map/ppermute | solution.py:269
  30.0 4.3 %collective-permute-start.8 = (f32[8,1024]{1,0:T(8,128)S(1)}, f32[8,1024]{1,0:T(8,128)S(1)}, u32[]{:S(2)}, u32[]{:S(2)}) collective-permute-start(f32[8,1024]{1,0:T(8,128)S(1)} %get-tuple-element.19), channel_id=1, source_target_pairs={{0,5},{1,4},{2,7},{3,6},{4,1},{5,0},{6,3},{7,2},{8,13},{9,12},{10,... | collective-permute-start | bytes 98312 | tf_op jit(solution)/shard_map/ppermute | solution.py:269
  30.7 4.4 %collective-permute-start.9 = (f32[8,1024]{1,0:T(8,128)S(1)}, f32[8,1024]{1,0:T(8,128)S(1)}, u32[]{:S(2)}, u32[]{:S(2)}) collective-permute-start(f32[8,1024]{1,0:T(8,128)S(1)} %get-tuple-element.20), channel_id=1, source_target_pairs={{0,6},{1,7},{2,4},{3,5},{4,2},{5,3},{6,0},{7,1},{8,14},{9,15},{10,... | collective-permute-start | bytes 98312 | tf_op jit(solution)/shard_map/ppermute | solution.py:269
  32.3 5.2 %collective-permute-start.10 = (f32[8,1024]{1,0:T(8,128)S(1)}, f32[8,1024]{1,0:T(8,128)S(1)}, u32[]{:S(2)}, u32[]{:S(2)}) collective-permute-start(f32[8,1024]{1,0:T(8,128)S(1)} %get-tuple-element.21), channel_id=1, source_target_pairs={{0,7},{1,6},{2,5},{3,4},{4,3},{5,2},{6,1},{7,0},{8,15},{9,14},{10,... | collective-permute-start | bytes 98312 | tf_op jit(solution)/shard_map/ppermute | solution.py:269
  37.5 1.3 %collective-permute-start.11 = (f32[8,1024]{1,0:T(8,128)S(1)}, f32[8,1024]{1,0:T(8,128)S(1)}, u32[]{:S(2)}, u32[]{:S(2)}) collective-permute-start(f32[8,1024]{1,0:T(8,128)S(1)} %add_add_fusion), channel_id=1, source_target_pairs={{0,4},{1,5},{2,6},{3,7},{4,0},{5,1},{6,2},{7,3},{8,12},{9,13},{10,... | collective-permute-start | bytes 98312 | tf_op jit(solution)/shard_map/ppermute | solution.py:269
  38.8 4.2 %collective-permute-start.14 = (f32[8,1024]{1,0:T(8,128)S(1)}, f32[8,1024]{1,0:T(8,128)S(1)}, u32[]{:S(2)}, u32[]{:S(2)}) collective-permute-start(f32[8,1024]{1,0:T(8,128)S(1)} %add.15.refs_0_), channel_id=1, source_target_pairs={{0,28},{1,29},{2,30},{3,31},{4,24},{5,25},{6,26},{7,27},{8,20},{9,... | collective-permute-start | bytes 98312 | tf_op jit(solution)/shard_map/ppermute | solution.py:269
  40.1 3.8 %collective-permute-start.13 = (f32[8,1024]{1,0:T(8,128)S(1)}, f32[8,1024]{1,0:T(8,128)S(1)}, u32[]{:S(2)}, u32[]{:S(2)}) collective-permute-start(f32[8,1024]{1,0:T(8,128)S(1)} %add.15.refs_0_), channel_id=1, source_target_pairs={{0,20},{1,21},{2,22},{3,23},{4,16},{5,17},{6,18},{7,19},{8,28},{9,... | collective-permute-start | bytes 98312 | tf_op jit(solution)/shard_map/ppermute | solution.py:269
  40.5 3.4 %collective-permute-start.12 = (f32[8,1024]{1,0:T(8,128)S(1)}, f32[8,1024]{1,0:T(8,128)S(1)}, u32[]{:S(2)}, u32[]{:S(2)}) collective-permute-start(f32[8,1024]{1,0:T(8,128)S(1)} %add.15.refs_0_), channel_id=1, source_target_pairs={{0,12},{1,13},{2,14},{3,15},{4,8},{5,9},{6,10},{7,11},{8,4},{9,5},... | collective-permute-start | bytes 98312 | tf_op jit(solution)/shard_map/ppermute | solution.py:269

commit v5 on v4

--- a/solution.py
+++ b/solution.py
@@ -79,19 +79,18 @@
     return (rows == start_t).astype(f32).astype(bf16)
 
 
-def weighted_sums(end_ref, store, hot, coef, value_row, width, split):
-    full = end_ref.shape[0]
-    for c in range(full // LANES):
-        y = end_ref[c * LANES : (c + 1) * LANES, :] * coef
-        if (c + 1) * LANES > width:
-            row = lax.broadcasted_iota(i32, y.shape, 0) + (c * LANES - width)
+def weighted_sums(end_ref, begin, out_ref, hot, coef, value_row, width, split):
+    for c in range(0, out_ref.shape[1], LANES):
+        y = end_ref[pl.ds(pl.multiple_of(begin + c, LANES), LANES), :] * coef
+        row = lax.broadcasted_iota(i32, y.shape, 0) + (begin + c - width)
+        if not isinstance(begin, int) or c + LANES > width - begin:
             y = jnp.where((row >= 0) & (row < VALUE_COPIES), value_row, y)
-        store(c, sum(contract_last(hot, part) for part in split(y)))
+        out_ref[:, c : c + LANES] = sum(contract_last(hot, part) for part in split(y))
 
 
 def first_kernel(
-    n_path, n_tm, inc_ref, lvl_hbm, time_hbm, mine_ref, other_ref, end_ref, rows_ref, buf,
-    lvl_ref, time_ref, part_ref, mask_ref, sems, table_sems,
+    n_path, n_tm, inc_ref, lvl_hbm, time_hbm, other_ref, end_ref, rows_ref, buf,
+    lvl_ref, time_ref, mask_ref, sems, table_sems,
 ):
     steps_k, width, paths = inc_ref.shape
     blk_dev = paths // BLOCK
@@ -155,16 +154,16 @@
     rows_ref[...] = jnp.concatenate(
         [level, start_t, first, share, coef, jnp.zeros((3, paths), f32)], axis=0
     )
-    half = mine_ref.shape[1]
-
-    def store(c, tile):
-        side, at = divmod(c * LANES, half)
-        part_ref[side, :, at : at + LANES] = tile
-
-    weighted_sums(end_ref, store, hot, coef * first, share * first, width, split3)
-    side = my_side()
-    mine_ref[...] = part_ref[side]
-    other_ref[...] = part_ref[1 - side]
+    half = other_ref.shape[1]
+    begin = (1 - my_side()) * half
+    weighted_sums(end_ref, begin, other_ref, hot, coef * first, share * first, width, split3)
+
+
+def own_sums_kernel(width, steps_k, end_ref, rows_ref, mine_ref):
+    _, start_t, first, share, coef = (rows_ref[r : r + 1, :] for r in range(5))
+    hot = start_hot(start_t, steps_k)
+    begin = my_side() * mine_ref.shape[1]
+    weighted_sums(end_ref, begin, mine_ref, hot, coef * first, share * first, width, split3)
 
 
 def dots_over(z_half, buf, begin, end):
@@ -224,10 +223,7 @@
     second = first + jnp.sum(weight * drift, axis=0, keepdims=True)
     hot = start_hot(start_t, steps_k)
 
-    def store(c, tile):
-        part_ref[:, c * LANES : (c + 1) * LANES] = tile
-
-    weighted_sums(end_ref, store, hot, coef * second, share * second, width, split2)
+    weighted_sums(end_ref, 0, part_ref, hot, coef * second, share * second, width, split2)
     me = lax.axis_index("tm")
     for away, out_ref in enumerate(out_refs):
         out_ref[...] = part_ref[pl.ds(pl.multiple_of((me ^ away) * group, group), group), :]
@@ -261,16 +257,28 @@
 
 
 def swap(x, flips, odd_flips=None):
-    n_tm = lax.axis_size("tm")
+    n_path, n_tm = lax.axis_size("path"), lax.axis_size("tm")
     even, odd = (path * n_tm + tm for path, tm in (flips, odd_flips or flips))
     pairs = [
-        (i, i ^ (odd if i // n_tm % 2 else even)) for i in range(lax.axis_size(("path", "tm")))
+        (i, i ^ (odd if side_of(i // n_tm, i % n_tm, n_path) else even))
+        for i in range(lax.axis_size(("path", "tm")))
     ]
     return lax.ppermute(x, ("path", "tm"), pairs)
 
 
+def parity(n):
+    return bin(n).count("1") % 2
+
+
+def side_of(path, tm, n_path):
+    bits = tm
+    for bit in range(n_path.bit_length() - 1):
+        bits = bits + (path >> bit)
+    return bits & 1
+
+
 def my_side():
-    return lax.axis_index("path") & 1
+    return side_of(lax.axis_index("path"), lax.axis_index("tm"), lax.axis_size("path"))
 
 
 def add_kernel(*refs):
@@ -326,21 +334,19 @@
     hbm = pl.BlockSpec(memory_space=pltpu.HBM)
     chunks = width // chunk_rows(width)
 
-    mine, other, end, rows, held = pl.pallas_call(
+    other, end, rows, held = pl.pallas_call(
         functools.partial(first_kernel, n_path, n_tm),
         out_shape=(
-            jax.ShapeDtypeStruct((steps_k, half), f32),
             jax.ShapeDtypeStruct((steps_k, half), f32),
             jax.ShapeDtypeStruct((full, paths), f32),
             jax.ShapeDtypeStruct((8, paths), f32),
             jax.ShapeDtypeStruct(inc.shape, bf16),
         ),
         in_specs=[hbm, hbm, hbm],
-        out_specs=(vmem,) * 5,
+        out_specs=(vmem,) * 4,
         scratch_shapes=[
             pltpu.VMEM((1, level_table.shape[0]), i32),
             pltpu.VMEM((1, time_table.shape[0]), i32),
-            pltpu.VMEM((2, steps_k, half), f32),
             pltpu.VMEM((steps_k, PACKED, paths), bf16),
             pltpu.SemaphoreType.DMA((chunks,)),
             pltpu.SemaphoreType.DMA((2,)),
@@ -349,9 +355,21 @@
         name="first_iterate",
     )(inc, *(in_hbm(table.reshape(1, -1)) for table in (level_table, time_table)))
 
-    parts = [mine, swap(other, (1, 0))]
-    over_path = [[(flip, 0) for flip in step] for step in path_steps(n_path)]
-    over_tm = [[(0, flip) for flip in step] for step in tm_steps(n_tm)]
+    other = swap(other, (1, 0))
+    mine = pl.pallas_call(
+        functools.partial(own_sums_kernel, width, steps_k),
+        out_shape=jax.ShapeDtypeStruct((steps_k, half), f32),
+        in_specs=[vmem] * 2,
+        out_specs=vmem,
+        compiler_params=pltpu.CompilerParams(vmem_limit_bytes=SMALL_LIMIT),
+        cost_estimate=pl.CostEstimate(
+            flops=6 * steps_k * half * paths, bytes_accessed=0, transcendentals=0
+        ),
+        name="own_sums",
+    )(end, rows)
+    parts = [mine, other]
+    over_path = [[(flip + parity(flip), 0) for flip in step] for step in path_steps(n_path)]
+    over_tm = [[(flip % 2, flip) for flip in step] for step in tm_steps(n_tm)]
     odd, even = over_tm + over_path, over_path + over_tm
     if [len(step) for step in even] != [len(step) for step in odd]:
         odd = even

time: 44.8 us -> 43.7 us (0.975)
  waiting for transfers between devices: 15.8 us -> 14.7 us
    ppermute x15, waiting for transfers between devices: 15.8 us -> 14.7 us  [swap(): return lax.ppermute(x, ('path', 'tm'), pairs)]
  transfers between devices with their start and end apart: 15 -> 15, of which waited for: 11 -> 11; matrix products, arithmetic and copies ran while one was open for 0% -> 0% of each run, Pallas kernels for 3% -> 4%
where the time goes in v5:
time: 43.7 us; the launch traced here: 43.5 us
  starting transfers between devices  17 us (39%)
  waiting for transfers between devices  14.7 us (34%)
  Pallas kernels  11.1 us (25%)
  between operations  0.69 us (2%)
    ppermute x15, starting transfers between devices, swap(): return lax.ppermute(x, ('path', 'tm'), pairs)  17 us
    ppermute x15, waiting for transfers between devices, swap(): return lax.ppermute(x, ('path', 'tm'), pairs)  14.7 us
    pallas_call x1, Pallas kernels, shards(): pl.pallas_call(functools.partial(first_kernel, n_path, n_tm), out_shape=(...  6.6 us
    pallas_call x1, Pallas kernels, shards(): pl.pallas_call(functools.partial(second_kernel, n_tm), out_shape=(jax.Sha...  1.93 us
    pallas_call x1, Pallas kernels, shards(): pl.pallas_call(own_half_kernel, out_shape=jax.ShapeDtypeStruct((steps_k,...  1.48 us
  transfers between devices with their start and end apart: 15, of which 11 were waited for; matrix products, arithmetic and copies ran while one was open for 0% of the time, Pallas kernels for 4%

profile of v5, /device:TPU:0, one launch (start us, length us, event | category | flops | bytes accessed | tf_op | source)
XLA Modules:
  0.0 43.5 jit_solution(15001720128667126700)
XLA Ops:
  0.6 6.6 %first_iterate.1 = (f32[32,512]{1,0:T(8,128)S(1)}, f32[1024,256]{1,0:T(8,128)S(1)}, f32[8,256]{1,0:T(8,128)S(1)}, bf16[32,1000,256]{2,1,0:T(8,128)(2,1)S(1)}) custom-call(bf16[32,1000,256]{2,1,0:T(8,128)(2,1)} %bitcast.4, s32[1,4096]{1,0:T(1,128)} %bitcast.5, s32[1,4096]{1,0:T(1,128)} %bitcast.6), custom_call_target="tpu_custom_call" | custom-call | tf_op jit(solution)/shard_map/first_iterate/pallas_call | solution.py:337
  7.2 0.6 %collective-permute-start = (f32[32,512]{1,0:T(8,128)S(1)}, f32[32,512]{1,0:T(8,128)S(1)}, u32[]{:S(2)}, u32[]{:S(2)}) collective-permute-start(f32[32,512]{1,0:T(8,128)S(1)} %get-tuple-element.15), channel_id=1, source_target_pairs={{0,4},{1,5},{2,6},{3,7},{4,0},{5,1},{6,2},{7,3},{8,12},{9,13},{10,... | collective-permute-start | bytes 196616 | tf_op jit(solution)/shard_map/ppermute | solution.py:266
  7.8 0.4 own_sums.1.refs_0_
  8.2 0.5 %collective-permute-done.refs_1_ = f32[32,512]{1,0:T(8,128)S(1)} collective-permute-done((f32[32,512]{1,0:T(8,128)S(1)}, f32[32,512]{1,0:T(8,128)S(1)}, u32[]{:S(2)}, u32[]{:S(2)}) %collective-permute-start) | collective-permute-done | bytes 65568 | tf_op jit(solution)/shard_map/ppermute | solution.py:266
  8.7 3.8 %collective-permute-start.3 = (f32[32,512]{1,0:T(8,128)S(1)}, f32[32,512]{1,0:T(8,128)S(1)}, u32[]{:S(2)}, u32[]{:S(2)}) collective-permute-start(f32[32,512]{1,0:T(8,128)S(1)} %shard_map.50.refs_0_), channel_id=1, source_target_pairs={{0,24},{1,6},{2,26},{3,4},{4,3},{5,29},{6,1},{7,31},{8,15},{9,17},... | collective-permute-start | bytes 196616 | tf_op jit(solution)/shard_map/ppermute | solution.py:266
  12.6 0.0 collective-permute-start.2
  12.6 0.4 collective-permute-start.1
  12.9 1.9 %collective-permute-done.3.refs_3_ = f32[32,512]{1,0:T(8,128)S(1)} collective-permute-done((f32[32,512]{1,0:T(8,128)S(1)}, f32[32,512]{1,0:T(8,128)S(1)}, u32[]{:S(2)}, u32[]{:S(2)}) %collective-permute-start.3) | collective-permute-done | bytes 65568 | tf_op jit(solution)/shard_map/ppermute | solution.py:266
  14.8 1.4 %collective-permute-done.2.refs_2_ = f32[32,512]{1,0:T(8,128)S(1)} collective-permute-done((f32[32,512]{1,0:T(8,128)S(1)}, f32[32,512]{1,0:T(8,128)S(1)}, u32[]{:S(2)}, u32[]{:S(2)}) %collective-permute-start.2) | collective-permute-done | bytes 65568 | tf_op jit(solution)/shard_map/ppermute | solution.py:266
  16.3 0.0 collective-permute-done.1.refs_1_
  16.3 3.9 %collective-permute-start.6 = (f32[32,512]{1,0:T(8,128)S(1)}, f32[32,512]{1,0:T(8,128)S(1)}, u32[]{:S(2)}, u32[]{:S(2)}) collective-permute-start(f32[32,512]{1,0:T(8,128)S(1)} %shard_map.51.refs_0_), channel_id=1, source_target_pairs={{0,7},{1,25},{2,5},{3,27},{4,28},{5,2},{6,30},{7,0},{8,16},{9,14},... | collective-permute-start | bytes 196616 | tf_op jit(solution)/shard_map/ppermute | solution.py:266
  20.2 0.0 collective-permute-start.5
  20.2 0.4 collective-permute-start.4
  20.5 1.7 %collective-permute-done.6.refs_3_ = f32[32,512]{1,0:T(8,128)S(1)} collective-permute-done((f32[32,512]{1,0:T(8,128)S(1)}, f32[32,512]{1,0:T(8,128)S(1)}, u32[]{:S(2)}, u32[]{:S(2)}) %collective-permute-start.6) | collective-permute-done | bytes 65568 | tf_op jit(solution)/shard_map/ppermute | solution.py:266
  22.2 3.1 %collective-permute-done.5.refs_2_ = f32[32,512]{1,0:T(8,128)S(1)} collective-permute-done((f32[32,512]{1,0:T(8,128)S(1)}, f32[32,512]{1,0:T(8,128)S(1)}, u32[]{:S(2)}, u32[]{:S(2)}) %collective-permute-start.5) | collective-permute-done | bytes 65568 | tf_op jit(solution)/shard_map/ppermute | solution.py:266
  25.3 0.0 collective-permute-done.4.refs_1_
  25.4 0.2 collective-permute-start.7
  25.6 1.5 %own_half.1.total_ref = f32[32,256]{1,0:T(8,128)S(1)} custom-call(bf16[32,1000,256]{2,1,0:T(8,128)(2,1)S(1)} %get-tuple-element.12.buf, bf16[32,512]{1,0:T(8,128)(2,1)S(1)} %shard_map.52.z_ref.mine_ref), custom_call_target="tpu_custom_call" | custom-call | flops 262144000 | tf_op jit(solution)/shard_map/own_half/pallas_call | solution.py:382
  27.1 0.0 collective-permute-done.7.other_ref
  27.1 1.9 %second_iterate.1 = (f32[8,1024]{1,0:T(8,128)S(1)}, f32[8,1024]{1,0:T(8,128)S(1)}, f32[8,1024]{1,0:T(8,128)S(1)}, f32[8,1024]{1,0:T(8,128)S(1)}) custom-call(bf16[32,1000,256]{2,1,0:T(8,128)(2,1)S(1)} %get-tuple-element.12.buf, bf16[32,512]{1,0:T(8,128)(2,1)S(1)} %shard_map.52.z_ref.mine_ref, bf16[32,512]{1,0:T(8,128)(2,1)S(1)} %collective-permute-done.7.other_ref, ...), custom_call_target="tpu_custom_call" | custom-call | tf_op jit(solution)/shard_map/second_iterate/pallas_call | solution.py:393
  29.0 0.1 collective-permute-start.8
  29.1 1.5 %collective-permute-start.9 = (f32[8,1024]{1,0:T(8,128)S(1)}, f32[8,1024]{1,0:T(8,128)S(1)}, u32[]{:S(2)}, u32[]{:S(2)}) collective-permute-start(f32[8,1024]{1,0:T(8,128)S(1)} %get-tuple-element.18), channel_id=1, source_target_pairs={{0,6},{1,7},{2,4},{3,5},{4,2},{5,3},{6,0},{7,1},{8,14},{9,15},{10,... | collective-permute-start | bytes 98312 | tf_op jit(solution)/shard_map/ppermute | solution.py:266
  30.7 2.5 %collective-permute-start.10 = (f32[8,1024]{1,0:T(8,128)S(1)}, f32[8,1024]{1,0:T(8,128)S(1)}, u32[]{:S(2)}, u32[]{:S(2)}) collective-permute-start(f32[8,1024]{1,0:T(8,128)S(1)} %get-tuple-element.19), channel_id=1, source_target_pairs={{0,7},{1,6},{2,5},{3,4},{4,3},{5,2},{6,1},{7,0},{8,15},{9,14},{10,... | collective-permute-start | bytes 98312 | tf_op jit(solution)/shard_map/ppermute | solution.py:266
  33.2 0.0 collective-permute-done.8
  33.2 0.2 collective-permute-done.9
  33.4 2.4 %collective-permute-done.10 = f32[8,1024]{1,0:T(8,128)S(1)} collective-permute-done((f32[8,1024]{1,0:T(8,128)S(1)}, f32[8,1024]{1,0:T(8,128)S(1)}, u32[]{:S(2)}, u32[]{:S(2)}) %collective-permute-start.10) | collective-permute-done | bytes 32800 | tf_op jit(solution)/shard_map/ppermute | solution.py:266
  35.8 0.4 collective-permute-start.11
  36.2 0.9 %collective-permute-done.11 = f32[8,1024]{1,0:T(8,128)S(1)} collective-permute-done((f32[8,1024]{1,0:T(8,128)S(1)}, f32[8,1024]{1,0:T(8,128)S(1)}, u32[]{:S(2)}, u32[]{:S(2)}) %collective-permute-start.11) | collective-permute-done | bytes 32800 | tf_op jit(solution)/shard_map/ppermute | solution.py:266
  37.1 1.7 %collective-permute-start.14 = (f32[8,1024]{1,0:T(8,128)S(1)}, f32[8,1024]{1,0:T(8,128)S(1)}, u32[]{:S(2)}, u32[]{:S(2)}) collective-permute-start(f32[8,1024]{1,0:T(8,128)S(1)} %add.15.refs_0_), channel_id=1, source_target_pairs={{0,28},{1,29},{2,30},{3,31},{4,24},{5,25},{6,26},{7,27},{8,20},{9,... | collective-permute-start | bytes 98312 | tf_op jit(solution)/shard_map/ppermute | solution.py:266
  38.8 0.7 %collective-permute-start.13 = (f32[8,1024]{1,0:T(8,128)S(1)}, f32[8,1024]{1,0:T(8,128)S(1)}, u32[]{:S(2)}, u32[]{:S(2)}) collective-permute-start(f32[8,1024]{1,0:T(8,128)S(1)} %add.15.refs_0_), channel_id=1, source_target_pairs={{0,20},{1,21},{2,22},{3,23},{4,16},{5,17},{6,18},{7,19},{8,28},{9,... | collective-permute-start | bytes 98312 | tf_op jit(solution)/shard_map/ppermute | solution.py:266
  39.5 0.8 %collective-permute-start.12 = (f32[8,1024]{1,0:T(8,128)S(1)}, f32[8,1024]{1,0:T(8,128)S(1)}, u32[]{:S(2)}, u32[]{:S(2)}) collective-permute-start(f32[8,1024]{1,0:T(8,128)S(1)} %add.15.refs_0_), channel_id=1, source_target_pairs={{0,12},{1,13},{2,14},{3,15},{4,8},{5,9},{6,10},{7,11},{8,4},{9,5},... | collective-permute-start | bytes 98312 | tf_op jit(solution)/shard_map/ppermute | solution.py:266
  40.3 1.0 %collective-permute-done.14.refs_3_ = f32[8,1024]{1,0:T(8,128)S(1)} collective-permute-done((f32[8,1024]{1,0:T(8,128)S(1)}, f32[8,1024]{1,0:T(8,128)S(1)}, u32[]{:S(2)}, u32[]{:S(2)}) %collective-permute-start.14) | collective-permute-done | bytes 32800 | tf_op jit(solution)/shard_map/ppermute | solution.py:266
  41.3 0.9 %collective-permute-done.13.refs_2_ = f32[8,1024]{1,0:T(8,128)S(1)} collective-permute-done((f32[8,1024]{1,0:T(8,128)S(1)}, f32[8,1024]{1,0:T(8,128)S(1)}, u32[]{:S(2)}, u32[]{:S(2)}) %collective-permute-start.13) | collective-permute-done | bytes 32800 | tf_op jit(solution)/shard_map/ppermute | solution.py:266
  42.2 0.6 %collective-permute-done.12.refs_1_ = f32[8,1024]{1,0:T(8,128)S(1)} collective-permute-done((f32[8,1024]{1,0:T(8,128)S(1)}, f32[8,1024]{1,0:T(8,128)S(1)}, u32[]{:S(2)}, u32[]{:S(2)}) %collective-permute-start.12) | collective-permute-done | bytes 32800 | tf_op jit(solution)/shard_map/ppermute | solution.py:266
  42.8 0.6 %last_sum.1 = (f32[1,8]{1,0:T(1,128)}, f32[8,1000]{1,0:T(8,128)}) custom-call(f32[8,1024]{1,0:T(8,128)S(1)} %add.15.refs_0_, f32[8,1024]{1,0:T(8,128)S(1)} %collective-permute-done.12.refs_1_, f32[8,1024]{1,0:T(8,128)S(1)} %collective-permute-done.13.refs_2_, f32[8,1024]{1,0:T(8,128)S(1)} %collective-permute-done.14.refs_3_), custom_call_target="tpu_custom_call" | custom-call | tf_op jit(solution)/shard_map/last_sum/pallas_call | solution.py:412
  (5 shorter events, 0.1 us)
Async XLA Ops:
  7.2 1.5 %collective-permute-start = (f32[32,512]{1,0:T(8,128)S(1)}, f32[32,512]{1,0:T(8,128)S(1)}, u32[]{:S(2)}, u32[]{:S(2)}) collective-permute-start(f32[32,512]{1,0:T(8,128)S(1)} %get-tuple-element.15), channel_id=1, source_target_pairs={{0,4},{1,5},{2,6},{3,7},{4,0},{5,1},{6,2},{7,3},{8,12},{9,13},{10,... | collective-permute-start | bytes 196616 | tf_op jit(solution)/shard_map/ppermute | solution.py:266
  8.7 6.1 %collective-permute-start.3 = (f32[32,512]{1,0:T(8,128)S(1)}, f32[32,512]{1,0:T(8,128)S(1)}, u32[]{:S(2)}, u32[]{:S(2)}) collective-permute-start(f32[32,512]{1,0:T(8,128)S(1)} %shard_map.50.refs_0_), channel_id=1, source_target_pairs={{0,24},{1,6},{2,26},{3,4},{4,3},{5,29},{6,1},{7,31},{8,15},{9,17},... | collective-permute-start | bytes 196616 | tf_op jit(solution)/shard_map/ppermute | solution.py:266
  12.6 3.7 %collective-permute-start.2 = (f32[32,512]{1,0:T(8,128)S(1)}, f32[32,512]{1,0:T(8,128)S(1)}, u32[]{:S(2)}, u32[]{:S(2)}) collective-permute-start(f32[32,512]{1,0:T(8,128)S(1)} %shard_map.50.refs_0_), channel_id=1, source_target_pairs={{0,20},{1,3},{2,22},{3,1},{4,6},{5,17},{6,4},{7,19},{8,10},{9,29},... | collective-permute-start | bytes 196616 | tf_op jit(solution)/shard_map/ppermute | solution.py:266
  12.6 3.7 %collective-permute-start.1 = (f32[32,512]{1,0:T(8,128)S(1)}, f32[32,512]{1,0:T(8,128)S(1)}, u32[]{:S(2)}, u32[]{:S(2)}) collective-permute-start(f32[32,512]{1,0:T(8,128)S(1)} %shard_map.50.refs_0_), channel_id=1, source_target_pairs={{0,12},{1,4},{2,14},{3,6},{4,1},{5,9},{6,3},{7,11},{8,13},{9,5},{1... | collective-permute-start | bytes 196616 | tf_op jit(solution)/shard_map/ppermute | solution.py:266
  16.3 5.9 %collective-permute-start.6 = (f32[32,512]{1,0:T(8,128)S(1)}, f32[32,512]{1,0:T(8,128)S(1)}, u32[]{:S(2)}, u32[]{:S(2)}) collective-permute-start(f32[32,512]{1,0:T(8,128)S(1)} %shard_map.51.refs_0_), channel_id=1, source_target_pairs={{0,7},{1,25},{2,5},{3,27},{4,28},{5,2},{6,30},{7,0},{8,16},{9,14},... | collective-permute-start | bytes 196616 | tf_op jit(solution)/shard_map/ppermute | solution.py:266
  20.2 5.2 %collective-permute-start.5 = (f32[32,512]{1,0:T(8,128)S(1)}, f32[32,512]{1,0:T(8,128)S(1)}, u32[]{:S(2)}, u32[]{:S(2)}) collective-permute-start(f32[32,512]{1,0:T(8,128)S(1)} %shard_map.51.refs_0_), channel_id=1, source_target_pairs={{0,2},{1,21},{2,0},{3,23},{4,16},{5,7},{6,18},{7,5},{8,28},{9,11},... | collective-permute-start | bytes 196616 | tf_op jit(solution)/shard_map/ppermute | solution.py:266
  20.2 5.2 %collective-permute-start.4 = (f32[32,512]{1,0:T(8,128)S(1)}, f32[32,512]{1,0:T(8,128)S(1)}, u32[]{:S(2)}, u32[]{:S(2)}) collective-permute-start(f32[32,512]{1,0:T(8,128)S(1)} %shard_map.51.refs_0_), channel_id=1, source_target_pairs={{0,5},{1,13},{2,7},{3,15},{4,8},{5,0},{6,10},{7,2},{8,4},{9,12},{1... | collective-permute-start | bytes 196616 | tf_op jit(solution)/shard_map/ppermute | solution.py:266
  25.4 1.7 %collective-permute-start.7 = (bf16[32,512]{1,0:T(8,128)(2,1)S(1)}, bf16[32,512]{1,0:T(8,128)(2,1)S(1)}, u32[]{:S(2)}, u32[]{:S(2)}) collective-permute-start(bf16[32,512]{1,0:T(8,128)(2,1)S(1)} %shard_map.52.z_ref.mine_ref), channel_id=1, source_target_pairs={{0,4},{1,5},{2,6},{3,7},{4,0},{5,1},{6,2},{7,3},{8,12},{9,13},{10,... | collective-permute-start | bytes 98312 | tf_op jit(solution)/shard_map/ppermute | solution.py:266
  29.0 4.1 %collective-permute-start.8 = (f32[8,1024]{1,0:T(8,128)S(1)}, f32[8,1024]{1,0:T(8,128)S(1)}, u32[]{:S(2)}, u32[]{:S(2)}) collective-permute-start(f32[8,1024]{1,0:T(8,128)S(1)} %get-tuple-element.17), channel_id=1, source_target_pairs={{0,5},{1,4},{2,7},{3,6},{4,1},{5,0},{6,3},{7,2},{8,13},{9,12},{10,... | collective-permute-start | bytes 98312 | tf_op jit(solution)/shard_map/ppermute | solution.py:266
  29.1 4.3 %collective-permute-start.9 = (f32[8,1024]{1,0:T(8,128)S(1)}, f32[8,1024]{1,0:T(8,128)S(1)}, u32[]{:S(2)}, u32[]{:S(2)}) collective-permute-start(f32[8,1024]{1,0:T(8,128)S(1)} %get-tuple-element.18), channel_id=1, source_target_pairs={{0,6},{1,7},{2,4},{3,5},{4,2},{5,3},{6,0},{7,1},{8,14},{9,15},{10,... | collective-permute-start | bytes 98312 | tf_op jit(solution)/shard_map/ppermute | solution.py:266
  30.7 5.1 %collective-permute-start.10 = (f32[8,1024]{1,0:T(8,128)S(1)}, f32[8,1024]{1,0:T(8,128)S(1)}, u32[]{:S(2)}, u32[]{:S(2)}) collective-permute-start(f32[8,1024]{1,0:T(8,128)S(1)} %get-tuple-element.19), channel_id=1, source_target_pairs={{0,7},{1,6},{2,5},{3,4},{4,3},{5,2},{6,1},{7,0},{8,15},{9,14},{10,... | collective-permute-start | bytes 98312 | tf_op jit(solution)/shard_map/ppermute | solution.py:266
  35.8 1.3 %collective-permute-start.11 = (f32[8,1024]{1,0:T(8,128)S(1)}, f32[8,1024]{1,0:T(8,128)S(1)}, u32[]{:S(2)}, u32[]{:S(2)}) collective-permute-start(f32[8,1024]{1,0:T(8,128)S(1)} %add_add_fusion), channel_id=1, source_target_pairs={{0,4},{1,5},{2,6},{3,7},{4,0},{5,1},{6,2},{7,3},{8,12},{9,13},{10,... | collective-permute-start | bytes 98312 | tf_op jit(solution)/shard_map/ppermute | solution.py:266
  37.1 4.2 %collective-permute-start.14 = (f32[8,1024]{1,0:T(8,128)S(1)}, f32[8,1024]{1,0:T(8,128)S(1)}, u32[]{:S(2)}, u32[]{:S(2)}) collective-permute-start(f32[8,1024]{1,0:T(8,128)S(1)} %add.15.refs_0_), channel_id=1, source_target_pairs={{0,28},{1,29},{2,30},{3,31},{4,24},{5,25},{6,26},{7,27},{8,20},{9,... | collective-permute-start | bytes 98312 | tf_op jit(solution)/shard_map/ppermute | solution.py:266
  38.8 3.4 %collective-permute-start.13 = (f32[8,1024]{1,0:T(8,128)S(1)}, f32[8,1024]{1,0:T(8,128)S(1)}, u32[]{:S(2)}, u32[]{:S(2)}) collective-permute-start(f32[8,1024]{1,0:T(8,128)S(1)} %add.15.refs_0_), channel_id=1, source_target_pairs={{0,20},{1,21},{2,22},{3,23},{4,16},{5,17},{6,18},{7,19},{8,28},{9,... | collective-permute-start | bytes 98312 | tf_op jit(solution)/shard_map/ppermute | solution.py:266
  39.5 3.3 %collective-permute-start.12 = (f32[8,1024]{1,0:T(8,128)S(1)}, f32[8,1024]{1,0:T(8,128)S(1)}, u32[]{:S(2)}, u32[]{:S(2)}) collective-permute-start(f32[8,1024]{1,0:T(8,128)S(1)} %add.15.refs_0_), channel_id=1, source_target_pairs={{0,12},{1,13},{2,14},{3,15},{4,8},{5,9},{6,10},{7,11},{8,4},{9,5},... | collective-permute-start | bytes 98312 | tf_op jit(solution)/shard_map/ppermute | solution.py:266

commit v6 on v5

--- a/solution.py
+++ b/solution.py
@@ -321,7 +321,8 @@
 
 
 def tm_steps(n_tm):
-    return [tuple(step // 2 for step in steps) for steps in path_steps(2 * n_tm)]
+    steps = [tuple(flip // 2 for flip in step) for step in path_steps(2 * n_tm)]
+    return [(step[0], *step[:0:-1]) for step in steps]
 
 
 def shards(n_path, n_tm, increments, level_table, time_table):
@@ -404,7 +405,8 @@
         name="second_iterate",
     )(held, own, other, total, end, rows)
 
-    own = pairwise([parts[0]] + [swap(parts[away], (1, away)) for away in range(1, n_tm)])
+    order = [away for away in (*range(2, n_tm), 1) if away < n_tm]
+    own = pairwise([parts[0]] + [swap(parts[away], (1, away)) for away in order])
     parts = [own, swap(own, (1, 0))]
     for step in path_steps(n_path):
         total = pairwise(parts)

time: 43.7 us -> 42.6 us (0.975)
  starting transfers between devices: 17 us -> 16 us
    ppermute x15, starting transfers between devices: 17 us -> 16 us  [swap(): return lax.ppermute(x, ('path', 'tm'), pairs)]
  transfers between devices with their start and end apart: 15 -> 15, of which waited for: 11 -> 12; matrix products, arithmetic and copies ran while one was open for 0% -> 0% of each run, Pallas kernels for 4% -> 4%
where the time goes in v6:
time: 42.6 us; the launch traced here: 42.4 us
  starting transfers between devices  16 us (38%)
  waiting for transfers between devices  14.5 us (34%)
  Pallas kernels  11.1 us (26%)
  between operations  0.68 us (2%)
    ppermute x15, starting transfers between devices, swap(): return lax.ppermute(x, ('path', 'tm'), pairs)  16 us
    ppermute x15, waiting for transfers between devices, swap(): return lax.ppermute(x, ('path', 'tm'), pairs)  14.5 us
    pallas_call x1, Pallas kernels, shards(): pl.pallas_call(functools.partial(first_kernel, n_path, n_tm), out_shape=(...  6.6 us
    pallas_call x1, Pallas kernels, shards(): pl.pallas_call(functools.partial(second_kernel, n_tm), out_shape=(jax.Sha...  1.93 us
    pallas_call x1, Pallas kernels, shards(): pl.pallas_call(own_half_kernel, out_shape=jax.ShapeDtypeStruct((steps_k,...  1.48 us
  transfers between devices with their start and end apart: 15, of which 12 were waited for; matrix products, arithmetic and copies ran while one was open for 0% of the time, Pallas kernels for 4%

profile of v6, /device:TPU:0, one launch (start us, length us, event | category | flops | bytes accessed | tf_op | source)
XLA Modules:
  0.0 42.4 jit_solution(1537938517084882564)
XLA Ops:
  0.6 6.6 %first_iterate.1 = (f32[32,512]{1,0:T(8,128)S(1)}, f32[1024,256]{1,0:T(8,128)S(1)}, f32[8,256]{1,0:T(8,128)S(1)}, bf16[32,1000,256]{2,1,0:T(8,128)(2,1)S(1)}) custom-call(bf16[32,1000,256]{2,1,0:T(8,128)(2,1)} %bitcast.4, s32[1,4096]{1,0:T(1,128)} %bitcast.5, s32[1,4096]{1,0:T(1,128)} %bitcast.6), custom_call_target="tpu_custom_call" | custom-call | tf_op jit(solution)/shard_map/first_iterate/pallas_call | solution.py:338
  7.2 0.6 %collective-permute-start = (f32[32,512]{1,0:T(8,128)S(1)}, f32[32,512]{1,0:T(8,128)S(1)}, u32[]{:S(2)}, u32[]{:S(2)}) collective-permute-start(f32[32,512]{1,0:T(8,128)S(1)} %get-tuple-element.15), channel_id=1, source_target_pairs={{0,4},{1,5},{2,6},{3,7},{4,0},{5,1},{6,2},{7,3},{8,12},{9,13},{10,... | collective-permute-start | bytes 196616 | tf_op jit(solution)/shard_map/ppermute | solution.py:266
  7.8 0.4 own_sums.1.refs_0_
  8.2 0.5 %collective-permute-done.refs_1_ = f32[32,512]{1,0:T(8,128)S(1)} collective-permute-done((f32[32,512]{1,0:T(8,128)S(1)}, f32[32,512]{1,0:T(8,128)S(1)}, u32[]{:S(2)}, u32[]{:S(2)}) %collective-permute-start) | collective-permute-done | bytes 65568 | tf_op jit(solution)/shard_map/ppermute | solution.py:266
  8.7 3.8 %collective-permute-start.3 = (f32[32,512]{1,0:T(8,128)S(1)}, f32[32,512]{1,0:T(8,128)S(1)}, u32[]{:S(2)}, u32[]{:S(2)}) collective-permute-start(f32[32,512]{1,0:T(8,128)S(1)} %shard_map.50.refs_0_), channel_id=1, source_target_pairs={{0,24},{1,3},{2,26},{3,1},{4,6},{5,29},{6,4},{7,31},{8,10},{9,17},... | collective-permute-start | bytes 196616 | tf_op jit(solution)/shard_map/ppermute | solution.py:266
  12.6 0.0 collective-permute-start.2
  12.6 0.4 collective-permute-start.1
  12.9 1.9 %collective-permute-done.3.refs_3_ = f32[32,512]{1,0:T(8,128)S(1)} collective-permute-done((f32[32,512]{1,0:T(8,128)S(1)}, f32[32,512]{1,0:T(8,128)S(1)}, u32[]{:S(2)}, u32[]{:S(2)}) %collective-permute-start.3) | collective-permute-done | bytes 65568 | tf_op jit(solution)/shard_map/ppermute | solution.py:266
  14.8 1.4 %collective-permute-done.2.refs_2_ = f32[32,512]{1,0:T(8,128)S(1)} collective-permute-done((f32[32,512]{1,0:T(8,128)S(1)}, f32[32,512]{1,0:T(8,128)S(1)}, u32[]{:S(2)}, u32[]{:S(2)}) %collective-permute-start.2) | collective-permute-done | bytes 65568 | tf_op jit(solution)/shard_map/ppermute | solution.py:266
  16.3 0.0 collective-permute-done.1.refs_1_
  16.3 2.7 %collective-permute-start.6 = (f32[32,512]{1,0:T(8,128)S(1)}, f32[32,512]{1,0:T(8,128)S(1)}, u32[]{:S(2)}, u32[]{:S(2)}) collective-permute-start(f32[32,512]{1,0:T(8,128)S(1)} %shard_map.51.refs_0_), channel_id=1, source_target_pairs={{0,2},{1,25},{2,0},{3,27},{4,28},{5,7},{6,30},{7,5},{8,16},{9,11},... | collective-permute-start | bytes 196616 | tf_op jit(solution)/shard_map/ppermute | solution.py:266
  18.9 1.4 %collective-permute-start.5 = (f32[32,512]{1,0:T(8,128)S(1)}, f32[32,512]{1,0:T(8,128)S(1)}, u32[]{:S(2)}, u32[]{:S(2)}) collective-permute-start(f32[32,512]{1,0:T(8,128)S(1)} %shard_map.51.refs_0_), channel_id=1, source_target_pairs={{0,7},{1,21},{2,5},{3,23},{4,16},{5,2},{6,18},{7,0},{8,28},{9,14},... | collective-permute-start | bytes 196616 | tf_op jit(solution)/shard_map/ppermute | solution.py:266
  20.3 0.1 collective-permute-start.4
  20.5 1.1 %collective-permute-done.6.refs_3_ = f32[32,512]{1,0:T(8,128)S(1)} collective-permute-done((f32[32,512]{1,0:T(8,128)S(1)}, f32[32,512]{1,0:T(8,128)S(1)}, u32[]{:S(2)}, u32[]{:S(2)}) %collective-permute-start.6) | collective-permute-done | bytes 65568 | tf_op jit(solution)/shard_map/ppermute | solution.py:266
  21.5 3.0 %collective-permute-done.5.refs_2_ = f32[32,512]{1,0:T(8,128)S(1)} collective-permute-done((f32[32,512]{1,0:T(8,128)S(1)}, f32[32,512]{1,0:T(8,128)S(1)}, u32[]{:S(2)}, u32[]{:S(2)}) %collective-permute-start.5) | collective-permute-done | bytes 65568 | tf_op jit(solution)/shard_map/ppermute | solution.py:266
  24.5 0.2 collective-permute-done.4.refs_1_
  24.8 0.4 collective-permute-start.7
  25.1 1.5 %own_half.1.total_ref = f32[32,256]{1,0:T(8,128)S(1)} custom-call(bf16[32,1000,256]{2,1,0:T(8,128)(2,1)S(1)} %get-tuple-element.12.buf, bf16[32,512]{1,0:T(8,128)(2,1)S(1)} %shard_map.52.z_ref.mine_ref), custom_call_target="tpu_custom_call" | custom-call | flops 262144000 | tf_op jit(solution)/shard_map/own_half/pallas_call | solution.py:383
  26.6 0.0 collective-permute-done.7.other_ref
  26.7 1.9 %second_iterate.1 = (f32[8,1024]{1,0:T(8,128)S(1)}, f32[8,1024]{1,0:T(8,128)S(1)}, f32[8,1024]{1,0:T(8,128)S(1)}, f32[8,1024]{1,0:T(8,128)S(1)}) custom-call(bf16[32,1000,256]{2,1,0:T(8,128)(2,1)S(1)} %get-tuple-element.12.buf, bf16[32,512]{1,0:T(8,128)(2,1)S(1)} %shard_map.52.z_ref.mine_ref, bf16[32,512]{1,0:T(8,128)(2,1)S(1)} %collective-permute-done.7.other_ref, ...), custom_call_target="tpu_custom_call" | custom-call | tf_op jit(solution)/shard_map/second_iterate/pallas_call | solution.py:394
  28.6 1.1 %collective-permute-start.8 = (f32[8,1024]{1,0:T(8,128)S(1)}, f32[8,1024]{1,0:T(8,128)S(1)}, u32[]{:S(2)}, u32[]{:S(2)}) collective-permute-start(f32[8,1024]{1,0:T(8,128)S(1)} %get-tuple-element.17), channel_id=1, source_target_pairs={{0,6},{1,7},{2,4},{3,5},{4,2},{5,3},{6,0},{7,1},{8,14},{9,15},{10,... | collective-permute-start | bytes 98312 | tf_op jit(solution)/shard_map/ppermute | solution.py:266
  29.7 1.2 %collective-permute-start.9 = (f32[8,1024]{1,0:T(8,128)S(1)}, f32[8,1024]{1,0:T(8,128)S(1)}, u32[]{:S(2)}, u32[]{:S(2)}) collective-permute-start(f32[8,1024]{1,0:T(8,128)S(1)} %get-tuple-element.18), channel_id=1, source_target_pairs={{0,7},{1,6},{2,5},{3,4},{4,3},{5,2},{6,1},{7,0},{8,15},{9,14},{10,... | collective-permute-start | bytes 98312 | tf_op jit(solution)/shard_map/ppermute | solution.py:266
  30.9 0.7 %collective-permute-start.10 = (f32[8,1024]{1,0:T(8,128)S(1)}, f32[8,1024]{1,0:T(8,128)S(1)}, u32[]{:S(2)}, u32[]{:S(2)}) collective-permute-start(f32[8,1024]{1,0:T(8,128)S(1)} %get-tuple-element.19), channel_id=1, source_target_pairs={{0,5},{1,4},{2,7},{3,6},{4,1},{5,0},{6,3},{7,2},{8,13},{9,12},{10,... | collective-permute-start | bytes 98312 | tf_op jit(solution)/shard_map/ppermute | solution.py:266
  31.7 1.9 %collective-permute-done.8 = f32[8,1024]{1,0:T(8,128)S(1)} collective-permute-done((f32[8,1024]{1,0:T(8,128)S(1)}, f32[8,1024]{1,0:T(8,128)S(1)}, u32[]{:S(2)}, u32[]{:S(2)}) %collective-permute-start.8) | collective-permute-done | bytes 32800 | tf_op jit(solution)/shard_map/ppermute | solution.py:266
  33.6 1.4 %collective-permute-done.9 = f32[8,1024]{1,0:T(8,128)S(1)} collective-permute-done((f32[8,1024]{1,0:T(8,128)S(1)}, f32[8,1024]{1,0:T(8,128)S(1)}, u32[]{:S(2)}, u32[]{:S(2)}) %collective-permute-start.9) | collective-permute-done | bytes 32800 | tf_op jit(solution)/shard_map/ppermute | solution.py:266
  34.9 0.0 collective-permute-done.10
  35.0 0.5 %collective-permute-start.11 = (f32[8,1024]{1,0:T(8,128)S(1)}, f32[8,1024]{1,0:T(8,128)S(1)}, u32[]{:S(2)}, u32[]{:S(2)}) collective-permute-start(f32[8,1024]{1,0:T(8,128)S(1)} %add_add_fusion), channel_id=1, source_target_pairs={{0,4},{1,5},{2,6},{3,7},{4,0},{5,1},{6,2},{7,3},{8,12},{9,13},{10,... | collective-permute-start | bytes 98312 | tf_op jit(solution)/shard_map/ppermute | solution.py:266
  35.4 0.9 %collective-permute-done.11 = f32[8,1024]{1,0:T(8,128)S(1)} collective-permute-done((f32[8,1024]{1,0:T(8,128)S(1)}, f32[8,1024]{1,0:T(8,128)S(1)}, u32[]{:S(2)}, u32[]{:S(2)}) %collective-permute-start.11) | collective-permute-done | bytes 32800 | tf_op jit(solution)/shard_map/ppermute | solution.py:266
  36.3 1.6 %collective-permute-start.14 = (f32[8,1024]{1,0:T(8,128)S(1)}, f32[8,1024]{1,0:T(8,128)S(1)}, u32[]{:S(2)}, u32[]{:S(2)}) collective-permute-start(f32[8,1024]{1,0:T(8,128)S(1)} %add.15.refs_0_), channel_id=1, source_target_pairs={{0,28},{1,29},{2,30},{3,31},{4,24},{5,25},{6,26},{7,27},{8,20},{9,... | collective-permute-start | bytes 98312 | tf_op jit(solution)/shard_map/ppermute | solution.py:266
  37.9 0.5 %collective-permute-start.13 = (f32[8,1024]{1,0:T(8,128)S(1)}, f32[8,1024]{1,0:T(8,128)S(1)}, u32[]{:S(2)}, u32[]{:S(2)}) collective-permute-start(f32[8,1024]{1,0:T(8,128)S(1)} %add.15.refs_0_), channel_id=1, source_target_pairs={{0,20},{1,21},{2,22},{3,23},{4,16},{5,17},{6,18},{7,19},{8,28},{9,... | collective-permute-start | bytes 98312 | tf_op jit(solution)/shard_map/ppermute | solution.py:266
  38.4 1.1 %collective-permute-start.12 = (f32[8,1024]{1,0:T(8,128)S(1)}, f32[8,1024]{1,0:T(8,128)S(1)}, u32[]{:S(2)}, u32[]{:S(2)}) collective-permute-start(f32[8,1024]{1,0:T(8,128)S(1)} %add.15.refs_0_), channel_id=1, source_target_pairs={{0,12},{1,13},{2,14},{3,15},{4,8},{5,9},{6,10},{7,11},{8,4},{9,5},... | collective-permute-start | bytes 98312 | tf_op jit(solution)/shard_map/ppermute | solution.py:266
  39.5 1.1 %collective-permute-done.14.refs_3_ = f32[8,1024]{1,0:T(8,128)S(1)} collective-permute-done((f32[8,1024]{1,0:T(8,128)S(1)}, f32[8,1024]{1,0:T(8,128)S(1)}, u32[]{:S(2)}, u32[]{:S(2)}) %collective-permute-start.14) | collective-permute-done | bytes 32800 | tf_op jit(solution)/shard_map/ppermute | solution.py:266
  40.6 1.0 %collective-permute-done.13.refs_2_ = f32[8,1024]{1,0:T(8,128)S(1)} collective-permute-done((f32[8,1024]{1,0:T(8,128)S(1)}, f32[8,1024]{1,0:T(8,128)S(1)}, u32[]{:S(2)}, u32[]{:S(2)}) %collective-permute-start.13) | collective-permute-done | bytes 32800 | tf_op jit(solution)/shard_map/ppermute | solution.py:266
  41.6 0.2 collective-permute-done.12.refs_1_
  41.8 0.6 %last_sum.1 = (f32[1,8]{1,0:T(1,128)}, f32[8,1000]{1,0:T(8,128)}) custom-call(f32[8,1024]{1,0:T(8,128)S(1)} %add.15.refs_0_, f32[8,1024]{1,0:T(8,128)S(1)} %collective-permute-done.12.refs_1_, f32[8,1024]{1,0:T(8,128)S(1)} %collective-permute-done.13.refs_2_, f32[8,1024]{1,0:T(8,128)S(1)} %collective-permute-done.14.refs_3_), custom_call_target="tpu_custom_call" | custom-call | tf_op jit(solution)/shard_map/last_sum/pallas_call | solution.py:414
  (5 shorter events, 0.1 us)
Async XLA Ops:
  7.2 1.5 %collective-permute-start = (f32[32,512]{1,0:T(8,128)S(1)}, f32[32,512]{1,0:T(8,128)S(1)}, u32[]{:S(2)}, u32[]{:S(2)}) collective-permute-start(f32[32,512]{1,0:T(8,128)S(1)} %get-tuple-element.15), channel_id=1, source_target_pairs={{0,4},{1,5},{2,6},{3,7},{4,0},{5,1},{6,2},{7,3},{8,12},{9,13},{10,... | collective-permute-start | bytes 196616 | tf_op jit(solution)/shard_map/ppermute | solution.py:266
  8.7 6.1 %collective-permute-start.3 = (f32[32,512]{1,0:T(8,128)S(1)}, f32[32,512]{1,0:T(8,128)S(1)}, u32[]{:S(2)}, u32[]{:S(2)}) collective-permute-start(f32[32,512]{1,0:T(8,128)S(1)} %shard_map.50.refs_0_), channel_id=1, source_target_pairs={{0,24},{1,3},{2,26},{3,1},{4,6},{5,29},{6,4},{7,31},{8,10},{9,17},... | collective-permute-start | bytes 196616 | tf_op jit(solution)/shard_map/ppermute | solution.py:266
  12.6 3.7 %collective-permute-start.2 = (f32[32,512]{1,0:T(8,128)S(1)}, f32[32,512]{1,0:T(8,128)S(1)}, u32[]{:S(2)}, u32[]{:S(2)}) collective-permute-start(f32[32,512]{1,0:T(8,128)S(1)} %shard_map.50.refs_0_), channel_id=1, source_target_pairs={{0,20},{1,6},{2,22},{3,4},{4,3},{5,17},{6,1},{7,19},{8,15},{9,29},... | collective-permute-start | bytes 196616 | tf_op jit(solution)/shard_map/ppermute | solution.py:266
  12.6 3.7 %collective-permute-start.1 = (f32[32,512]{1,0:T(8,128)S(1)}, f32[32,512]{1,0:T(8,128)S(1)}, u32[]{:S(2)}, u32[]{:S(2)}) collective-permute-start(f32[32,512]{1,0:T(8,128)S(1)} %shard_map.50.refs_0_), channel_id=1, source_target_pairs={{0,12},{1,4},{2,14},{3,6},{4,1},{5,9},{6,3},{7,11},{8,13},{9,5},{1... | collective-permute-start | bytes 196616 | tf_op jit(solution)/shard_map/ppermute | solution.py:266
  16.3 5.2 %collective-permute-start.6 = (f32[32,512]{1,0:T(8,128)S(1)}, f32[32,512]{1,0:T(8,128)S(1)}, u32[]{:S(2)}, u32[]{:S(2)}) collective-permute-start(f32[32,512]{1,0:T(8,128)S(1)} %shard_map.51.refs_0_), channel_id=1, source_target_pairs={{0,2},{1,25},{2,0},{3,27},{4,28},{5,7},{6,30},{7,5},{8,16},{9,11},... | collective-permute-start | bytes 196616 | tf_op jit(solution)/shard_map/ppermute | solution.py:266
  18.9 5.6 %collective-permute-start.5 = (f32[32,512]{1,0:T(8,128)S(1)}, f32[32,512]{1,0:T(8,128)S(1)}, u32[]{:S(2)}, u32[]{:S(2)}) collective-permute-start(f32[32,512]{1,0:T(8,128)S(1)} %shard_map.51.refs_0_), channel_id=1, source_target_pairs={{0,7},{1,21},{2,5},{3,23},{4,16},{5,2},{6,18},{7,0},{8,28},{9,14},... | collective-permute-start | bytes 196616 | tf_op jit(solution)/shard_map/ppermute | solution.py:266
  20.3 4.4 %collective-permute-start.4 = (f32[32,512]{1,0:T(8,128)S(1)}, f32[32,512]{1,0:T(8,128)S(1)}, u32[]{:S(2)}, u32[]{:S(2)}) collective-permute-start(f32[32,512]{1,0:T(8,128)S(1)} %shard_map.51.refs_0_), channel_id=1, source_target_pairs={{0,5},{1,13},{2,7},{3,15},{4,8},{5,0},{6,10},{7,2},{8,4},{9,12},{1... | collective-permute-start | bytes 196616 | tf_op jit(solution)/shard_map/ppermute | solution.py:266
  24.8 1.9 %collective-permute-start.7 = (bf16[32,512]{1,0:T(8,128)(2,1)S(1)}, bf16[32,512]{1,0:T(8,128)(2,1)S(1)}, u32[]{:S(2)}, u32[]{:S(2)}) collective-permute-start(bf16[32,512]{1,0:T(8,128)(2,1)S(1)} %shard_map.52.z_ref.mine_ref), channel_id=1, source_target_pairs={{0,4},{1,5},{2,6},{3,7},{4,0},{5,1},{6,2},{7,3},{8,12},{9,13},{10,... | collective-permute-start | bytes 98312 | tf_op jit(solution)/shard_map/ppermute | solution.py:266
  28.6 5.0 %collective-permute-start.8 = (f32[8,1024]{1,0:T(8,128)S(1)}, f32[8,1024]{1,0:T(8,128)S(1)}, u32[]{:S(2)}, u32[]{:S(2)}) collective-permute-start(f32[8,1024]{1,0:T(8,128)S(1)} %get-tuple-element.17), channel_id=1, source_target_pairs={{0,6},{1,7},{2,4},{3,5},{4,2},{5,3},{6,0},{7,1},{8,14},{9,15},{10,... | collective-permute-start | bytes 98312 | tf_op jit(solution)/shard_map/ppermute | solution.py:266
  29.7 5.2 %collective-permute-start.9 = (f32[8,1024]{1,0:T(8,128)S(1)}, f32[8,1024]{1,0:T(8,128)S(1)}, u32[]{:S(2)}, u32[]{:S(2)}) collective-permute-start(f32[8,1024]{1,0:T(8,128)S(1)} %get-tuple-element.18), channel_id=1, source_target_pairs={{0,7},{1,6},{2,5},{3,4},{4,3},{5,2},{6,1},{7,0},{8,15},{9,14},{10,... | collective-permute-start | bytes 98312 | tf_op jit(solution)/shard_map/ppermute | solution.py:266
  30.9 4.0 %collective-permute-start.10 = (f32[8,1024]{1,0:T(8,128)S(1)}, f32[8,1024]{1,0:T(8,128)S(1)}, u32[]{:S(2)}, u32[]{:S(2)}) collective-permute-start(f32[8,1024]{1,0:T(8,128)S(1)} %get-tuple-element.19), channel_id=1, source_target_pairs={{0,5},{1,4},{2,7},{3,6},{4,1},{5,0},{6,3},{7,2},{8,13},{9,12},{10,... | collective-permute-start | bytes 98312 | tf_op jit(solution)/shard_map/ppermute | solution.py:266
  35.0 1.4 %collective-permute-start.11 = (f32[8,1024]{1,0:T(8,128)S(1)}, f32[8,1024]{1,0:T(8,128)S(1)}, u32[]{:S(2)}, u32[]{:S(2)}) collective-permute-start(f32[8,1024]{1,0:T(8,128)S(1)} %add_add_fusion), channel_id=1, source_target_pairs={{0,4},{1,5},{2,6},{3,7},{4,0},{5,1},{6,2},{7,3},{8,12},{9,13},{10,... | collective-permute-start | bytes 98312 | tf_op jit(solution)/shard_map/ppermute | solution.py:266
  36.3 4.2 %collective-permute-start.14 = (f32[8,1024]{1,0:T(8,128)S(1)}, f32[8,1024]{1,0:T(8,128)S(1)}, u32[]{:S(2)}, u32[]{:S(2)}) collective-permute-start(f32[8,1024]{1,0:T(8,128)S(1)} %add.15.refs_0_), channel_id=1, source_target_pairs={{0,28},{1,29},{2,30},{3,31},{4,24},{5,25},{6,26},{7,27},{8,20},{9,... | collective-permute-start | bytes 98312 | tf_op jit(solution)/shard_map/ppermute | solution.py:266
  37.9 3.6 %collective-permute-start.13 = (f32[8,1024]{1,0:T(8,128)S(1)}, f32[8,1024]{1,0:T(8,128)S(1)}, u32[]{:S(2)}, u32[]{:S(2)}) collective-permute-start(f32[8,1024]{1,0:T(8,128)S(1)} %add.15.refs_0_), channel_id=1, source_target_pairs={{0,20},{1,21},{2,22},{3,23},{4,16},{5,17},{6,18},{7,19},{8,28},{9,... | collective-permute-start | bytes 98312 | tf_op jit(solution)/shard_map/ppermute | solution.py:266
  38.4 3.3 %collective-permute-start.12 = (f32[8,1024]{1,0:T(8,128)S(1)}, f32[8,1024]{1,0:T(8,128)S(1)}, u32[]{:S(2)}, u32[]{:S(2)}) collective-permute-start(f32[8,1024]{1,0:T(8,128)S(1)} %add.15.refs_0_), channel_id=1, source_target_pairs={{0,12},{1,13},{2,14},{3,15},{4,8},{5,9},{6,10},{7,11},{8,4},{9,5},... | collective-permute-start | bytes 98312 | tf_op jit(solution)/shard_map/ppermute | solution.py:266

commit v7 on v6

--- a/solution.py
+++ b/solution.py
@@ -159,9 +159,16 @@
     weighted_sums(end_ref, begin, other_ref, hot, coef * first, share * first, width, split3)
 
 
-def own_sums_kernel(width, steps_k, end_ref, rows_ref, mine_ref):
+def own_sums_kernel(width, steps_k, end_ref, rows_ref, mine_ref, high_ref, mid_ref):
     _, start_t, first, share, coef = (rows_ref[r : r + 1, :] for r in range(5))
     hot = start_hot(start_t, steps_k)
+    remaining = horizon - start_t * (horizon / steps_k)
+    for c in range(0, end_ref.shape[0], LANES):
+        y = end_ref[c : c + LANES, :]
+        if c + LANES > width:
+            row = lax.broadcasted_iota(i32, y.shape, 0) + (c - width)
+            y = jnp.where((row >= 0) & (row < VALUE_COPIES), remaining, y)
+        high_ref[c : c + LANES, :], mid_ref[c : c + LANES, :] = split2(y)
     begin = my_side() * mine_ref.shape[1]
     weighted_sums(end_ref, begin, mine_ref, hot, coef * first, share * first, width, split3)
 
@@ -194,7 +201,7 @@
 
 
 def second_kernel(
-    n_tm, buf, mine_ref, other_ref, total_ref, end_ref, rows_ref, *refs
+    n_tm, buf, mine_ref, other_ref, total_ref, high_ref, mid_ref, rows_ref, *refs
 ):
     *out_refs, z_ref, part_ref, rest_ref = refs
     steps_k, width, paths = buf.shape
@@ -223,7 +230,12 @@
     second = first + jnp.sum(weight * drift, axis=0, keepdims=True)
     hot = start_hot(start_t, steps_k)
 
-    weighted_sums(end_ref, 0, part_ref, hot, coef * second, share * second, width, split2)
+    weights = jnp.concatenate(split3(hot.astype(f32) * (coef * second)), axis=0)
+    for c in range(0, part_ref.shape[1], LANES):
+        sums = sum(contract_last(weights, ref[c : c + LANES, :]) for ref in (high_ref, mid_ref))
+        part_ref[:, c : c + LANES] = sum(
+            sums[r : r + steps_k] for r in range(0, 3 * steps_k, steps_k)
+        )
     me = lax.axis_index("tm")
     for away, out_ref in enumerate(out_refs):
         out_ref[...] = part_ref[pl.ds(pl.multiple_of((me ^ away) * group, group), group), :]
@@ -357,11 +369,15 @@
     )(inc, *(in_hbm(table.reshape(1, -1)) for table in (level_table, time_table)))
 
     other = swap(other, (1, 0))
-    mine = pl.pallas_call(
+    mine, high, mid = pl.pallas_call(
         functools.partial(own_sums_kernel, width, steps_k),
-        out_shape=jax.ShapeDtypeStruct((steps_k, half), f32),
+        out_shape=(
+            jax.ShapeDtypeStruct((steps_k, half), f32),
+            jax.ShapeDtypeStruct((full, paths), bf16),
+            jax.ShapeDtypeStruct((full, paths), bf16),
+        ),
         in_specs=[vmem] * 2,
-        out_specs=vmem,
+        out_specs=(vmem,) * 3,
         compiler_params=pltpu.CompilerParams(vmem_limit_bytes=SMALL_LIMIT),
         cost_estimate=pl.CostEstimate(
             flops=6 * steps_k * half * paths, bytes_accessed=0, transcendentals=0
@@ -394,7 +410,7 @@
     parts = pl.pallas_call(
         functools.partial(second_kernel, n_tm),
         out_shape=(jax.ShapeDtypeStruct((group, full), f32),) * n_tm,
-        in_specs=[vmem] * 6,
+        in_specs=[vmem] * 7,
         out_specs=(vmem,) * n_tm,
         scratch_shapes=[
             pltpu.VMEM((2, steps_k, half), f32),
@@ -403,7 +419,7 @@
         ],
         compiler_params=params(),
         name="second_iterate",
-    )(held, own, other, total, end, rows)
+    )(held, own, other, total, high, mid, rows)
 
     order = [away for away in (*range(2, n_tm), 1) if away < n_tm]
     own = pairwise([parts[0]] + [swap(parts[away], (1, away)) for away in order])

time: 42.6 us -> 42.6 us (level)
  transfers between devices with their start and end apart: 15 -> 15, of which waited for: 12 -> 12; matrix products, arithmetic and copies ran while one was open for 0% -> 0% of each run, Pallas kernels for 4% -> 5%
where the time goes in v7:
time: 42.6 us; the launch traced here: 42.3 us
  starting transfers between devices  16.1 us (38%)
  waiting for transfers between devices  14.4 us (34%)
  Pallas kernels  11.2 us (26%)
  between operations  0.69 us (2%)
    ppermute x15, starting transfers between devices, swap(): return lax.ppermute(x, ('path', 'tm'), pairs)  16.1 us
    ppermute x15, waiting for transfers between devices, swap(): return lax.ppermute(x, ('path', 'tm'), pairs)  14.4 us
    pallas_call x1, Pallas kernels, shards(): pl.pallas_call(functools.partial(first_kernel, n_path, n_tm), out_shape=(...  6.6 us
    pallas_call x1, Pallas kernels, shards(): pl.pallas_call(functools.partial(second_kernel, n_tm), out_shape=(jax.Sha...  1.9 us
    pallas_call x1, Pallas kernels, shards(): pl.pallas_call(own_half_kernel, out_shape=jax.ShapeDtypeStruct((steps_k,...  1.48 us
  transfers between devices with their start and end apart: 15, of which 12 were waited for; matrix products, arithmetic and copies ran while one was open for 0% of the time, Pallas kernels for 5%

profile of v7, /device:TPU:0, one launch (start us, length us, event | category | flops | bytes accessed | tf_op | source)
XLA Modules:
  0.0 42.3 jit_solution(8427908331461244296)
XLA Ops:
  0.6 6.6 %first_iterate.1 = (f32[32,512]{1,0:T(8,128)S(1)}, f32[1024,256]{1,0:T(8,128)S(1)}, f32[8,256]{1,0:T(8,128)S(1)}, bf16[32,1000,256]{2,1,0:T(8,128)(2,1)S(1)}) custom-call(bf16[32,1000,256]{2,1,0:T(8,128)(2,1)} %bitcast.4, s32[1,4096]{1,0:T(1,128)} %bitcast.5, s32[1,4096]{1,0:T(1,128)} %bitcast.6), custom_call_target="tpu_custom_call" | custom-call | tf_op jit(solution)/shard_map/first_iterate/pallas_call | solution.py:350
  7.2 0.6 %collective-permute-start = (f32[32,512]{1,0:T(8,128)S(1)}, f32[32,512]{1,0:T(8,128)S(1)}, u32[]{:S(2)}, u32[]{:S(2)}) collective-permute-start(f32[32,512]{1,0:T(8,128)S(1)} %get-tuple-element.19), channel_id=1, source_target_pairs={{0,4},{1,5},{2,6},{3,7},{4,0},{5,1},{6,2},{7,3},{8,12},{9,13},{10,... | collective-permute-start | bytes 196616 | tf_op jit(solution)/shard_map/ppermute | solution.py:278
  7.8 0.5 %own_sums.1 = (f32[32,512]{1,0:T(8,128)S(1)}, bf16[1024,256]{1,0:T(8,128)(2,1)S(1)}, bf16[1024,256]{1,0:T(8,128)(2,1)S(1)}) custom-call(f32[1024,256]{1,0:T(8,128)S(1)} %get-tuple-element.16.end_ref, f32[8,256]{1,0:T(8,128)S(1)} %get-tuple-element.17.rows_ref), custom_call_target="tpu_custom_call" | custom-call | flops 25165824 | tf_op jit(solution)/shard_map/own_sums/pallas_call | solution.py:372
  8.3 0.4 collective-permute-done.refs_1_
  8.7 3.8 %collective-permute-start.3 = (f32[32,512]{1,0:T(8,128)S(1)}, f32[32,512]{1,0:T(8,128)S(1)}, u32[]{:S(2)}, u32[]{:S(2)}) collective-permute-start(f32[32,512]{1,0:T(8,128)S(1)} %shard_map.50.refs_0_), channel_id=1, source_target_pairs={{0,24},{1,3},{2,26},{3,1},{4,6},{5,29},{6,4},{7,31},{8,10},{9,17},... | collective-permute-start | bytes 196616 | tf_op jit(solution)/shard_map/ppermute | solution.py:278
  12.6 0.0 collective-permute-start.2
  12.6 0.4 collective-permute-start.1
  12.9 1.9 %collective-permute-done.3.refs_3_ = f32[32,512]{1,0:T(8,128)S(1)} collective-permute-done((f32[32,512]{1,0:T(8,128)S(1)}, f32[32,512]{1,0:T(8,128)S(1)}, u32[]{:S(2)}, u32[]{:S(2)}) %collective-permute-start.3) | collective-permute-done | bytes 65568 | tf_op jit(solution)/shard_map/ppermute | solution.py:278
  14.8 1.4 %collective-permute-done.2.refs_2_ = f32[32,512]{1,0:T(8,128)S(1)} collective-permute-done((f32[32,512]{1,0:T(8,128)S(1)}, f32[32,512]{1,0:T(8,128)S(1)}, u32[]{:S(2)}, u32[]{:S(2)}) %collective-permute-start.2) | collective-permute-done | bytes 65568 | tf_op jit(solution)/shard_map/ppermute | solution.py:278
  16.3 0.0 collective-permute-done.1.refs_1_
  16.3 2.7 %collective-permute-start.6 = (f32[32,512]{1,0:T(8,128)S(1)}, f32[32,512]{1,0:T(8,128)S(1)}, u32[]{:S(2)}, u32[]{:S(2)}) collective-permute-start(f32[32,512]{1,0:T(8,128)S(1)} %shard_map.51.refs_0_), channel_id=1, source_target_pairs={{0,2},{1,25},{2,0},{3,27},{4,28},{5,7},{6,30},{7,5},{8,16},{9,11},... | collective-permute-start | bytes 196616 | tf_op jit(solution)/shard_map/ppermute | solution.py:278
  18.9 1.4 %collective-permute-start.5 = (f32[32,512]{1,0:T(8,128)S(1)}, f32[32,512]{1,0:T(8,128)S(1)}, u32[]{:S(2)}, u32[]{:S(2)}) collective-permute-start(f32[32,512]{1,0:T(8,128)S(1)} %shard_map.51.refs_0_), channel_id=1, source_target_pairs={{0,7},{1,21},{2,5},{3,23},{4,16},{5,2},{6,18},{7,0},{8,28},{9,14},... | collective-permute-start | bytes 196616 | tf_op jit(solution)/shard_map/ppermute | solution.py:278
  20.3 0.1 collective-permute-start.4
  20.5 1.1 %collective-permute-done.6.refs_3_ = f32[32,512]{1,0:T(8,128)S(1)} collective-permute-done((f32[32,512]{1,0:T(8,128)S(1)}, f32[32,512]{1,0:T(8,128)S(1)}, u32[]{:S(2)}, u32[]{:S(2)}) %collective-permute-start.6) | collective-permute-done | bytes 65568 | tf_op jit(solution)/shard_map/ppermute | solution.py:278
  21.5 3.0 %collective-permute-done.5.refs_2_ = f32[32,512]{1,0:T(8,128)S(1)} collective-permute-done((f32[32,512]{1,0:T(8,128)S(1)}, f32[32,512]{1,0:T(8,128)S(1)}, u32[]{:S(2)}, u32[]{:S(2)}) %collective-permute-start.5) | collective-permute-done | bytes 65568 | tf_op jit(solution)/shard_map/ppermute | solution.py:278
  24.5 0.2 collective-permute-done.4.refs_1_
  24.8 0.4 collective-permute-start.7
  25.1 1.5 %own_half.1.total_ref = f32[32,256]{1,0:T(8,128)S(1)} custom-call(bf16[32,1000,256]{2,1,0:T(8,128)(2,1)S(1)} %get-tuple-element.15.buf, bf16[32,512]{1,0:T(8,128)(2,1)S(1)} %shard_map.52.z_ref.mine_ref), custom_call_target="tpu_custom_call" | custom-call | flops 262144000 | tf_op jit(solution)/shard_map/own_half/pallas_call | solution.py:399
  26.6 0.0 collective-permute-done.7.other_ref
  26.7 1.9 %second_iterate.1 = (f32[8,1024]{1,0:T(8,128)S(1)}, f32[8,1024]{1,0:T(8,128)S(1)}, f32[8,1024]{1,0:T(8,128)S(1)}, f32[8,1024]{1,0:T(8,128)S(1)}) custom-call(bf16[32,1000,256]{2,1,0:T(8,128)(2,1)S(1)} %get-tuple-element.15.buf, bf16[32,512]{1,0:T(8,128)(2,1)S(1)} %shard_map.52.z_ref.mine_ref, bf16[32,512]{1,0:T(8,128)(2,1)S(1)} %collective-permute-done.7.other_ref, ...), custom_call_target="tpu_custom_call" | custom-call | tf_op jit(solution)/shard_map/second_iterate/pallas_call | solution.py:410
  28.6 1.1 %collective-permute-start.8 = (f32[8,1024]{1,0:T(8,128)S(1)}, f32[8,1024]{1,0:T(8,128)S(1)}, u32[]{:S(2)}, u32[]{:S(2)}) collective-permute-start(f32[8,1024]{1,0:T(8,128)S(1)} %get-tuple-element.23), channel_id=1, source_target_pairs={{0,6},{1,7},{2,4},{3,5},{4,2},{5,3},{6,0},{7,1},{8,14},{9,15},{10,... | collective-permute-start | bytes 98312 | tf_op jit(solution)/shard_map/ppermute | solution.py:278
  29.7 1.2 %collective-permute-start.9 = (f32[8,1024]{1,0:T(8,128)S(1)}, f32[8,1024]{1,0:T(8,128)S(1)}, u32[]{:S(2)}, u32[]{:S(2)}) collective-permute-start(f32[8,1024]{1,0:T(8,128)S(1)} %get-tuple-element.24), channel_id=1, source_target_pairs={{0,7},{1,6},{2,5},{3,4},{4,3},{5,2},{6,1},{7,0},{8,15},{9,14},{10,... | collective-permute-start | bytes 98312 | tf_op jit(solution)/shard_map/ppermute | solution.py:278
  30.9 0.7 %collective-permute-start.10 = (f32[8,1024]{1,0:T(8,128)S(1)}, f32[8,1024]{1,0:T(8,128)S(1)}, u32[]{:S(2)}, u32[]{:S(2)}) collective-permute-start(f32[8,1024]{1,0:T(8,128)S(1)} %get-tuple-element.25), channel_id=1, source_target_pairs={{0,5},{1,4},{2,7},{3,6},{4,1},{5,0},{6,3},{7,2},{8,13},{9,12},{10,... | collective-permute-start | bytes 98312 | tf_op jit(solution)/shard_map/ppermute | solution.py:278
  31.6 1.9 %collective-permute-done.8 = f32[8,1024]{1,0:T(8,128)S(1)} collective-permute-done((f32[8,1024]{1,0:T(8,128)S(1)}, f32[8,1024]{1,0:T(8,128)S(1)}, u32[]{:S(2)}, u32[]{:S(2)}) %collective-permute-start.8) | collective-permute-done | bytes 32800 | tf_op jit(solution)/shard_map/ppermute | solution.py:278
  33.5 1.4 %collective-permute-done.9 = f32[8,1024]{1,0:T(8,128)S(1)} collective-permute-done((f32[8,1024]{1,0:T(8,128)S(1)}, f32[8,1024]{1,0:T(8,128)S(1)}, u32[]{:S(2)}, u32[]{:S(2)}) %collective-permute-start.9) | collective-permute-done | bytes 32800 | tf_op jit(solution)/shard_map/ppermute | solution.py:278
  34.9 0.0 collective-permute-done.10
  34.9 0.5 %collective-permute-start.11 = (f32[8,1024]{1,0:T(8,128)S(1)}, f32[8,1024]{1,0:T(8,128)S(1)}, u32[]{:S(2)}, u32[]{:S(2)}) collective-permute-start(f32[8,1024]{1,0:T(8,128)S(1)} %add_add_fusion), channel_id=1, source_target_pairs={{0,4},{1,5},{2,6},{3,7},{4,0},{5,1},{6,2},{7,3},{8,12},{9,13},{10,... | collective-permute-start | bytes 98312 | tf_op jit(solution)/shard_map/ppermute | solution.py:278
  35.4 0.9 %collective-permute-done.11 = f32[8,1024]{1,0:T(8,128)S(1)} collective-permute-done((f32[8,1024]{1,0:T(8,128)S(1)}, f32[8,1024]{1,0:T(8,128)S(1)}, u32[]{:S(2)}, u32[]{:S(2)}) %collective-permute-start.11) | collective-permute-done | bytes 32800 | tf_op jit(solution)/shard_map/ppermute | solution.py:278
  36.3 1.6 %collective-permute-start.14 = (f32[8,1024]{1,0:T(8,128)S(1)}, f32[8,1024]{1,0:T(8,128)S(1)}, u32[]{:S(2)}, u32[]{:S(2)}) collective-permute-start(f32[8,1024]{1,0:T(8,128)S(1)} %add.15.refs_0_), channel_id=1, source_target_pairs={{0,28},{1,29},{2,30},{3,31},{4,24},{5,25},{6,26},{7,27},{8,20},{9,... | collective-permute-start | bytes 98312 | tf_op jit(solution)/shard_map/ppermute | solution.py:278
  37.9 0.5 %collective-permute-start.13 = (f32[8,1024]{1,0:T(8,128)S(1)}, f32[8,1024]{1,0:T(8,128)S(1)}, u32[]{:S(2)}, u32[]{:S(2)}) collective-permute-start(f32[8,1024]{1,0:T(8,128)S(1)} %add.15.refs_0_), channel_id=1, source_target_pairs={{0,20},{1,21},{2,22},{3,23},{4,16},{5,17},{6,18},{7,19},{8,28},{9,... | collective-permute-start | bytes 98312 | tf_op jit(solution)/shard_map/ppermute | solution.py:278
  38.4 1.1 %collective-permute-start.12 = (f32[8,1024]{1,0:T(8,128)S(1)}, f32[8,1024]{1,0:T(8,128)S(1)}, u32[]{:S(2)}, u32[]{:S(2)}) collective-permute-start(f32[8,1024]{1,0:T(8,128)S(1)} %add.15.refs_0_), channel_id=1, source_target_pairs={{0,12},{1,13},{2,14},{3,15},{4,8},{5,9},{6,10},{7,11},{8,4},{9,5},... | collective-permute-start | bytes 98312 | tf_op jit(solution)/shard_map/ppermute | solution.py:278
  39.4 1.1 %collective-permute-done.14.refs_3_ = f32[8,1024]{1,0:T(8,128)S(1)} collective-permute-done((f32[8,1024]{1,0:T(8,128)S(1)}, f32[8,1024]{1,0:T(8,128)S(1)}, u32[]{:S(2)}, u32[]{:S(2)}) %collective-permute-start.14) | collective-permute-done | bytes 32800 | tf_op jit(solution)/shard_map/ppermute | solution.py:278
  40.5 1.0 %collective-permute-done.13.refs_2_ = f32[8,1024]{1,0:T(8,128)S(1)} collective-permute-done((f32[8,1024]{1,0:T(8,128)S(1)}, f32[8,1024]{1,0:T(8,128)S(1)}, u32[]{:S(2)}, u32[]{:S(2)}) %collective-permute-start.13) | collective-permute-done | bytes 32800 | tf_op jit(solution)/shard_map/ppermute | solution.py:278
  41.5 0.2 collective-permute-done.12.refs_1_
  41.7 0.6 %last_sum.1 = (f32[1,8]{1,0:T(1,128)}, f32[8,1000]{1,0:T(8,128)}) custom-call(f32[8,1024]{1,0:T(8,128)S(1)} %add.15.refs_0_, f32[8,1024]{1,0:T(8,128)S(1)} %collective-permute-done.12.refs_1_, f32[8,1024]{1,0:T(8,128)S(1)} %collective-permute-done.13.refs_2_, f32[8,1024]{1,0:T(8,128)S(1)} %collective-permute-done.14.refs_3_), custom_call_target="tpu_custom_call" | custom-call | tf_op jit(solution)/shard_map/last_sum/pallas_call | solution.py:430
  (5 shorter events, 0.1 us)
Async XLA Ops:
  7.2 1.5 %collective-permute-start = (f32[32,512]{1,0:T(8,128)S(1)}, f32[32,512]{1,0:T(8,128)S(1)}, u32[]{:S(2)}, u32[]{:S(2)}) collective-permute-start(f32[32,512]{1,0:T(8,128)S(1)} %get-tuple-element.19), channel_id=1, source_target_pairs={{0,4},{1,5},{2,6},{3,7},{4,0},{5,1},{6,2},{7,3},{8,12},{9,13},{10,... | collective-permute-start | bytes 196616 | tf_op jit(solution)/shard_map/ppermute | solution.py:278
  8.7 6.1 %collective-permute-start.3 = (f32[32,512]{1,0:T(8,128)S(1)}, f32[32,512]{1,0:T(8,128)S(1)}, u32[]{:S(2)}, u32[]{:S(2)}) collective-permute-start(f32[32,512]{1,0:T(8,128)S(1)} %shard_map.50.refs_0_), channel_id=1, source_target_pairs={{0,24},{1,3},{2,26},{3,1},{4,6},{5,29},{6,4},{7,31},{8,10},{9,17},... | collective-permute-start | bytes 196616 | tf_op jit(solution)/shard_map/ppermute | solution.py:278
  12.6 3.7 %collective-permute-start.2 = (f32[32,512]{1,0:T(8,128)S(1)}, f32[32,512]{1,0:T(8,128)S(1)}, u32[]{:S(2)}, u32[]{:S(2)}) collective-permute-start(f32[32,512]{1,0:T(8,128)S(1)} %shard_map.50.refs_0_), channel_id=1, source_target_pairs={{0,20},{1,6},{2,22},{3,4},{4,3},{5,17},{6,1},{7,19},{8,15},{9,29},... | collective-permute-start | bytes 196616 | tf_op jit(solution)/shard_map/ppermute | solution.py:278
  12.6 3.7 %collective-permute-start.1 = (f32[32,512]{1,0:T(8,128)S(1)}, f32[32,512]{1,0:T(8,128)S(1)}, u32[]{:S(2)}, u32[]{:S(2)}) collective-permute-start(f32[32,512]{1,0:T(8,128)S(1)} %shard_map.50.refs_0_), channel_id=1, source_target_pairs={{0,12},{1,4},{2,14},{3,6},{4,1},{5,9},{6,3},{7,11},{8,13},{9,5},{1... | collective-permute-start | bytes 196616 | tf_op jit(solution)/shard_map/ppermute | solution.py:278
  16.3 5.2 %collective-permute-start.6 = (f32[32,512]{1,0:T(8,128)S(1)}, f32[32,512]{1,0:T(8,128)S(1)}, u32[]{:S(2)}, u32[]{:S(2)}) collective-permute-start(f32[32,512]{1,0:T(8,128)S(1)} %shard_map.51.refs_0_), channel_id=1, source_target_pairs={{0,2},{1,25},{2,0},{3,27},{4,28},{5,7},{6,30},{7,5},{8,16},{9,11},... | collective-permute-start | bytes 196616 | tf_op jit(solution)/shard_map/ppermute | solution.py:278
  18.9 5.6 %collective-permute-start.5 = (f32[32,512]{1,0:T(8,128)S(1)}, f32[32,512]{1,0:T(8,128)S(1)}, u32[]{:S(2)}, u32[]{:S(2)}) collective-permute-start(f32[32,512]{1,0:T(8,128)S(1)} %shard_map.51.refs_0_), channel_id=1, source_target_pairs={{0,7},{1,21},{2,5},{3,23},{4,16},{5,2},{6,18},{7,0},{8,28},{9,14},... | collective-permute-start | bytes 196616 | tf_op jit(solution)/shard_map/ppermute | solution.py:278
  20.3 4.4 %collective-permute-start.4 = (f32[32,512]{1,0:T(8,128)S(1)}, f32[32,512]{1,0:T(8,128)S(1)}, u32[]{:S(2)}, u32[]{:S(2)}) collective-permute-start(f32[32,512]{1,0:T(8,128)S(1)} %shard_map.51.refs_0_), channel_id=1, source_target_pairs={{0,5},{1,13},{2,7},{3,15},{4,8},{5,0},{6,10},{7,2},{8,4},{9,12},{1... | collective-permute-start | bytes 196616 | tf_op jit(solution)/shard_map/ppermute | solution.py:278
  24.8 1.9 %collective-permute-start.7 = (bf16[32,512]{1,0:T(8,128)(2,1)S(1)}, bf16[32,512]{1,0:T(8,128)(2,1)S(1)}, u32[]{:S(2)}, u32[]{:S(2)}) collective-permute-start(bf16[32,512]{1,0:T(8,128)(2,1)S(1)} %shard_map.52.z_ref.mine_ref), channel_id=1, source_target_pairs={{0,4},{1,5},{2,6},{3,7},{4,0},{5,1},{6,2},{7,3},{8,12},{9,13},{10,... | collective-permute-start | bytes 98312 | tf_op jit(solution)/shard_map/ppermute | solution.py:278
  28.6 5.0 %collective-permute-start.8 = (f32[8,1024]{1,0:T(8,128)S(1)}, f32[8,1024]{1,0:T(8,128)S(1)}, u32[]{:S(2)}, u32[]{:S(2)}) collective-permute-start(f32[8,1024]{1,0:T(8,128)S(1)} %get-tuple-element.23), channel_id=1, source_target_pairs={{0,6},{1,7},{2,4},{3,5},{4,2},{5,3},{6,0},{7,1},{8,14},{9,15},{10,... | collective-permute-start | bytes 98312 | tf_op jit(solution)/shard_map/ppermute | solution.py:278
  29.7 5.2 %collective-permute-start.9 = (f32[8,1024]{1,0:T(8,128)S(1)}, f32[8,1024]{1,0:T(8,128)S(1)}, u32[]{:S(2)}, u32[]{:S(2)}) collective-permute-start(f32[8,1024]{1,0:T(8,128)S(1)} %get-tuple-element.24), channel_id=1, source_target_pairs={{0,7},{1,6},{2,5},{3,4},{4,3},{5,2},{6,1},{7,0},{8,15},{9,14},{10,... | collective-permute-start | bytes 98312 | tf_op jit(solution)/shard_map/ppermute | solution.py:278
  30.9 4.0 %collective-permute-start.10 = (f32[8,1024]{1,0:T(8,128)S(1)}, f32[8,1024]{1,0:T(8,128)S(1)}, u32[]{:S(2)}, u32[]{:S(2)}) collective-permute-start(f32[8,1024]{1,0:T(8,128)S(1)} %get-tuple-element.25), channel_id=1, source_target_pairs={{0,5},{1,4},{2,7},{3,6},{4,1},{5,0},{6,3},{7,2},{8,13},{9,12},{10,... | collective-permute-start | bytes 98312 | tf_op jit(solution)/shard_map/ppermute | solution.py:278
  34.9 1.3 %collective-permute-start.11 = (f32[8,1024]{1,0:T(8,128)S(1)}, f32[8,1024]{1,0:T(8,128)S(1)}, u32[]{:S(2)}, u32[]{:S(2)}) collective-permute-start(f32[8,1024]{1,0:T(8,128)S(1)} %add_add_fusion), channel_id=1, source_target_pairs={{0,4},{1,5},{2,6},{3,7},{4,0},{5,1},{6,2},{7,3},{8,12},{9,13},{10,... | collective-permute-start | bytes 98312 | tf_op jit(solution)/shard_map/ppermute | solution.py:278
  36.3 4.2 %collective-permute-start.14 = (f32[8,1024]{1,0:T(8,128)S(1)}, f32[8,1024]{1,0:T(8,128)S(1)}, u32[]{:S(2)}, u32[]{:S(2)}) collective-permute-start(f32[8,1024]{1,0:T(8,128)S(1)} %add.15.refs_0_), channel_id=1, source_target_pairs={{0,28},{1,29},{2,30},{3,31},{4,24},{5,25},{6,26},{7,27},{8,20},{9,... | collective-permute-start | bytes 98312 | tf_op jit(solution)/shard_map/ppermute | solution.py:278
  37.9 3.6 %collective-permute-start.13 = (f32[8,1024]{1,0:T(8,128)S(1)}, f32[8,1024]{1,0:T(8,128)S(1)}, u32[]{:S(2)}, u32[]{:S(2)}) collective-permute-start(f32[8,1024]{1,0:T(8,128)S(1)} %add.15.refs_0_), channel_id=1, source_target_pairs={{0,20},{1,21},{2,22},{3,23},{4,16},{5,17},{6,18},{7,19},{8,28},{9,... | collective-permute-start | bytes 98312 | tf_op jit(solution)/shard_map/ppermute | solution.py:278
  38.4 3.3 %collective-permute-start.12 = (f32[8,1024]{1,0:T(8,128)S(1)}, f32[8,1024]{1,0:T(8,128)S(1)}, u32[]{:S(2)}, u32[]{:S(2)}) collective-permute-start(f32[8,1024]{1,0:T(8,128)S(1)} %add.15.refs_0_), channel_id=1, source_target_pairs={{0,12},{1,13},{2,14},{3,15},{4,8},{5,9},{6,10},{7,11},{8,4},{9,5},... | collective-permute-start | bytes 98312 | tf_op jit(solution)/shard_map/ppermute | solution.py:278
